TPU v7x, 512 devices: a whole 4x4x16 slice. The times are simulated.
512 devices in a mesh: row: 16 (over z), col: 32 (over x, y, core).
Axes of the slice: x: 4, y: 4, z: 16, core: 2. Of those that a mesh axis runs over, the one named last changes fastest.
Arguments:
- points: float32 [8, 32768], P(None, ('row', 'col')), may hold values from -15 to 15
- noise_level: float32 [32768], P('row'), may hold values from 0.5 to 2
- right_sides: float32 [64, 32768], P(None, 'row'), may hold values from -6 to 6
Outputs:
- solution: float32 [64, 32768], P(None, 'row')
- residual: float32 [64, 32768], P(None, 'row')
- rel_norms: float32 [64], replicated
All inputs are finite; a program needn't handle non-finite values.
Results may differ from a plain program's by a relative error of at most 0.0008.
Values sent between devices are 32-bit elements; how exact they have to be, the bound alone decides.
No kernel may reach another device: no remote copies, remote signals or barrier semaphores. Data moves between devices by JAX's collectives and lax.ppermute only.
A program may use at most 64 MiB of HBM per device.

v0:
```python
import math

import jax
import jax.numpy as jnp
from jax import lax
from jax.sharding import Mesh
from jax.sharding import PartitionSpec as P

ITERS = 2
COL = ("col_0", "col_1", "col_2")
ROW_COL = ("row", "col_0", "col_1", "col_2")


HIGH = lax.Precision.HIGHEST


def sent_to_all(value, axis):
    devices = lax.axis_size(axis)
    return lax.all_to_all(
        jnp.broadcast_to(value[None], (devices, *value.shape)), axis, 0, 0, tiled=True
    )


def taken_together(value, axis):
    return sent_to_all(value, axis).sum(axis=0)


def in_order(parts, dim):
    parts = jnp.moveaxis(parts, 0, dim)
    dims = parts.shape
    return parts.reshape(*dims[:dim], dims[dim] * dims[dim + 1], *dims[dim + 2 :])


def gathered_by_axis(value, axes, dim):
    far, near = axes
    leading = sent_to_all(value, far)
    parts = jnp.swapaxes(sent_to_all(leading, near), 0, 1)
    return in_order(parts.reshape(-1, *value.shape), dim)


def picked(value, axis, root):
    return lax.dynamic_index_in_dim(lax.all_gather(value, axis), root, 0, keepdims=False)


def cut_along(value, dim, devices):
    dims = value.shape
    parts = value.reshape(*dims[:dim], devices, dims[dim] // devices, *dims[dim + 1 :])
    return jnp.moveaxis(parts, dim, 0)


def sent_and_summed(value, axis, dim):
    devices = lax.axis_size(axis)
    parts = lax.all_to_all(cut_along(value, dim, devices), axis, 0, 0, tiled=True)
    return jnp.sum(parts, axis=0)


def padded_to(lines, devices):
    spare = -len(lines) % devices
    return jnp.pad(lines, [(0, spare)] + [(0, 0)] * (lines.ndim - 1))


def gather_directly(value, axis, dim):
    parts = sent_to_all(value, axis)
    return in_order(parts, dim)


def nested_sum(value, axes):
    lines = value.reshape(-1, value.shape[-1])
    own = sent_and_summed(padded_to(lines, lax.axis_size(axes)), axes, 0)
    whole = gather_directly(own, axes, 0)
    return whole[: len(lines)].reshape(value.shape)


def products(first, second):
    return lax.dot_general(first, second, (((1,), (1,)), ((), ())), precision=HIGH)


def solve_sym(matrix, target):
    lower = jnp.linalg.cholesky(0.5 * (matrix + matrix.T))
    return jax.scipy.linalg.cho_solve((lower, True), target)


def gram_sum(single):
    return taken_together(single, "row")


def on_device(points, noise_level, right_sides):
    row_count = lax.axis_size("row")
    col_count = lax.axis_size(COL)
    row_index = lax.axis_index("row")
    col_index = lax.axis_index(COL)
    pts_dev = points.shape[1]
    row_len = pts_dev * col_count
    col_len = pts_dev * row_count
    col_ratio = col_count // row_count
    all_points = gathered_by_axis(points, (("row", "col_0"), ("col_1", "col_2")), 1)
    sq_norms = jnp.sum(all_points * all_points, axis=0)
    row_points = lax.dynamic_slice_in_dim(all_points, row_index * row_len, row_len, 1)
    row_sq = lax.dynamic_slice_in_dim(sq_norms, row_index * row_len, row_len, 0)
    col_points = lax.dynamic_slice_in_dim(all_points, col_index * col_len, col_len, 1)
    col_sq = lax.dynamic_slice_in_dim(sq_norms, col_index * col_len, col_len, 0)
    tile_rows = math.gcd(row_len, 512)
    tile_count = row_len // tile_rows
    rhs_count = right_sides.shape[0]
    residual = right_sides
    solution = jnp.zeros_like(residual)
    direction = residual
    gram = gram_sum(products(residual, residual))
    first = gram
    new_gram = gram
    for iteration in range(ITERS):
        source = lax.dynamic_slice_in_dim(direction, col_index % col_ratio * col_len, col_len, 1)
        col_direction = picked(source, "row", col_index // col_ratio)

        def one_tile(index, result):
            offset = index * tile_rows
            tile_points = lax.dynamic_slice_in_dim(row_points, offset, tile_rows, 1)
            tile_sq = lax.dynamic_slice_in_dim(row_sq, offset, tile_rows, 0)
            sq_dist = (
                tile_sq[:, None]
                + col_sq[None, :]
                - 2.0 * jnp.dot(tile_points.T, col_points, precision=HIGH)
            )
            kernel = jnp.exp(-0.5 * sq_dist)
            return lax.dynamic_update_slice_in_dim(
                result, products(col_direction, kernel), offset, 1
            )

        image = (
            nested_sum(
                lax.fori_loop(
                    0, tile_count, one_tile, jnp.zeros((rhs_count, row_len), jnp.float32)
                ),
                COL,
            )
            + noise_level[None, :] * direction
        )
        curv = gram_sum(products(direction, image))
        step_coef = solve_sym(curv, gram)
        solution = solution + jnp.dot(step_coef.T, direction, precision=HIGH)
        residual = residual - jnp.dot(step_coef.T, image, precision=HIGH)
        new_gram = gram_sum(products(residual, residual))
        if iteration + 1 < ITERS:
            dir_coef = solve_sym(gram, new_gram)
            direction = residual + jnp.dot(dir_coef.T, direction, precision=HIGH)
        gram = new_gram
    rel_norms = jnp.sqrt(jnp.diagonal(new_gram) / jnp.diagonal(first))
    return (solution, residual, rel_norms)


def solution(mesh):
    torus = Mesh(
        mesh.devices.reshape(mesh.shape["row"], 4, 4, 2), ("row", "col_0", "col_1", "col_2")
    )
    return jax.shard_map(
        on_device,
        mesh=torus,
        in_specs=(P(None, ROW_COL), P("row"), P(None, "row")),
        out_specs=(P(None, "row"), P(None, "row"), P()),
        check_vma=False,
    )
```

profile of v0, /device:TPU:1, one launch (start us, length us, event | category | flops | bytes accessed | tf_op | source)
XLA Modules:
  0.0 441.4 jit_solution(1342012569931358783)
XLA Ops:
  7.2 1.7 constant_dynamic-slice_fusion.1
  9.8 34.0 %all_to_all.55 = f32[64,1,512]{2,1,0:T(1,128)S(1)} all-to-all(f32[64,1,512]{2,1,0:T(1,128)S(1)} %reshape.71), channel_id=1, replica_groups=mesh['row'=16,'col_0'=4,'col_1'=4,'col_2'=2] {'row','col_0'}, dimensions={0} | all-to-all | bytes 262144 | tf_op jit(solution)/shard_map/all_to_all | solution.py:19
  45.7 2.2 reshape.73
  47.8 9.0 %all-to-all-start.1 = ((f32[8,1,32768]{2,1,0:T(1,128)}), f32[8,1,32768]{2,1,0:T(1,128)S(1)}, u32[]{:S(2)}, u32[]{:S(2)}) async-start(f32[8,1,32768]{2,1,0:T(1,128)} %reshape.73), calls=%async_computation.1 | async-start | bytes 2097152 | tf_op jit(solution)/shard_map/all_to_all | solution.py:19
  56.8 14.9 %all-to-all-done.1 = f32[8,1,32768]{2,1,0:T(1,128)S(1)} async-done(((f32[8,1,32768]{2,1,0:T(1,128)}), f32[8,1,32768]{2,1,0:T(1,128)S(1)}, u32[]{:S(2)}, u32[]{:S(2)}) %all-to-all-start.1) | async-done | bytes 1048608 | tf_op jit(solution)/shard_map/all_to_all | solution.py:19
  71.7 3.3 reduce.7
  77.3 1.7 copy.40
  79.0 2.2 reshape.50
  82.1 4.3 all-gather.5.cloned.1.call-done
  87.4 18.4 %while.26 = (s32[]{:T(128)}, f32[64,2048]{1,0:T(8,128)S(1)}, f32[2048]{0:T(1024)S(1)}, f32[1024]{0:T(1024)S(1)}, f32[8,2048]{1,0:T(8,128)S(1)}, /*index=5*/f32[8...) while((s32[]{:T(128)}, f32[64,2048]{1,0:T(8,128)S(1)}, ...), condition=%wide.region_2.3_spmd, body=%wide.region_1.0_spmd.sunk | while | flops 455081984 | bytes 4647079 | solution.py:131
  87.4 1.8 fusion.114
  89.3 2.6 fusion.115
  92.0 1.8 fusion.114
  93.9 2.6 fusion.115
  96.6 1.8 fusion.114
  98.5 2.6 fusion.115
  101.2 1.8 fusion.114
  103.1 2.6 fusion.115
  106.1 28.0 %all_to_all.57 = f32[32,2,2048]{2,1,0:T(2,128)S(1)} all-to-all(f32[32,2,2048]{2,1,0:T(2,128)S(1)} %reshape.51), channel_id=1, replica_groups=mesh['row'=16,'col_0'=4,'col_1'=4,'col_2'=2] {'col_0','col_1','col_2'}, dimensions={0} | all-to-all | bytes 1048576 | tf_op jit(solution)/shard_map/all_to_all | solution.py:53
  135.3 3.9 all-to-all-start.3
  140.9 9.8 %all-to-all-done.3 = f32[32,2,2048]{2,1,0:T(2,128)S(1)} async-done(((f32[32,2,2048]{2,1,0:T(2,128)}), f32[32,2,2048]{2,1,0:T(2,128)S(1)}, u32[]{:S(2)}, u32[]{:S(2)}) %all-to-all-start.3) | async-done | bytes 524320 | tf_op jit(solution)/shard_map/all_to_all | solution.py:19
  150.7 6.5 %all-to-all-start.5 = ((f32[16,1,4096]{2,1,0:T(1,128)}), f32[16,1,4096]{2,1,0:T(1,128)S(1)}, u32[]{:S(2)}, u32[]{:S(2)}) async-start(f32[16,1,4096]{2,1,0:T(1,128)} %reshape.69), calls=%async_computation.5 | async-start | bytes 524288 | tf_op jit(solution)/shard_map/all_to_all | solution.py:19
  159.3 13.1 %all-to-all-done.5 = f32[16,1,4096]{2,1,0:T(1,128)S(1)} async-done(((f32[16,1,4096]{2,1,0:T(1,128)}), f32[16,1,4096]{2,1,0:T(1,128)S(1)}, u32[]{:S(2)}, u32[]{:S(2)}) %all-to-all-start.5) | async-done | bytes 262176 | tf_op jit(solution)/shard_map/all_to_all | solution.py:19
  172.4 9.1 %all-to-all-start.4 = ((f32[16,1,4096]{2,1,0:T(1,128)}), f32[16,1,4096]{2,1,0:T(1,128)S(1)}, u32[]{:S(2)}, u32[]{:S(2)}) async-start(f32[16,1,4096]{2,1,0:T(1,128)} %reshape.75), calls=%async_computation.4 | async-start | bytes 524288 | tf_op jit(solution)/shard_map/all_to_all | solution.py:19
  183.1 12.3 %all-to-all-done.4 = f32[16,1,4096]{2,1,0:T(1,128)S(1)} async-done(((f32[16,1,4096]{2,1,0:T(1,128)}), f32[16,1,4096]{2,1,0:T(1,128)S(1)}, u32[]{:S(2)}, u32[]{:S(2)}) %all-to-all-start.4) | async-done | bytes 262176 | tf_op jit(solution)/shard_map/all_to_all | solution.py:19
  197.2 5.8 %cholesky.59 = f32[64,64]{1,0:T(8,128)S(1)} custom-call(f32[64,64]{1,0:T(8,128)S(1)} %fusion.66), custom_call_target="Cholesky" | custom-call | tf_op jit(solution)/shard_map/jit(cholesky)/cholesky | solution.py:79
  204.3 4.9 %custom-call.13 = f32[1,64,64]{1,2,0:T(8,128)S(1)} custom-call(f32[1,64,64]{2,1,0:T(8,128)S(1)} %fusion.47), custom_call_target="InvertDiagBlocksLowerTriangular" | custom-call | tf_op jit(solution)/shard_map/jit(_cho_solve)/triangular_solve | solution.py:80
  212.0 10.3 %all-to-all-start.6 = ((f32[16,1,4096]{2,1,0:T(1,128)}), f32[16,1,4096]{2,1,0:T(1,128)S(1)}, u32[]{:S(2)}, u32[]{:S(2)}) async-start(f32[16,1,4096]{2,1,0:T(1,128)} %reshape.77), calls=%async_computation.6 | async-start | bytes 524288 | tf_op jit(solution)/shard_map/all_to_all | solution.py:19
  222.7 5.8 %cholesky.70 = f32[64,64]{1,0:T(8,128)S(1)} custom-call(f32[64,64]{1,0:T(8,128)S(1)} %fusion.60), custom_call_target="Cholesky" | custom-call | tf_op jit(solution)/shard_map/jit(cholesky)/cholesky | solution.py:79
  229.9 4.9 %custom-call.14 = f32[1,64,64]{1,2,0:T(8,128)S(1)} custom-call(f32[1,64,64]{2,1,0:T(8,128)S(1)} %fusion.48), custom_call_target="InvertDiagBlocksLowerTriangular" | custom-call | tf_op jit(solution)/shard_map/jit(_cho_solve)/triangular_solve | solution.py:80
  239.4 66.0 %all-gather.7.cloned.1.call-done = f32[1024,1024]{1,0:T(8,128)} async-done(((f32[64,1024]{1,0:T(8,128)}), f32[1024,1024]{1,0:T(8,128)}) %all-gather.7.cloned.1.call-update) | async-done | bytes 4194320 | tf_op jit(solution)/shard_map/all_gather | solution.py:42
  306.4 18.3 %while.27 = (s32[]{:T(128)}, f32[64,2048]{1,0:T(8,128)S(1)}, f32[2048]{0:T(1024)S(1)}, f32[1024]{0:T(1024)S(1)}, f32[8,2048]{1,0:T(8,128)S(1)}, /*index=5*/f32[8...) while((s32[]{:T(128)}, f32[64,2048]{1,0:T(8,128)S(1)}, ...), condition=%wide.region_10.13_spmd, body=%wide.region_9.12_spmd.sunk | while | flops 455081984 | bytes 4647079 | solution.py:131
  306.4 1.8 fusion.120
  308.3 2.6 fusion.121
  311.0 1.8 fusion.120
  312.9 2.6 fusion.121
  315.6 1.8 fusion.120
  317.5 2.6 fusion.121
  320.1 1.8 fusion.120
  322.1 2.6 fusion.121
  325.0 27.7 %all_to_all.58 = f32[32,2,2048]{2,1,0:T(2,128)S(1)} all-to-all(f32[32,2,2048]{2,1,0:T(2,128)S(1)} %reshape.53), channel_id=1, replica_groups=mesh['row'=16,'col_0'=4,'col_1'=4,'col_2'=2] {'col_0','col_1','col_2'}, dimensions={0} | all-to-all | bytes 1048576 | tf_op jit(solution)/shard_map/all_to_all | solution.py:53
  353.1 15.0 %all_to_all.56 = f32[32,2,2048]{2,1,0:T(2,128)S(1)} all-to-all(f32[32,2,2048]{2,1,0:T(2,128)S(1)} %broadcast_in_dim.41), channel_id=1, replica_groups=mesh['row'=16,'col_0'=4,'col_1'=4,'col_2'=2] {'col_0','col_1','col_2'}, dimensions={0} | all-to-all | bytes 1048576 | tf_op jit(solution)/shard_map/all_to_all | solution.py:19
  369.4 22.4 %all_to_all.59 = f32[16,1,4096]{2,1,0:T(1,128)S(1)} all-to-all(f32[16,1,4096]{2,1,0:T(1,128)S(1)} %reshape.79), channel_id=1, replica_groups=mesh['row'=16,'col_0'=4,'col_1'=4,'col_2'=2] {'row'}, dimensions={0} | all-to-all | bytes 524288 | tf_op jit(solution)/shard_map/all_to_all | solution.py:19
  393.6 5.8 %cholesky.81 = f32[64,64]{1,0:T(8,128)S(1)} custom-call(f32[64,64]{1,0:T(8,128)S(1)} %fusion.54), custom_call_target="Cholesky" | custom-call | tf_op jit(solution)/shard_map/jit(cholesky)/cholesky | solution.py:79
  400.8 4.9 %custom-call.15 = f32[1,64,64]{1,2,0:T(8,128)S(1)} custom-call(f32[1,64,64]{2,1,0:T(8,128)S(1)} %fusion.49), custom_call_target="InvertDiagBlocksLowerTriangular" | custom-call | tf_op jit(solution)/shard_map/jit(_cho_solve)/triangular_solve | solution.py:80
  408.4 9.1 %all-to-all-start.10 = ((f32[16,1,4096]{2,1,0:T(1,128)}), f32[16,1,4096]{2,1,0:T(1,128)S(1)}, u32[]{:S(2)}, u32[]{:S(2)}) async-start(f32[16,1,4096]{2,1,0:T(1,128)} %reshape.81), calls=%async_computation.10 | async-start | bytes 524288 | tf_op jit(solution)/shard_map/all_to_all | solution.py:19
  419.0 1.4 convolution_add_fusion
  420.4 11.0 %all-to-all-done.10 = f32[16,1,4096]{2,1,0:T(1,128)S(1)} async-done(((f32[16,1,4096]{2,1,0:T(1,128)}), f32[16,1,4096]{2,1,0:T(1,128)S(1)}, u32[]{:S(2)}, u32[]{:S(2)}) %all-to-all-start.10) | async-done | bytes 262176 | tf_op jit(solution)/shard_map/all_to_all | solution.py:19
  (114 shorter events, 39.3 us)
Async XLA Ops:
  7.2 79.2 %all-gather.5.cloned.1.call-start = ((), (), s32[]{:S(2)}) async-start(), calls=%async_computation.11 | async-start | bytes 4456448 | tf_op jit(solution)/shard_map/all_gather | solution.py:42
  47.8 23.9 %all-to-all-start.1 = ((f32[8,1,32768]{2,1,0:T(1,128)}), f32[8,1,32768]{2,1,0:T(1,128)S(1)}, u32[]{:S(2)}, u32[]{:S(2)}) async-start(f32[8,1,32768]{2,1,0:T(1,128)} %reshape.73), calls=%async_computation.1 | async-start | bytes 2097152 | tf_op jit(solution)/shard_map/all_to_all | solution.py:19
  105.7 33.4 %copy-start = (f32[64,2048]{1,0:T(8,128)S(1)}, f32[64,2048]{1,0:T(8,128)}, u32[]{:S(2)}) copy-start(f32[64,2048]{1,0:T(8,128)} %param.12) | copy-start | bytes 1572868
  135.3 15.4 %all-to-all-start.3 = ((f32[32,2,2048]{2,1,0:T(2,128)}), f32[32,2,2048]{2,1,0:T(2,128)S(1)}, u32[]{:S(2)}, u32[]{:S(2)}) async-start(f32[32,2,2048]{2,1,0:T(2,128)} %broadcast_in_dim.37), calls=%async_computation.3 | async-start | bytes 1048576 | tf_op jit(solution)/shard_map/all_to_all | solution.py:19
  139.2 18.3 %copy-start.2 = (f32[2048]{0:T(1024)S(1)}, f32[2048]{0:T(1024)}, u32[]{:S(2)}) copy-start(f32[2048]{0:T(1024)} %param.11) | copy-start | bytes 24580
  150.7 21.7 %all-to-all-start.5 = ((f32[16,1,4096]{2,1,0:T(1,128)}), f32[16,1,4096]{2,1,0:T(1,128)S(1)}, u32[]{:S(2)}, u32[]{:S(2)}) async-start(f32[16,1,4096]{2,1,0:T(1,128)} %reshape.69), calls=%async_computation.5 | async-start | bytes 524288 | tf_op jit(solution)/shard_map/all_to_all | solution.py:19
  172.4 23.0 %all-to-all-start.4 = ((f32[16,1,4096]{2,1,0:T(1,128)}), f32[16,1,4096]{2,1,0:T(1,128)S(1)}, u32[]{:S(2)}, u32[]{:S(2)}) async-start(f32[16,1,4096]{2,1,0:T(1,128)} %reshape.75), calls=%async_computation.4 | async-start | bytes 524288 | tf_op jit(solution)/shard_map/all_to_all | solution.py:19
  212.0 24.1 %all-to-all-start.6 = ((f32[16,1,4096]{2,1,0:T(1,128)}), f32[16,1,4096]{2,1,0:T(1,128)S(1)}, u32[]{:S(2)}, u32[]{:S(2)}) async-start(f32[16,1,4096]{2,1,0:T(1,128)} %reshape.77), calls=%async_computation.6 | async-start | bytes 524288 | tf_op jit(solution)/shard_map/all_to_all | solution.py:19
  222.3 83.1 %all-gather.7.cloned.1.call-start = ((), (), s32[]{:S(2)}) async-start(), calls=%async_computation.12 | async-start | bytes 4456448 | tf_op jit(solution)/shard_map/all_gather | solution.py:42
  406.8 12.2 %copy-start.1 = (f32[64,2048]{1,0:T(8,128)}, f32[64,2048]{1,0:T(8,128)S(1)}, u32[]{:S(2)}) copy-start(f32[64,2048]{1,0:T(8,128)S(1)} %convolution_subtract_fusion) | copy-start | bytes 1572868
  408.4 23.0 %all-to-all-start.10 = ((f32[16,1,4096]{2,1,0:T(1,128)}), f32[16,1,4096]{2,1,0:T(1,128)S(1)}, u32[]{:S(2)}, u32[]{:S(2)}) async-start(f32[16,1,4096]{2,1,0:T(1,128)} %reshape.81), calls=%async_computation.10 | async-start | bytes 524288 | tf_op jit(solution)/shard_map/all_to_all | solution.py:19
Sparse Core Ops, SparseCore 0:
  10.6 75.6 all-gather.4
  239.5 65.7 all-gather.6
where the time goes:
time: 449 us; the launch traced here: 441 us
  waiting for transfers between devices  133 us (30%)
  blocking collectives  127 us (28%)
  other arithmetic  48.5 us (11%)
  starting transfers between devices  48.2 us (11%)
  matrix products  43.9 us (10%)
  local copies, waits for them, and re-layouts  25.9 us (6%)
  between operations  15 us (3%)
    all_to_all x3, blocking collectives, sent_to_all(): lax.all_to_all(jnp.broadcast_to(value[None], (devices, *value.shape)), ax...  71.4 us
    all_gather x2, waiting for transfers between devices, picked(): lax.all_gather(value, axis)  70.2 us
    all_to_all x6, waiting for transfers between devices, sent_to_all(): lax.all_to_all(jnp.broadcast_to(value[None], (devices, *value.shape)), ax...  62.3 us
    all_to_all x2, blocking collectives, sent_and_summed(): lax.all_to_all(cut_along(value, dim, devices), axis, 0, 0, tiled=True)  55.7 us
    all_to_all x6, starting transfers between devices, sent_to_all(): lax.all_to_all(jnp.broadcast_to(value[None], (devices, *value.shape)), ax...  47.9 us
    dot_general x13, matrix products, products(): lax.dot_general(first, second, (((1,), (1,)), ((), ())), precision=HIGH)  24 us
    another operation x9, other arithmetic, solve_sym(): lower = jnp.linalg.cholesky(0.5 * (matrix + matrix.T))  19.6 us
    another operation x6, other arithmetic, solve_sym(): return jax.scipy.linalg.cho_solve((lower, True), target)  16.6 us
  transfers between devices with their start and end apart: 8, of which 8 were waited for; matrix products, arithmetic and copies ran while one was open for 8% of the time, Pallas kernels for 0%

commit v1 on v0

v1 whole, which is shorter than its diff:
```python
import functools

import jax
import jax.numpy as jnp
from jax import lax
from jax.experimental import pallas as pl
from jax.experimental.pallas import tpu as pltpu
from jax.sharding import Mesh
from jax.sharding import PartitionSpec as P

COL = ("col_0", "col_1", "col_2")
ROW_COL = ("row", "col_0", "col_1", "col_2")
HIGH = lax.Precision.HIGHEST
F32 = jnp.float32
BF16 = jnp.bfloat16
THETA = 0.5
LANES = 128
HALF = 64
VMEM = pl.BlockSpec(memory_space=pltpu.VMEM)


def lane_of(shape):
    return lax.broadcasted_iota(jnp.int32, shape, len(shape) - 1)


def packed(turned):
    return jnp.concatenate([turned[:32], turned[32:64]], axis=1)


def own_kernel(col_ref, rhs_ref, pts_ref, row_out, col_out):
    turned = rhs_ref[...].T
    odd = lax.rem(col_ref[0], 2) == 1
    block = packed(jnp.where(odd, turned[HALF:], turned[:HALF]))
    pts = jnp.concatenate([pts_ref[...], pts_ref[...]], axis=1)
    unit = jnp.concatenate([block, pts], axis=0)
    for place in range(row_out.shape[0]):
        row_out[place] = unit
    for place in range(col_out.shape[0]):
        col_out[place] = pts


def own_units(col_index, right_sides, points, rows, cols):
    return pl.pallas_call(
        own_kernel,
        grid_spec=pltpu.PrefetchScalarGridSpec(
            num_scalar_prefetch=1,
            grid=(1,),
            in_specs=[
                pl.BlockSpec((HALF, LANES), lambda i, c: (0, c[0] // 2)),
                pl.BlockSpec((8, HALF), lambda i, c: (0, 0)),
            ],
            out_specs=[
                pl.BlockSpec((rows, 40, LANES), lambda i, c: (0, 0, 0)),
                pl.BlockSpec((cols, 8, LANES), lambda i, c: (0, 0, 0)),
            ],
        ),
        out_shape=[
            jax.ShapeDtypeStruct((rows, 40, LANES), F32),
            jax.ShapeDtypeStruct((cols, 8, LANES), F32),
        ],
        name="own_units",
    )(col_index, right_sides, points)


def block_dot(first, second):
    both = lax.dot_general(
        first, second, (((0,), (0,)), ((), ())), precision=HIGH, preferred_element_type=F32
    )
    return both[:HALF, :HALF] + both[HALF:, HALF:]


def packed_kernel(rhs_ref, noise_ref, packed_out, noise_out):
    low = lane_of((32, LANES)) < HALF
    for tile in range(rhs_ref.shape[1] // LANES):
        turned = rhs_ref[:, tile * LANES : (tile + 1) * LANES].T
        noise = noise_ref[:, tile * LANES : (tile + 1) * LANES]
        noise = jnp.broadcast_to(noise, (LANES, LANES)).T
        for part in range(2):
            rows = slice(tile * 64 + part * 32, tile * 64 + part * 32 + 32)
            packed_out[rows] = packed(turned[part * 64 : part * 64 + 64])
            noise_out[rows] = jnp.where(
                low, noise[part * 64 : part * 64 + 32], noise[part * 64 + 32 : part * 64 + 64]
            )


def packed_rows(right_sides, noise_level):
    rows = right_sides.shape[1] // 2
    return pl.pallas_call(
        packed_kernel,
        in_specs=[VMEM] * 2,
        out_specs=[VMEM] * 2,
        out_shape=[jax.ShapeDtypeStruct((rows, LANES), F32)] * 2,
        cost_estimate=pl.CostEstimate(
            flops=4 * 10**9, bytes_accessed=3 * 4 * rows * LANES, transcendentals=0
        ),
        name="packed_rows",
    )(right_sides, noise_level[None, :])


def ordered(units):
    place = lane_of((8, LANES)) // 32
    pieces = []
    for h in range(2):
        for start in range(0, len(units), 4):
            piece = None
            for q in range(4):
                unit = units[start + q]
                if (q - h) % 2:
                    unit = pltpu.roll(unit, 32, 1)
                piece = unit if piece is None else jnp.where(place == q, unit, piece)
            pieces.append(piece)
    return jnp.concatenate(pieces, axis=1)


def rounded(value):
    return value.astype(BF16).astype(F32)


def three_parts(value):
    first = rounded(value)
    rest = value - first
    second = rounded(rest)
    return first, second, rest - second


def augmented(pts, as_rows):
    x1, x2, x3 = three_parts(pts)
    half_sq = -0.5 * jnp.sum(pts * pts, axis=0, keepdims=True)
    s1, s2, s3 = three_parts(half_sq)
    sub = lax.broadcasted_iota(jnp.int32, pts.shape, 0)
    squares = jnp.where(sub == 0, s1, jnp.where(sub == 1, s2, jnp.where(sub == 2, s3, 0.0)))
    ones = jnp.where(sub < 3, 1.0, 0.0)
    zeros = jnp.zeros_like(pts)
    if as_rows:
        blocks = [x1, x1, x2, x2, x1, x3, x2, x3, squares, ones]
    else:
        blocks = [x1, x2, x1, x2, x3, x1, x3, x2, ones, squares]
    return jnp.concatenate(blocks + [zeros] * 6, axis=0)


def apply_kernel_matrix(out_pts, in_pts, values, result, left, right, stack):
    outs = left.shape[0]
    ins = right.shape[1]
    tile = min(256, outs // 2)
    for start in range(0, outs, LANES):
        piece = augmented(out_pts[:, start : start + LANES], True)
        left[start : start + LANES] = piece.T.astype(BF16)
    for start in range(0, ins, 256):
        right[:, start : start + 256] = augmented(in_pts[:, start : start + 256], False).astype(BF16)
    groups = ins // 256
    low = lane_of((LANES, LANES)) < HALF
    for group in range(groups):
        rows = values[group * LANES : (group + 1) * LANES]
        turned = pltpu.roll(rows, HALF, 1)
        for h in range(2):
            top = jnp.where(low, turned if h else rows, 0.0)
            bottom = jnp.where(low, 0.0, rows if h else turned)
            both = jnp.concatenate([top, bottom], axis=0)
            high = both.astype(BF16)
            rest = (both - high.astype(F32)).astype(BF16)
            stack[h * groups + group, :, :LANES] = high
            stack[h * groups + group, :, LANES:] = rest
    result[...] = jnp.zeros_like(result)
    pairs = ins // 256

    def step(index, carry):
        at = pl.multiple_of(lax.div(index, pairs) * tile, tile)
        pair = lax.rem(index, pairs)
        columns = right[:, pl.ds(pl.multiple_of(pair * 256, 256), 256)]
        highs, lows = [], []
        for h in range(2):
            lines = left[pl.ds(h * (outs // 2) + at, tile)]
            kernel = jnp.exp(jnp.dot(lines, columns, preferred_element_type=F32))
            high = kernel.astype(BF16)
            highs.append(high)
            lows.append((kernel - high.astype(F32)).astype(BF16))
        total = result[pl.ds(at, tile)]
        for a in range(2):
            weights = stack[pair * 2 + a]
            cut = slice(a * LANES, (a + 1) * LANES)
            high = jnp.concatenate([highs[0][:, cut], highs[1][:, cut]], axis=1)
            rest = jnp.concatenate([lows[0][:, cut], lows[1][:, cut]], axis=1)
            both = jnp.dot(high, weights, preferred_element_type=F32)
            total = total + both[:, :LANES] + both[:, LANES:]
            total = total + jnp.dot(rest, weights[:, :LANES], preferred_element_type=F32)
        result[pl.ds(at, tile)] = total
        return carry

    lax.fori_loop(0, (outs // 2 // tile) * pairs, step, 0)


def first_product_kernel(unit_ref, col_ref, out_ref, left, right, stack):
    col_pts = ordered([unit_ref[i, 32:] for i in range(unit_ref.shape[0])])
    row_pts = ordered([col_ref[i] for i in range(col_ref.shape[0])])
    values = jnp.concatenate([unit_ref[i, :32] for i in range(unit_ref.shape[0])], axis=0)
    apply_kernel_matrix(row_pts, col_pts, values, out_ref, left, right, stack)


def second_product_kernel(unit_ref, col_ref, raw_ref, rhs_ref, noise_ref, out_ref, image_ref, left, right, stack):
    col_pts = ordered([unit_ref[i, 32:] for i in range(unit_ref.shape[0])])
    row_pts = ordered([col_ref[i] for i in range(col_ref.shape[0])])
    rhs = rhs_ref[...]
    image = raw_ref[...] + noise_ref[...] * rhs
    image_ref[...] = image
    values = rhs - THETA * image
    apply_kernel_matrix(col_pts, row_pts, values, out_ref, left, right, stack)


def product_scratch(outs, ins):
    return [
        pltpu.VMEM((outs, LANES), BF16),
        pltpu.VMEM((LANES, ins), BF16),
        pltpu.VMEM((ins // LANES, 256, 256), BF16),
    ]


def product_cost(outs, ins):
    return pl.CostEstimate(
        flops=2 * outs * ins * 512, bytes_accessed=8 * (outs + ins) * HALF, transcendentals=outs * ins
    )


def first_product(units, col_pts):
    ins, outs = units.shape[0] * 64, col_pts.shape[0] * 64
    return pl.pallas_call(
        first_product_kernel,
        in_specs=[VMEM] * 2,
        out_specs=VMEM,
        out_shape=jax.ShapeDtypeStruct((outs // 2, LANES), F32),
        scratch_shapes=product_scratch(outs, ins),
        cost_estimate=product_cost(outs, ins),
        name="first_product",
    )(units, col_pts)


def second_product(units, col_pts, raw, rhs, noise):
    outs, ins = units.shape[0] * 64, col_pts.shape[0] * 64
    return pl.pallas_call(
        second_product_kernel,
        in_specs=[VMEM] * 5,
        out_specs=[VMEM] * 2,
        out_shape=[
            jax.ShapeDtypeStruct((outs // 2, LANES), F32),
            jax.ShapeDtypeStruct((ins // 2, LANES), F32),
        ],
        scratch_shapes=product_scratch(outs, ins),
        cost_estimate=product_cost(outs, ins),
        name="second_product",
    )(units, col_pts, raw, rhs, noise)


def final_kernel(rhs_ref, packed_ref, image_ref, second_ref, sol_c_ref, res_c_ref, sol_ref, res_ref):
    low = lane_of((32, LANES)) < HALF

    def spread(ref, tile):
        pieces = []
        for part in range(2):
            rows = ref[tile * 64 + part * 32 : tile * 64 + part * 32 + 32]
            pieces += [jnp.where(low, rows, 0.0), jnp.where(low, 0.0, rows)]
        return jnp.concatenate(pieces, axis=0)

    def mixed(coefs, spreads):
        return lax.dot_general(
            coefs, spreads, (((1,), (1,)), ((), ())), precision=HIGH, preferred_element_type=F32
        )

    for tile in range(rhs_ref.shape[1] // LANES):
        cut = slice(tile * LANES, (tile + 1) * LANES)
        image = spread(image_ref, tile)
        sol_ref[:, cut] = mixed(
            sol_c_ref[...], jnp.concatenate([spread(packed_ref, tile), image], axis=1)
        )
        res_ref[:, cut] = rhs_ref[:, cut] - mixed(
            res_c_ref[...], jnp.concatenate([image, spread(second_ref, tile)], axis=1)
        )


def final_outputs(right_sides, rhs, image, second, sol_coefs, res_coefs):
    return pl.pallas_call(
        final_kernel,
        in_specs=[VMEM] * 6,
        out_specs=[VMEM] * 2,
        out_shape=[jax.ShapeDtypeStruct(right_sides.shape, F32)] * 2,
        name="final_outputs",
    )(right_sides, rhs, image, second, sol_coefs, res_coefs)


def exchanged(parts, axis):
    return lax.all_to_all(parts, axis, 0, 0, tiled=True)


def shared(value, axis):
    return exchanged(jnp.broadcast_to(value[None], (lax.axis_size(axis), *value.shape)), axis)


def solve_sym(matrix, target):
    lower = jnp.linalg.cholesky(0.5 * (matrix + matrix.T))
    return jax.scipy.linalg.cho_solve((lower, True), target)


def twice(coefs):
    zero = jnp.zeros_like(coefs)
    return jnp.block([[coefs, zero], [zero, coefs]])


def times(value, coefs):
    return jnp.dot(value, twice(coefs), precision=HIGH)


def side_by_side(first, second):
    return jnp.concatenate([first, second], axis=1)


def on_device(points, noise_level, right_sides):
    rows, cols = lax.axis_size("row"), lax.axis_size(COL)
    col_index = lax.axis_index(COL)[None].astype(jnp.int32)
    row_units, col_units = own_units(col_index, right_sides, points, rows, cols)
    units = exchanged(row_units, "row")
    col_pts = exchanged(col_units, COL)
    rhs, noise = packed_rows(right_sides, noise_level)

    part = first_product(units, col_pts).reshape(cols, 32, LANES)
    own = jnp.sum(exchanged(part, COL), axis=0)
    raw = shared(own, COL).reshape(-1, LANES)
    part, image = second_product(units, col_pts, raw, rhs, noise)
    part = part.reshape(rows, 32, LANES)

    grams = side_by_side(block_dot(rhs, rhs), block_dot(rhs, image))
    grams = jnp.sum(shared(grams, "row"), axis=0)
    gram, curv = grams[:, :HALF], grams[:, HALF:]
    own = jnp.sum(exchanged(part, "row"), axis=0)
    coef0 = solve_sym(curv, gram)
    residual = rhs - times(image, coef0)
    gram1 = block_dot(residual, residual)
    gram1 = side_by_side(gram1[:32], gram1[32:])
    gram1 = jnp.sum(shared(gram1, "row"), axis=0)
    gram1 = jnp.concatenate([gram1[:, :HALF], gram1[:, HALF:]], axis=0)
    raw = shared(own, COL).reshape(-1, LANES)
    dcoef = solve_sym(gram, gram1)
    second = raw + noise * (rhs - THETA * image)

    direction = residual + times(rhs, dcoef)
    scaled = coef0 / THETA
    image1 = times(image, jnp.eye(HALF, dtype=F32) - scaled + dcoef) + times(second, scaled)
    curv1 = block_dot(direction, image1)
    curv1 = side_by_side(curv1[:32], curv1[32:])
    curv1 = jnp.sum(shared(curv1, "row"), axis=0)
    curv1 = jnp.concatenate([curv1[:, :HALF], curv1[:, HALF:]], axis=0)
    coef1 = solve_sym(curv1, gram1)

    linear = coef0 + coef1 + jnp.dot(dcoef, coef1, precision=HIGH)
    square = jnp.dot(coef0, coef1, precision=HIGH)
    scaled = square / THETA
    doubled = lambda a, b: jnp.concatenate([a.T, a.T, b.T, b.T], axis=1)
    sol, res = final_outputs(
        right_sides, rhs, image, second, doubled(linear, -square), doubled(linear - scaled, scaled)
    )
    norms = jnp.sum(res * res, axis=1)[None, :]
    norms = jnp.sum(shared(side_by_side(norms, norms), "row"), axis=0)[0, :HALF]
    return sol, res, jnp.sqrt(norms / jnp.diagonal(gram))


def solution(mesh):
    torus = Mesh(
        mesh.devices.reshape(mesh.shape["row"], 4, 4, 2), ("row", "col_0", "col_1", "col_2")
    )
    return jax.shard_map(
        on_device,
        mesh=torus,
        in_specs=(P(None, ROW_COL), P("row"), P(None, "row")),
        out_specs=(P(None, "row"), P(None, "row"), P()),
        check_vma=False,
    )
```

time: 449 us -> 283 us (0.63); the launches traced: 441 us -> 281 us
  waiting for transfers between devices: 133 us -> 56.8 us
  matrix products: 43.9 us -> 8.23 us
  blocking collectives: 127 us -> 92.4 us
  Pallas kernels: 0 us -> 30.4 us
  local copies, waits for them, and re-layouts: 25.9 us -> 6.4 us
  between operations: 15 us -> 1.01 us
  other arithmetic: 48.5 us -> 40.3 us
    all_gather x2 -> x0, waiting for transfers between devices: 70.2 us -> none  [picked(): lax.all_gather(value, axis)]
    dot_general x26 -> x10, matrix products: 42.7 us -> 6.93 us  [the longest x4 4.02 us: block_dot(): lax.dot_general(first, second, (((0,), (0,)), ((), ())), precision=HIGH,...]
    all_to_all x5 -> x4, blocking collectives: 127 us -> 92.4 us  [exchanged(): return lax.all_to_all(parts, axis, 0, 0, tiled=True)]
    pallas_call x0 -> x5, Pallas kernels: none -> 30.4 us  [the longest x1 9.8 us: second_product(): pl.pallas_call(second_product_kernel, in_specs=[VMEM] * 5, out_specs=[VME...]
    all_to_all x7 -> x0, other arithmetic: 10.5 us -> none  [sent_to_all(): lax.all_to_all(jnp.broadcast_to(value[None], (devices, *value.shape)), ax...]
    unnamed x21 -> x10, local copies, waits for them, and re-layouts: 9.02 us -> 0.83 us
    all_to_all x6, waiting for transfers between devices: 62.3 us -> 56.8 us  [exchanged(): return lax.all_to_all(parts, axis, 0, 0, tiled=True)]
  transfers between devices with their start and end apart: 8 -> 6, of which waited for: 8 -> 5; matrix products, arithmetic and copies ran while one was open for 8% -> 11% of each run, Pallas kernels for 0% -> 1%
where the time goes in v1:
time: 283 us; the launch traced here: 281 us
  blocking collectives  92.4 us (33%)
  waiting for transfers between devices  56.8 us (20%)
  starting transfers between devices  45.6 us (16%)
  other arithmetic  40.3 us (14%)
  Pallas kernels  30.4 us (11%)
  matrix products  8.23 us (3%)
  local copies, waits for them, and re-layouts  6.4 us (2%)
    all_to_all x4, blocking collectives, exchanged(): return lax.all_to_all(parts, axis, 0, 0, tiled=True)  92.4 us
    all_to_all x6, waiting for transfers between devices, exchanged(): return lax.all_to_all(parts, axis, 0, 0, tiled=True)  56.8 us
    all_to_all x6, starting transfers between devices, exchanged(): return lax.all_to_all(parts, axis, 0, 0, tiled=True)  45.6 us
    another operation x9, other arithmetic, solve_sym(): lower = jnp.linalg.cholesky(0.5 * (matrix + matrix.T))  19.6 us
    another operation x6, other arithmetic, solve_sym(): return jax.scipy.linalg.cho_solve((lower, True), target)  16.6 us
    pallas_call x1, Pallas kernels, second_product(): pl.pallas_call(second_product_kernel, in_specs=[VMEM] * 5, out_specs=[VME...  9.8 us
    pallas_call x1, Pallas kernels, first_product(): pl.pallas_call(first_product_kernel, in_specs=[VMEM] * 2, out_specs=VMEM,...  9.22 us
    pallas_call x1, Pallas kernels, final_outputs(): pl.pallas_call(final_kernel, in_specs=[VMEM] * 6, out_specs=[VMEM] * 2, o...  6.92 us
  transfers between devices with their start and end apart: 6, of which 5 were waited for; matrix products, arithmetic and copies ran while one was open for 11% of the time, Pallas kernels for 1%

profile of v1, /device:TPU:1, one launch (start us, length us, event | category | flops | bytes accessed | tf_op | source)
XLA Modules:
  0.0 281.1 jit_solution(6895777773601940563)
XLA Ops:
  0.6 1.7 own_units.1
  2.4 18.8 %all_to_all.50.col_ref = f32[32,8,128]{2,1,0:T(8,128)} all-to-all(f32[32,8,128]{2,1,0:T(8,128)} %get-tuple-element.15), channel_id=1, replica_groups=mesh['row'=16,'col_0'=4,'col_1'=4,'col_2'=2] {'col_0','col_1','col_2'}, dimensions={0} | all-to-all | bytes 262144 | tf_op jit(solution)/shard_map/all_to_all | solution.py:289
  21.2 28.0 %all_to_all.51.unit_ref = f32[16,40,128]{2,1,0:T(8,128)} all-to-all(f32[16,40,128]{2,1,0:T(8,128)} %get-tuple-element.14), channel_id=1, replica_groups=mesh['row'=16,'col_0'=4,'col_1'=4,'col_2'=2] {'row'}, dimensions={0} | all-to-all | bytes 655360 | tf_op jit(solution)/shard_map/all_to_all | solution.py:289
  49.1 9.2 %first_product.1 = f32[1024,128]{1,0:T(8,128)} custom-call(f32[16,40,128]{2,1,0:T(8,128)} %all_to_all.51.unit_ref, f32[32,8,128]{2,1,0:T(8,128)} %all_to_all.50.col_ref), custom_call_target="tpu_custom_call" | custom-call | flops 2147483648 | bytes 1572864 | tf_op jit(solution)/shard_map/first_product/pallas_call | solution.py:225
  58.4 21.8 %all_to_all.52 = f32[32,32,128]{2,1,0:T(8,128)S(1)} all-to-all(f32[32,32,128]{2,1,0:T(8,128)} %bitcast.90), channel_id=1, replica_groups=mesh['row'=16,'col_0'=4,'col_1'=4,'col_2'=2] {'col_0','col_1','col_2'}, dimensions={0} | all-to-all | bytes 1048576 | tf_op jit(solution)/shard_map/all_to_all | solution.py:289
  80.2 0.9 broadcast_in_dim.25
  81.1 3.7 %all-to-all-start.3 = ((f32[32,32,128]{2,1,0:T(8,128)}), f32[32,32,128]{2,1,0:T(8,128)S(1)}, u32[]{:S(2)}, u32[]{:S(2)}) async-start(f32[32,32,128]{2,1,0:T(8,128)} %broadcast_in_dim.25), calls=%async_computation.3 | async-start | bytes 1048576 | tf_op jit(solution)/shard_map/all_to_all | solution.py:289
  84.8 2.8 packed_rows.1
  87.6 8.7 %all-to-all-done.3 = f32[32,32,128]{2,1,0:T(8,128)S(1)} async-done(((f32[32,32,128]{2,1,0:T(8,128)}), f32[32,32,128]{2,1,0:T(8,128)S(1)}, u32[]{:S(2)}, u32[]{:S(2)}) %all-to-all-start.3) | async-done | bytes 524320 | tf_op jit(solution)/shard_map/all_to_all | solution.py:289
  96.3 0.8 copy-done.4
  97.1 9.8 %second_product.1 = (f32[512,128]{1,0:T(8,128)}, f32[1024,128]{1,0:T(8,128)}) custom-call(f32[16,40,128]{2,1,0:T(8,128)} %all_to_all.51.unit_ref, f32[32,8,128]{2,1,0:T(8,128)} %all_to_all.50.col_ref, f32[1024,128]{1,0:T(8,128)} %bitcast.89, f32[1024,128]{1,0:T(8,128)} %get-tuple-element.13.rhs_ref.packed_ref, f32[1024,128]{1,0:T(8,128)} %get-tuple-element.16.noise_ref), custom_call_target="tpu_custom_call" | custom-call | flops 2147483648 | bytes 1572864 | tf_op jit(solution)/shard_map/second_product/pallas_call | solution.py:238
  106.9 5.8 %all-to-all-start.4 = ((f32[16,32,128]{2,1,0:T(8,128)}), f32[16,32,128]{2,1,0:T(8,128)S(1)}, u32[]{:S(2)}, u32[]{:S(2)}) async-start(f32[16,32,128]{2,1,0:T(8,128)} %bitcast.92), calls=%async_computation.4 | async-start | bytes 524288 | tf_op jit(solution)/shard_map/all_to_all | solution.py:289
  112.7 1.0 fusion.63
  113.7 1.0 fusion.64
  114.9 13.1 %all-to-all-done.4 = f32[16,32,128]{2,1,0:T(8,128)S(1)} async-done(((f32[16,32,128]{2,1,0:T(8,128)}), f32[16,32,128]{2,1,0:T(8,128)S(1)}, u32[]{:S(2)}, u32[]{:S(2)}) %all-to-all-start.4) | async-done | bytes 262176 | tf_op jit(solution)/shard_map/all_to_all | solution.py:289
  128.0 0.8 broadcast_in_dim.27
  128.8 9.1 %all-to-all-start.6 = ((f32[16,64,128]{2,1,0:T(8,128)}), f32[16,64,128]{2,1,0:T(8,128)S(1)}, u32[]{:S(2)}, u32[]{:S(2)}) async-start(f32[16,64,128]{2,1,0:T(8,128)} %broadcast_in_dim.27), calls=%async_computation.6 | async-start | bytes 1048576 | tf_op jit(solution)/shard_map/all_to_all | solution.py:289
  137.9 22.8 %all-to-all-done.6 = f32[16,64,128]{2,1,0:T(8,128)S(1)} async-done(((f32[16,64,128]{2,1,0:T(8,128)}), f32[16,64,128]{2,1,0:T(8,128)S(1)}, u32[]{:S(2)}, u32[]{:S(2)}) %all-to-all-start.6) | async-done | bytes 524320 | tf_op jit(solution)/shard_map/all_to_all | solution.py:289
  160.7 0.9 broadcast_in_dim.26
  161.6 10.6 %all-to-all-start.5 = ((f32[32,32,128]{2,1,0:T(8,128)}), f32[32,32,128]{2,1,0:T(8,128)S(1)}, u32[]{:S(2)}, u32[]{:S(2)}) async-start(f32[32,32,128]{2,1,0:T(8,128)} %broadcast_in_dim.26), calls=%async_computation.5 | async-start | bytes 1048576 | tf_op jit(solution)/shard_map/all_to_all | solution.py:289
  172.7 5.8 %cholesky.59 = f32[64,64]{1,0:T(8,128)S(1)} custom-call(f32[64,64]{1,0:T(8,128)S(1)} %fusion.40), custom_call_target="Cholesky" | custom-call | tf_op jit(solution)/shard_map/jit(cholesky)/cholesky | solution.py:297
  178.6 0.6 compare_reduce_fusion.2
  179.2 0.7 fusion.13
  179.9 4.9 %custom-call.11 = f32[1,64,64]{1,2,0:T(8,128)S(1)} custom-call(f32[1,64,64]{2,1,0:T(8,128)S(1)} %fusion.13), custom_call_target="InvertDiagBlocksLowerTriangular" | custom-call | tf_op jit(solution)/shard_map/jit(_cho_solve)/triangular_solve | solution.py:298
  185.8 1.0 fusion.65
  187.0 0.7 broadcast_in_dim.28
  187.7 6.2 %all-to-all-start.7 = ((f32[16,32,128]{2,1,0:T(8,128)}), f32[16,32,128]{2,1,0:T(8,128)S(1)}, u32[]{:S(2)}, u32[]{:S(2)}) async-start(f32[16,32,128]{2,1,0:T(8,128)} %broadcast_in_dim.28), calls=%async_computation.7 | async-start | bytes 524288 | tf_op jit(solution)/shard_map/all_to_all | solution.py:289
  194.2 5.8 %cholesky.70 = f32[64,64]{1,0:T(8,128)S(1)} custom-call(f32[64,64]{1,0:T(8,128)S(1)} %fusion.34), custom_call_target="Cholesky" | custom-call | tf_op jit(solution)/shard_map/jit(cholesky)/cholesky | solution.py:297
  200.1 0.6 compare_reduce_fusion.1
  200.7 0.7 fusion.14
  201.4 4.9 %custom-call.12 = f32[1,64,64]{1,2,0:T(8,128)S(1)} custom-call(f32[1,64,64]{2,1,0:T(8,128)S(1)} %fusion.14), custom_call_target="InvertDiagBlocksLowerTriangular" | custom-call | tf_op jit(solution)/shard_map/jit(_cho_solve)/triangular_solve | solution.py:298
  206.3 1.7 all-to-all-done.7
  208.5 0.6 convolution_add_fusion.1
  209.2 0.6 fusion.3
  209.9 0.6 convolution_add_fusion
  210.5 1.0 fusion.66
  211.7 23.7 %all_to_all.53 = f32[16,32,128]{2,1,0:T(8,128)S(1)} all-to-all(f32[16,32,128]{2,1,0:T(8,128)S(1)} %broadcast_in_dim.29), channel_id=1, replica_groups=mesh['row'=16,'col_0'=4,'col_1'=4,'col_2'=2] {'row'}, dimensions={0} | all-to-all | bytes 524288 | tf_op jit(solution)/shard_map/all_to_all | solution.py:289
  235.8 5.8 %cholesky.81 = f32[64,64]{1,0:T(8,128)S(1)} custom-call(f32[64,64]{1,0:T(8,128)S(1)} %fusion.28), custom_call_target="Cholesky" | custom-call | tf_op jit(solution)/shard_map/jit(cholesky)/cholesky | solution.py:297
  241.6 0.6 compare_reduce_fusion
  242.3 0.7 fusion.15
  242.9 4.9 %custom-call.13 = f32[1,64,64]{1,2,0:T(8,128)S(1)} custom-call(f32[1,64,64]{2,1,0:T(8,128)S(1)} %fusion.15), custom_call_target="InvertDiagBlocksLowerTriangular" | custom-call | tf_op jit(solution)/shard_map/jit(_cho_solve)/triangular_solve | solution.py:298
  248.7 0.7 pad_maximum_fusion.1.res_c_ref
  249.5 0.7 pad_maximum_fusion.sol_c_ref
  250.2 6.9 %final_outputs.1 = (f32[64,2048]{1,0:T(8,128)}, f32[64,2048]{1,0:T(8,128)}) custom-call(f32[64,2048]{1,0:T(8,128)} %rhs_ref.5, f32[1024,128]{1,0:T(8,128)} %get-tuple-element.13.rhs_ref.packed_ref, f32[1024,128]{1,0:T(8,128)} %get-tuple-element.17.image_ref, f32[1024,128]{1,0:T(8,128)} %copy-done.2, f32[64,256]{1,0:T(8,128)} %pad_maximum_fusion.sol_c_ref, ...), custom_call_target="tpu_custom_call" | custom-call | tf_op jit(solution)/shard_map/final_outputs/pallas_call | solution.py:279
  257.1 1.2 multiply_reduce_fusion
  259.0 10.3 %all-to-all-start.9 = ((f32[16,1,128]{2,1,0:T(1,128)}), f32[16,1,128]{2,1,0:T(1,128)S(1)}, u32[]{:S(2)}, u32[]{:S(2)}) async-start(f32[16,1,128]{2,1,0:T(1,128)} %broadcast_in_dim.61), calls=%async_computation.9 | async-start | bytes 16384 | tf_op jit(solution)/shard_map/all_to_all | solution.py:289
  269.3 0.8 gather_fusion
  270.1 10.5 %all-to-all-done.9 = f32[16,1,128]{2,1,0:T(1,128)S(1)} async-done(((f32[16,1,128]{2,1,0:T(1,128)}), f32[16,1,128]{2,1,0:T(1,128)S(1)}, u32[]{:S(2)}, u32[]{:S(2)}) %all-to-all-start.9) | async-done | bytes 8224 | tf_op jit(solution)/shard_map/all_to_all | solution.py:289
  (60 shorter events, 5.4 us)
Async XLA Ops:
  81.1 15.2 %all-to-all-start.3 = ((f32[32,32,128]{2,1,0:T(8,128)}), f32[32,32,128]{2,1,0:T(8,128)S(1)}, u32[]{:S(2)}, u32[]{:S(2)}) async-start(f32[32,32,128]{2,1,0:T(8,128)} %broadcast_in_dim.25), calls=%async_computation.3 | async-start | bytes 1048576 | tf_op jit(solution)/shard_map/all_to_all | solution.py:289
  96.3 0.8 copy-start.4
  106.9 5.8 %copy-start = (f32[1024,128]{1,0:T(8,128)S(1)}, f32[1024,128]{1,0:T(8,128)}, u32[]{:S(2)}) copy-start(f32[1024,128]{1,0:T(8,128)} %get-tuple-element.13.rhs_ref.packed_ref) | copy-start | bytes 1572868
  106.9 21.1 %all-to-all-start.4 = ((f32[16,32,128]{2,1,0:T(8,128)}), f32[16,32,128]{2,1,0:T(8,128)S(1)}, u32[]{:S(2)}, u32[]{:S(2)}) async-start(f32[16,32,128]{2,1,0:T(8,128)} %bitcast.92), calls=%async_computation.4 | async-start | bytes 524288 | tf_op jit(solution)/shard_map/all_to_all | solution.py:289
  112.7 1.0 copy-start.1
  128.8 31.9 %all-to-all-start.6 = ((f32[16,64,128]{2,1,0:T(8,128)}), f32[16,64,128]{2,1,0:T(8,128)S(1)}, u32[]{:S(2)}, u32[]{:S(2)}) async-start(f32[16,64,128]{2,1,0:T(8,128)} %broadcast_in_dim.27), calls=%async_computation.6 | async-start | bytes 1048576 | tf_op jit(solution)/shard_map/all_to_all | solution.py:289
  161.6 25.4 %all-to-all-start.5 = ((f32[32,32,128]{2,1,0:T(8,128)}), f32[32,32,128]{2,1,0:T(8,128)S(1)}, u32[]{:S(2)}, u32[]{:S(2)}) async-start(f32[32,32,128]{2,1,0:T(8,128)} %broadcast_in_dim.26), calls=%async_computation.5 | async-start | bytes 1048576 | tf_op jit(solution)/shard_map/all_to_all | solution.py:289
  186.8 7.1 %copy-start.3 = (f32[1024,128]{1,0:T(8,128)S(1)}, f32[1024,128]{1,0:T(8,128)}, u32[]{:S(2)}) copy-start(f32[1024,128]{1,0:T(8,128)} %get-tuple-element.16.noise_ref) | copy-start | bytes 1572868
  187.7 20.2 %all-to-all-start.7 = ((f32[16,32,128]{2,1,0:T(8,128)}), f32[16,32,128]{2,1,0:T(8,128)S(1)}, u32[]{:S(2)}, u32[]{:S(2)}) async-start(f32[16,32,128]{2,1,0:T(8,128)} %broadcast_in_dim.28), calls=%async_computation.7 | async-start | bytes 524288 | tf_op jit(solution)/shard_map/all_to_all | solution.py:289
  194.0 15.8 %copy-start.2 = (f32[1024,128]{1,0:T(8,128)}, f32[1024,128]{1,0:T(8,128)S(1)}, u32[]{:S(2)}) copy-start(f32[1024,128]{1,0:T(8,128)S(1)} %bitcast_add_fusion.second_ref) | copy-start | bytes 1572868
  259.0 21.6 %all-to-all-start.9 = ((f32[16,1,128]{2,1,0:T(1,128)}), f32[16,1,128]{2,1,0:T(1,128)S(1)}, u32[]{:S(2)}, u32[]{:S(2)}) async-start(f32[16,1,128]{2,1,0:T(1,128)} %broadcast_in_dim.61), calls=%async_computation.9 | async-start | bytes 16384 | tf_op jit(solution)/shard_map/all_to_all | solution.py:289

commit v2 on v1

--- a/solution.py
+++ b/solution.py
@@ -1,5 +1,3 @@
-import functools
-
 import jax
 import jax.numpy as jnp
 from jax import lax
@@ -17,6 +15,7 @@
 LANES = 128
 HALF = 64
 VMEM = pl.BlockSpec(memory_space=pltpu.VMEM)
+SMEM = pl.BlockSpec(memory_space=pltpu.SMEM)
 
 
 def lane_of(shape):
@@ -60,13 +59,6 @@
         ],
         name="own_units",
     )(col_index, right_sides, points)
-
-
-def block_dot(first, second):
-    both = lax.dot_general(
-        first, second, (((0,), (0,)), ((), ())), precision=HIGH, preferred_element_type=F32
-    )
-    return both[:HALF, :HALF] + both[HALF:, HALF:]
 
 
 def packed_kernel(rhs_ref, noise_ref, packed_out, noise_out):
@@ -196,14 +188,26 @@
     apply_kernel_matrix(row_pts, col_pts, values, out_ref, left, right, stack)
 
 
-def second_product_kernel(unit_ref, col_ref, raw_ref, rhs_ref, noise_ref, out_ref, image_ref, left, right, stack):
+def second_product_kernel(
+    place_ref, unit_ref, col_ref, raw_ref, rhs_ref, noise_ref, out_ref, image_ref, left, right, stack, result, grams
+):
     col_pts = ordered([unit_ref[i, 32:] for i in range(unit_ref.shape[0])])
     row_pts = ordered([col_ref[i] for i in range(col_ref.shape[0])])
     rhs = rhs_ref[...]
     image = raw_ref[...] + noise_ref[...] * rhs
     image_ref[...] = image
     values = rhs - THETA * image
-    apply_kernel_matrix(col_pts, row_pts, values, out_ref, left, right, stack)
+    apply_kernel_matrix(col_pts, row_pts, values, result, left, right, stack)
+    both = jnp.concatenate([rhs, image], axis=1)
+    gram = transposed_dot(both, both)
+    grams[0:32] = folded(gram[:LANES, :LANES])
+    grams[32:64] = folded(gram[:LANES, LANES:])
+    grams[64:96] = folded(gram[LANES:, LANES:])
+    lines = [grams[pl.ds(32 * m + place_ref[0], 1)] for m in range(3)]
+    tail = jnp.concatenate(lines + [jnp.zeros((5, LANES), F32)], axis=0)
+    for place in range(out_ref.shape[0]):
+        out_ref[place, :32] = result[place * 32 : place * 32 + 32]
+        out_ref[place, 32:] = tail
 
 
 def product_scratch(outs, ins):
@@ -233,24 +237,158 @@
     )(units, col_pts)
 
 
-def second_product(units, col_pts, raw, rhs, noise):
+def second_product(place, units, col_pts, raw, rhs, noise):
     outs, ins = units.shape[0] * 64, col_pts.shape[0] * 64
     return pl.pallas_call(
         second_product_kernel,
-        in_specs=[VMEM] * 5,
+        in_specs=[SMEM] + [VMEM] * 5,
         out_specs=[VMEM] * 2,
         out_shape=[
-            jax.ShapeDtypeStruct((outs // 2, LANES), F32),
+            jax.ShapeDtypeStruct((units.shape[0], 40, LANES), F32),
             jax.ShapeDtypeStruct((ins // 2, LANES), F32),
         ],
-        scratch_shapes=product_scratch(outs, ins),
+        scratch_shapes=product_scratch(outs, ins)
+        + [pltpu.VMEM((outs // 2, LANES), F32), pltpu.VMEM((96, LANES), F32)],
         cost_estimate=product_cost(outs, ins),
         name="second_product",
-    )(units, col_pts, raw, rhs, noise)
-
-
-def final_kernel(rhs_ref, packed_ref, image_ref, second_ref, sol_c_ref, res_c_ref, sol_ref, res_ref):
+    )(place, units, col_pts, raw, rhs, noise)
+
+
+def transposed_dot(first, second):
+    return lax.dot_general(
+        first, second, (((0,), (0,)), ((), ())), precision=HIGH, preferred_element_type=F32
+    )
+
+
+def folded(gram):
+    total = gram[:HALF, :HALF] + gram[HALF:, HALF:]
+    return jnp.concatenate([total[:32], total[32:]], axis=1)
+
+
+def unfolded(lines):
+    return jnp.concatenate([lines[:, :HALF], lines[:, HALF:]], axis=0)
+
+
+def small_dot(first, second):
+    return jnp.dot(first, second, precision=HIGH, preferred_element_type=F32)
+
+
+def twice(coefs):
+    zero = jnp.zeros_like(coefs)
+    return jnp.concatenate(
+        [jnp.concatenate([coefs, zero], axis=1), jnp.concatenate([zero, coefs], axis=1)], axis=0
+    )
+
+
+def line(tile, index):
+    return jnp.broadcast_to(tile[index : index + 1], tile.shape)
+
+
+def solve_sym(matrix, target):
+    joined = jnp.concatenate([0.5 * (matrix + matrix.T), target], axis=1)
+    tiles = tuple(joined[8 * t : 8 * t + 8] for t in range(8))
+    sub = lax.broadcasted_iota(jnp.int32, (8, LANES), 0)
+
+    def step(group, tiles):
+        tiles = list(tiles)
+        for quad in range(2):
+            columns = []
+            for j in range(4):
+                lane = jnp.full((8, LANES), group * 8 + quad * 4 + j, jnp.int32)
+                columns.append([jnp.take_along_axis(tile, lane, axis=1) for tile in tiles])
+            for j in range(4):
+                at = quad * 4 + j
+                here = sub == at
+                inverse = 1.0 / line(columns[j][0], at)
+                row = line(tiles[0], at) * inverse
+                for t in range(8):
+                    new = tiles[t] - columns[j][t] * row
+                    tiles[t] = jnp.where(here, row, new) if t == 0 else new
+                for later in range(j + 1, 4):
+                    ratio = line(columns[later][0], at) * inverse
+                    for t in range(8):
+                        new = columns[later][t] - columns[j][t] * ratio
+                        columns[later][t] = jnp.where(here, ratio, new) if t == 0 else new
+        return tuple(tiles[1:] + tiles[:1])
+
+    tiles = lax.fori_loop(0, 8, step, tiles)
+    return jnp.concatenate(tiles, axis=0)[:, HALF:]
+
+
+def middle_kernel(core_ref, unit_ref, rhs_ref, image_ref, noise_ref, share_ref, second_ref, coef_ref, lines):
+    for place in range(unit_ref.shape[0]):
+        tail = unit_ref[place, 32:]
+        for m in range(3):
+            lines[32 * m + place : 32 * m + place + 1] = tail[m : m + 1]
+    gram, curv, square = (unfolded(lines[32 * m : 32 * m + 32]) for m in range(3))
+    coef0 = solve_sym(curv, gram)
+    cross = small_dot(curv, coef0)
+    gram1 = gram - cross - cross.T + small_dot(coef0.T, small_dot(square, coef0))
+    dcoef = solve_sym(gram, gram1)
+    rhs, image = rhs_ref[...], image_ref[...]
+    raw = jnp.concatenate([unit_ref[i, :32] for i in range(unit_ref.shape[0])], axis=0)
+    second = raw + noise_ref[...] * (rhs - THETA * image)
+    second_ref[...] = second
+    residual = rhs - small_dot(image, twice(coef0))
+    direction = residual + small_dot(rhs, twice(dcoef))
+    scaled = coef0 * (1.0 / THETA)
+    eye = (
+        lax.broadcasted_iota(jnp.int32, (HALF, HALF), 0) == lax.broadcasted_iota(jnp.int32, (HALF, HALF), 1)
+    ).astype(F32)
+    image1 = small_dot(
+        jnp.concatenate([image, second], axis=1),
+        jnp.concatenate([twice(eye - scaled + dcoef), twice(scaled)], axis=0),
+    )
+    crossed = transposed_dot(jnp.concatenate([direction, image1], axis=1), image1)
+    lines[0:32] = folded(crossed[:LANES])
+    lines[32:64] = folded(crossed[LANES:])
+    lines[64:96] = folded(transposed_dot(residual, residual))
+    start = pl.multiple_of(core_ref[0] * 16, 16)
+    part = jnp.concatenate([lines[pl.ds(32 * m + start, 16)] for m in range(3)], axis=0)
+    for place in range(share_ref.shape[0]):
+        share_ref[place] = part
+    coef_ref[0:64] = jnp.concatenate([coef0, dcoef], axis=1)
+    coef_ref[64:128] = jnp.concatenate([gram, eye], axis=1)
+
+
+def middle(core, units, rhs, image, noise, rows):
+    return pl.pallas_call(
+        middle_kernel,
+        in_specs=[SMEM] + [VMEM] * 4,
+        out_specs=[VMEM] * 3,
+        out_shape=[
+            jax.ShapeDtypeStruct((rows, 48, LANES), F32),
+            jax.ShapeDtypeStruct(rhs.shape, F32),
+            jax.ShapeDtypeStruct((128, LANES), F32),
+        ],
+        scratch_shapes=[pltpu.VMEM((96, LANES), F32)],
+        name="middle",
+    )(core, units, rhs, image, noise)
+
+
+def final_kernel(lines_ref, coef_ref, rhs_ref, packed_ref, image_ref, second_ref, sol_ref, res_ref, norm_ref):
     low = lane_of((32, LANES)) < HALF
+    curv1, square, gram1 = (
+        unfolded(jnp.concatenate([lines_ref[half, 16 * m : 16 * m + 16] for half in range(2)], axis=0))
+        for m in range(3)
+    )
+    coef0, dcoef = coef_ref[0:64, :HALF], coef_ref[0:64, HALF:]
+    gram, eye = coef_ref[64:128, :HALF], coef_ref[64:128, HALF:]
+    coef1 = solve_sym(curv1, gram1)
+    cross = small_dot(curv1, coef1)
+    gram2 = gram1 - cross - cross.T + small_dot(coef1.T, small_dot(square, coef1))
+    norms = jnp.sum(eye * gram2, axis=0, keepdims=True) / jnp.sum(eye * gram, axis=0, keepdims=True)
+    norm_ref[...] = jnp.sqrt(jnp.maximum(norms, 0.0))
+    linear = coef0 + coef1 + small_dot(dcoef, coef1)
+    quadratic = small_dot(coef0, coef1)
+    scaled = quadratic * (1.0 / THETA)
+
+    def doubled(first, second):
+        first, second = first.T, second.T
+        return jnp.concatenate([first, first, second, second], axis=1)
+
+    sol_c = doubled(linear, -quadratic)
+    res_c = doubled(linear - scaled, scaled)
 
     def spread(ref, tile):
         pieces = []
@@ -267,22 +405,21 @@
     for tile in range(rhs_ref.shape[1] // LANES):
         cut = slice(tile * LANES, (tile + 1) * LANES)
         image = spread(image_ref, tile)
-        sol_ref[:, cut] = mixed(
-            sol_c_ref[...], jnp.concatenate([spread(packed_ref, tile), image], axis=1)
+        sol_ref[:, cut] = mixed(sol_c, jnp.concatenate([spread(packed_ref, tile), image], axis=1))
+        res_ref[:, cut] = rhs_ref[:, cut] - mixed(
+            res_c, jnp.concatenate([image, spread(second_ref, tile)], axis=1)
         )
-        res_ref[:, cut] = rhs_ref[:, cut] - mixed(
-            res_c_ref[...], jnp.concatenate([image, spread(second_ref, tile)], axis=1)
-        )
-
-
-def final_outputs(right_sides, rhs, image, second, sol_coefs, res_coefs):
+
+
+def final_outputs(lines, coefs, right_sides, rhs, image, second):
     return pl.pallas_call(
         final_kernel,
         in_specs=[VMEM] * 6,
-        out_specs=[VMEM] * 2,
-        out_shape=[jax.ShapeDtypeStruct(right_sides.shape, F32)] * 2,
+        out_specs=[VMEM] * 3,
+        out_shape=[jax.ShapeDtypeStruct(right_sides.shape, F32)] * 2
+        + [jax.ShapeDtypeStruct((1, HALF), F32)],
         name="final_outputs",
-    )(right_sides, rhs, image, second, sol_coefs, res_coefs)
+    )(lines, coefs, right_sides, rhs, image, second)
 
 
 def exchanged(parts, axis):
@@ -291,24 +428,6 @@
 
 def shared(value, axis):
     return exchanged(jnp.broadcast_to(value[None], (lax.axis_size(axis), *value.shape)), axis)
-
-
-def solve_sym(matrix, target):
-    lower = jnp.linalg.cholesky(0.5 * (matrix + matrix.T))
-    return jax.scipy.linalg.cho_solve((lower, True), target)
-
-
-def twice(coefs):
-    zero = jnp.zeros_like(coefs)
-    return jnp.block([[coefs, zero], [zero, coefs]])
-
-
-def times(value, coefs):
-    return jnp.dot(value, twice(coefs), precision=HIGH)
-
-
-def side_by_side(first, second):
-    return jnp.concatenate([first, second], axis=1)
 
 
 def on_device(points, noise_level, right_sides):
@@ -322,42 +441,13 @@
     part = first_product(units, col_pts).reshape(cols, 32, LANES)
     own = jnp.sum(exchanged(part, COL), axis=0)
     raw = shared(own, COL).reshape(-1, LANES)
-    part, image = second_product(units, col_pts, raw, rhs, noise)
-    part = part.reshape(rows, 32, LANES)
-
-    grams = side_by_side(block_dot(rhs, rhs), block_dot(rhs, image))
-    grams = jnp.sum(shared(grams, "row"), axis=0)
-    gram, curv = grams[:, :HALF], grams[:, HALF:]
+    part, image = second_product(col_index, units, col_pts, raw, rhs, noise)
     own = jnp.sum(exchanged(part, "row"), axis=0)
-    coef0 = solve_sym(curv, gram)
-    residual = rhs - times(image, coef0)
-    gram1 = block_dot(residual, residual)
-    gram1 = side_by_side(gram1[:32], gram1[32:])
-    gram1 = jnp.sum(shared(gram1, "row"), axis=0)
-    gram1 = jnp.concatenate([gram1[:, :HALF], gram1[:, HALF:]], axis=0)
-    raw = shared(own, COL).reshape(-1, LANES)
-    dcoef = solve_sym(gram, gram1)
-    second = raw + noise * (rhs - THETA * image)
-
-    direction = residual + times(rhs, dcoef)
-    scaled = coef0 / THETA
-    image1 = times(image, jnp.eye(HALF, dtype=F32) - scaled + dcoef) + times(second, scaled)
-    curv1 = block_dot(direction, image1)
-    curv1 = side_by_side(curv1[:32], curv1[32:])
-    curv1 = jnp.sum(shared(curv1, "row"), axis=0)
-    curv1 = jnp.concatenate([curv1[:, :HALF], curv1[:, HALF:]], axis=0)
-    coef1 = solve_sym(curv1, gram1)
-
-    linear = coef0 + coef1 + jnp.dot(dcoef, coef1, precision=HIGH)
-    square = jnp.dot(coef0, coef1, precision=HIGH)
-    scaled = square / THETA
-    doubled = lambda a, b: jnp.concatenate([a.T, a.T, b.T, b.T], axis=1)
-    sol, res = final_outputs(
-        right_sides, rhs, image, second, doubled(linear, -square), doubled(linear - scaled, scaled)
-    )
-    norms = jnp.sum(res * res, axis=1)[None, :]
-    norms = jnp.sum(shared(side_by_side(norms, norms), "row"), axis=0)[0, :HALF]
-    return sol, res, jnp.sqrt(norms / jnp.diagonal(gram))
+    core = lax.axis_index(COL[-1])[None].astype(jnp.int32)
+    share, second, coefs = middle(core, shared(own, COL), rhs, image, noise, rows)
+    lines = lax.all_gather(jnp.sum(exchanged(share, "row"), axis=0), COL[-1])
+    sol, res, norms = final_outputs(lines, coefs, right_sides, rhs, image, second)
+    return sol, res, norms[0]
 
 
 def solution(mesh):

time: 283 us -> 207 us (0.73)
  blocking collectives: 92.4 us -> 145 us
  waiting for transfers between devices: 56.8 us -> 8.72 us
  starting transfers between devices: 45.6 us -> 3.68 us
  other arithmetic: 40.3 us -> 0.1 us
  Pallas kernels: 30.4 us -> 46 us
  matrix products: 8.23 us -> 0 us
  local copies, waits for them, and re-layouts: 6.4 us -> 1.69 us
    all_to_all x6 -> x1, waiting for transfers between devices: 56.8 us -> 8.72 us  [exchanged(): return lax.all_to_all(parts, axis, 0, 0, tiled=True)]
    all_to_all x4 -> x6, blocking collectives: 92.4 us -> 138 us  [exchanged(): return lax.all_to_all(parts, axis, 0, 0, tiled=True)]
    all_to_all x6 -> x1, starting transfers between devices: 45.6 us -> 3.68 us  [exchanged(): return lax.all_to_all(parts, axis, 0, 0, tiled=True)]
    another operation x15 -> x0, other arithmetic: 36.2 us -> none  [the longest x9 19.6 us: solve_sym(): lower = jnp.linalg.cholesky(0.5 * (matrix + matrix.T))]
    pallas_call x2 -> x3, Pallas kernels: 16.7 us -> 32.3 us  [the longest x1 11.6 us: middle(): pl.pallas_call(middle_kernel, in_specs=[SMEM] + [VMEM] * 4, out_specs=[VM...]
    all_gather x0 -> x1, blocking collectives: none -> 7.13 us  [on_device(): lines = lax.all_gather(jnp.sum(exchanged(share, 'row'), axis=0), COL[-1])]
    dot_general x10 -> x0, matrix products: 6.93 us -> none  [the longest x4 4.02 us: block_dot(): lax.dot_general(first, second, (((0,), (0,)), ((), ())), precision=HIGH,...]
    broadcast_in_dim x6 -> x2, local copies, waits for them, and re-layouts: 3.93 us -> 0.9 us  [shared(): jnp.broadcast_to(value[None], (lax.axis_size(axis), *value.shape))]
  transfers between devices with their start and end apart: 6 -> 1, of which waited for: 5 -> 1; matrix products, arithmetic and copies ran while one was open for 11% -> 0% of each run, Pallas kernels for 1% -> 1%
where the time goes in v2:
time: 207 us; the launch traced here: 206 us
  blocking collectives  145 us (70%)
  Pallas kernels  46 us (22%)
  waiting for transfers between devices  8.72 us (4%)
  starting transfers between devices  3.68 us (2%)
    all_to_all x6, blocking collectives, exchanged(): return lax.all_to_all(parts, axis, 0, 0, tiled=True)  138 us
    pallas_call x1, Pallas kernels, middle(): pl.pallas_call(middle_kernel, in_specs=[SMEM] + [VMEM] * 4, out_specs=[VM...  11.6 us
    pallas_call x1, Pallas kernels, second_product(): pl.pallas_call(second_product_kernel, in_specs=[SMEM] + [VMEM] * 5, out_s...  11.1 us
    pallas_call x1, Pallas kernels, final_outputs(): pl.pallas_call(final_kernel, in_specs=[VMEM] * 6, out_specs=[VMEM] * 3, o...  9.65 us
    pallas_call x1, Pallas kernels, first_product(): pl.pallas_call(first_product_kernel, in_specs=[VMEM] * 2, out_specs=VMEM,...  9.23 us
    all_to_all x1, waiting for transfers between devices, exchanged(): return lax.all_to_all(parts, axis, 0, 0, tiled=True)  8.72 us
    all_gather x1, blocking collectives, on_device(): lines = lax.all_gather(jnp.sum(exchanged(share, 'row'), axis=0), COL[-1])  7.13 us
  transfers between devices with their start and end apart: 1, of which 1 were waited for; matrix products, arithmetic and copies ran while one was open for 0% of the time, Pallas kernels for 1%

profile of v2, /device:TPU:1, one launch (start us, length us, event | category | flops | bytes accessed | tf_op | source)
XLA Modules:
  0.0 206.1 jit_solution(5020140212997734824)
XLA Ops:
  0.6 1.7 own_units.1
  2.4 18.8 %all_to_all.35.col_ref = f32[32,8,128]{2,1,0:T(8,128)} all-to-all(f32[32,8,128]{2,1,0:T(8,128)} %get-tuple-element.16), channel_id=1, replica_groups=mesh['row'=16,'col_0'=4,'col_1'=4,'col_2'=2] {'col_0','col_1','col_2'}, dimensions={0} | all-to-all | bytes 262144 | tf_op jit(solution)/shard_map/all_to_all | solution.py:426
  21.2 28.0 %all_to_all.36.unit_ref = f32[16,40,128]{2,1,0:T(8,128)} all-to-all(f32[16,40,128]{2,1,0:T(8,128)} %get-tuple-element.15), channel_id=1, replica_groups=mesh['row'=16,'col_0'=4,'col_1'=4,'col_2'=2] {'row'}, dimensions={0} | all-to-all | bytes 655360 | tf_op jit(solution)/shard_map/all_to_all | solution.py:426
  49.1 9.2 %first_product.1 = f32[1024,128]{1,0:T(8,128)} custom-call(f32[16,40,128]{2,1,0:T(8,128)} %all_to_all.36.unit_ref, f32[32,8,128]{2,1,0:T(8,128)} %all_to_all.35.col_ref), custom_call_target="tpu_custom_call" | custom-call | flops 2147483648 | bytes 1572864 | tf_op jit(solution)/shard_map/first_product/pallas_call | solution.py:229
  58.4 21.8 %all_to_all.37 = f32[32,32,128]{2,1,0:T(8,128)S(1)} all-to-all(f32[32,32,128]{2,1,0:T(8,128)} %bitcast.8), channel_id=1, replica_groups=mesh['row'=16,'col_0'=4,'col_1'=4,'col_2'=2] {'col_0','col_1','col_2'}, dimensions={0} | all-to-all | bytes 1048576 | tf_op jit(solution)/shard_map/all_to_all | solution.py:426
  80.2 0.9 broadcast_in_dim.23
  81.1 3.7 %all-to-all-start.3 = ((f32[32,32,128]{2,1,0:T(8,128)}), f32[32,32,128]{2,1,0:T(8,128)S(1)}, u32[]{:S(2)}, u32[]{:S(2)}) async-start(f32[32,32,128]{2,1,0:T(8,128)} %broadcast_in_dim.23), calls=%async_computation.3 | async-start | bytes 1048576 | tf_op jit(solution)/shard_map/all_to_all | solution.py:426
  84.8 2.8 %packed_rows.1 = (f32[1024,128]{1,0:T(8,128)}, f32[1024,128]{1,0:T(8,128)}) custom-call(f32[64,2048]{1,0:T(8,128)} %rhs_ref.5, f32[1,2048]{1,0:T(1,128)} %bitcast.10), custom_call_target="tpu_custom_call" | custom-call | flops 4000000000 | bytes 1572864 | tf_op jit(solution)/shard_map/packed_rows/pallas_call | solution.py:80
  87.6 8.7 %all-to-all-done.3 = f32[32,32,128]{2,1,0:T(8,128)S(1)} async-done(((f32[32,32,128]{2,1,0:T(8,128)}), f32[32,32,128]{2,1,0:T(8,128)S(1)}, u32[]{:S(2)}, u32[]{:S(2)}) %all-to-all-start.3) | async-done | bytes 524320 | tf_op jit(solution)/shard_map/all_to_all | solution.py:426
  96.3 0.0 copy-start
  96.3 0.8 copy-done
  97.1 11.1 %second_product.1 = (f32[16,40,128]{2,1,0:T(8,128)}, f32[1024,128]{1,0:T(8,128)}) custom-call(s32[1]{0:T(128)} %bitcast.1.col_ref.place_ref, f32[16,40,128]{2,1,0:T(8,128)} %all_to_all.36.unit_ref, f32[32,8,128]{2,1,0:T(8,128)} %all_to_all.35.col_ref, f32[1024,128]{1,0:T(8,128)} %bitcast.7, f32[1024,128]{1,0:T(8,128)} %get-tuple-element.17.rhs_ref.packed_ref, ...), custom_call_target="tpu_custom_call" | custom-call | flops 2147483648 | bytes 1572864 | tf_op jit(solution)/shard_map/second_product/pallas_call | solution.py:242
  108.2 23.7 %all_to_all.38 = f32[16,40,128]{2,1,0:T(8,128)S(1)} all-to-all(f32[16,40,128]{2,1,0:T(8,128)} %get-tuple-element.19), channel_id=1, replica_groups=mesh['row'=16,'col_0'=4,'col_1'=4,'col_2'=2] {'row'}, dimensions={0} | all-to-all | bytes 655360 | tf_op jit(solution)/shard_map/all_to_all | solution.py:426
  131.9 20.5 %all_to_all.39.unit_ref = f32[32,40,128]{2,1,0:T(8,128)} all-to-all(f32[32,40,128]{2,1,0:T(8,128)S(1)} %broadcast_in_dim.25), channel_id=1, replica_groups=mesh['row'=16,'col_0'=4,'col_1'=4,'col_2'=2] {'col_0','col_1','col_2'}, dimensions={0} | all-to-all | bytes 1310720 | tf_op jit(solution)/shard_map/all_to_all | solution.py:426
  152.5 11.6 %middle.1 = (f32[16,48,128]{2,1,0:T(8,128)}, f32[1024,128]{1,0:T(8,128)}, f32[128,128]{1,0:T(8,128)}) custom-call(s32[1]{0:T(128)} %bitcast.core_ref, f32[32,40,128]{2,1,0:T(8,128)} %all_to_all.39.unit_ref, f32[1024,128]{1,0:T(8,128)} %get-tuple-element.17.rhs_ref.packed_ref, f32[1024,128]{1,0:T(8,128)} %get-tuple-element.20.image_ref, ...), custom_call_target="tpu_custom_call" | custom-call | tf_op jit(solution)/shard_map/middle/pallas_call | solution.py:355
  164.1 25.3 %all_to_all.40 = f32[16,48,128]{2,1,0:T(8,128)S(1)} all-to-all(f32[16,48,128]{2,1,0:T(8,128)} %get-tuple-element.21), channel_id=1, replica_groups=mesh['row'=16,'col_0'=4,'col_1'=4,'col_2'=2] {'row'}, dimensions={0} | all-to-all | bytes 786432 | tf_op jit(solution)/shard_map/all_to_all | solution.py:426
  189.3 7.1 %all-gather = f32[96,128]{1,0:T(8,128)} all-gather(f32[48,128]{1,0:T(8,128)S(1)} %reduce_sum.29), channel_id=2, replica_groups=mesh['row'=16,'col_0'=4,'col_1'=4,'col_2'=2] {'col_2'}, dimensions={0}, use_global_device_ids=true | all-gather | bytes 73728 | tf_op jit(solution)/shard_map/all_gather | solution.py:448
  196.5 9.6 %final_outputs.1 = (f32[64,2048]{1,0:T(8,128)}, f32[64,2048]{1,0:T(8,128)}, f32[1,64]{1,0:T(1,128)}) custom-call(f32[2,48,128]{2,1,0:T(8,128)} %bitcast.9, f32[128,128]{1,0:T(8,128)} %get-tuple-element.22.coef_ref, f32[64,2048]{1,0:T(8,128)} %rhs_ref.5, f32[1024,128]{1,0:T(8,128)} %get-tuple-element.17.rhs_ref.packed_ref, ...), custom_call_target="tpu_custom_call" | custom-call | tf_op jit(solution)/shard_map/final_outputs/pallas_call | solution.py:415
  (4 shorter events, 0.1 us)
Async XLA Ops:
  81.1 15.2 %all-to-all-start.3 = ((f32[32,32,128]{2,1,0:T(8,128)}), f32[32,32,128]{2,1,0:T(8,128)S(1)}, u32[]{:S(2)}, u32[]{:S(2)}) async-start(f32[32,32,128]{2,1,0:T(8,128)} %broadcast_in_dim.23), calls=%async_computation.3 | async-start | bytes 1048576 | tf_op jit(solution)/shard_map/all_to_all | solution.py:426
  96.3 0.8 copy-start

commit v3 on v2

--- a/solution.py
+++ b/solution.py
@@ -26,39 +26,25 @@
     return jnp.concatenate([turned[:32], turned[32:64]], axis=1)
 
 
-def own_kernel(col_ref, rhs_ref, pts_ref, row_out, col_out):
-    turned = rhs_ref[...].T
-    odd = lax.rem(col_ref[0], 2) == 1
-    block = packed(jnp.where(odd, turned[HALF:], turned[:HALF]))
-    pts = jnp.concatenate([pts_ref[...], pts_ref[...]], axis=1)
-    unit = jnp.concatenate([block, pts], axis=0)
+def own_kernel(pts_ref, row_out, col_out):
+    unit = jnp.concatenate([pts_ref[:4], pts_ref[4:]], axis=1)
     for place in range(row_out.shape[0]):
         row_out[place] = unit
     for place in range(col_out.shape[0]):
-        col_out[place] = pts
-
-
-def own_units(col_index, right_sides, points, rows, cols):
+        col_out[place] = unit
+
+
+def own_units(points, rows, cols):
     return pl.pallas_call(
         own_kernel,
-        grid_spec=pltpu.PrefetchScalarGridSpec(
-            num_scalar_prefetch=1,
-            grid=(1,),
-            in_specs=[
-                pl.BlockSpec((HALF, LANES), lambda i, c: (0, c[0] // 2)),
-                pl.BlockSpec((8, HALF), lambda i, c: (0, 0)),
-            ],
-            out_specs=[
-                pl.BlockSpec((rows, 40, LANES), lambda i, c: (0, 0, 0)),
-                pl.BlockSpec((cols, 8, LANES), lambda i, c: (0, 0, 0)),
-            ],
-        ),
+        in_specs=[VMEM],
+        out_specs=[VMEM] * 2,
         out_shape=[
-            jax.ShapeDtypeStruct((rows, 40, LANES), F32),
-            jax.ShapeDtypeStruct((cols, 8, LANES), F32),
+            jax.ShapeDtypeStruct((rows, 4, LANES), F32),
+            jax.ShapeDtypeStruct((cols, 4, LANES), F32),
         ],
         name="own_units",
-    )(col_index, right_sides, points)
+    )(points)
 
 
 def packed_kernel(rhs_ref, noise_ref, packed_out, noise_out):
@@ -89,8 +75,16 @@
     )(right_sides, noise_level[None, :])
 
 
-def ordered(units):
+def ordered(ref):
     place = lane_of((8, LANES)) // 32
+    low = lane_of((4, LANES)) < HALF
+    units = []
+    for index in range(ref.shape[0]):
+        unit = ref[index]
+        turned = pltpu.roll(unit, HALF, 1)
+        units.append(
+            jnp.concatenate([jnp.where(low, unit, turned), jnp.where(low, turned, unit)], axis=0)
+        )
     pieces = []
     for h in range(2):
         for start in range(0, len(units), 4):
@@ -181,28 +175,25 @@
     lax.fori_loop(0, (outs // 2 // tile) * pairs, step, 0)
 
 
-def first_product_kernel(unit_ref, col_ref, out_ref, left, right, stack):
-    col_pts = ordered([unit_ref[i, 32:] for i in range(unit_ref.shape[0])])
-    row_pts = ordered([col_ref[i] for i in range(col_ref.shape[0])])
-    values = jnp.concatenate([unit_ref[i, :32] for i in range(unit_ref.shape[0])], axis=0)
-    apply_kernel_matrix(row_pts, col_pts, values, out_ref, left, right, stack)
+def first_product_kernel(row_ref, col_ref, rhs_ref, out_ref, left, right, stack, result):
+    apply_kernel_matrix(ordered(row_ref), ordered(col_ref), rhs_ref[...], result, left, right, stack)
+    for place in range(out_ref.shape[0]):
+        out_ref[place] = result[place * 32 : place * 32 + 32]
 
 
 def second_product_kernel(
-    place_ref, unit_ref, col_ref, raw_ref, rhs_ref, noise_ref, out_ref, image_ref, left, right, stack, result, grams
+    place_ref, row_ref, col_ref, raw_ref, rhs_ref, noise_ref, out_ref, image_ref, left, right, stack, result, grams
 ):
-    col_pts = ordered([unit_ref[i, 32:] for i in range(unit_ref.shape[0])])
-    row_pts = ordered([col_ref[i] for i in range(col_ref.shape[0])])
     rhs = rhs_ref[...]
     image = raw_ref[...] + noise_ref[...] * rhs
     image_ref[...] = image
     values = rhs - THETA * image
-    apply_kernel_matrix(col_pts, row_pts, values, result, left, right, stack)
+    apply_kernel_matrix(ordered(row_ref), ordered(col_ref), values, result, left, right, stack)
     both = jnp.concatenate([rhs, image], axis=1)
     gram = transposed_dot(both, both)
-    grams[0:32] = folded(gram[:LANES, :LANES])
-    grams[32:64] = folded(gram[:LANES, LANES:])
-    grams[64:96] = folded(gram[LANES:, LANES:])
+    grams[0:32] = folded(summed_halves(gram[:LANES, :LANES]))
+    grams[32:64] = folded(summed_halves(gram[:LANES, LANES:]))
+    grams[64:96] = folded(summed_halves(gram[LANES:, LANES:]))
     lines = [grams[pl.ds(32 * m + place_ref[0], 1)] for m in range(3)]
     tail = jnp.concatenate(lines + [jnp.zeros((5, LANES), F32)], axis=0)
     for place in range(out_ref.shape[0]):
@@ -215,6 +206,7 @@
         pltpu.VMEM((outs, LANES), BF16),
         pltpu.VMEM((LANES, ins), BF16),
         pltpu.VMEM((ins // LANES, 256, 256), BF16),
+        pltpu.VMEM((outs // 2, LANES), F32),
     ]
 
 
@@ -224,34 +216,33 @@
     )
 
 
-def first_product(units, col_pts):
-    ins, outs = units.shape[0] * 64, col_pts.shape[0] * 64
+def first_product(row_pts, col_pts, rhs):
+    outs, ins = row_pts.shape[0] * 64, col_pts.shape[0] * 64
     return pl.pallas_call(
         first_product_kernel,
-        in_specs=[VMEM] * 2,
+        in_specs=[VMEM] * 3,
         out_specs=VMEM,
-        out_shape=jax.ShapeDtypeStruct((outs // 2, LANES), F32),
+        out_shape=jax.ShapeDtypeStruct((row_pts.shape[0], 32, LANES), F32),
         scratch_shapes=product_scratch(outs, ins),
         cost_estimate=product_cost(outs, ins),
         name="first_product",
-    )(units, col_pts)
-
-
-def second_product(place, units, col_pts, raw, rhs, noise):
-    outs, ins = units.shape[0] * 64, col_pts.shape[0] * 64
+    )(row_pts, col_pts, rhs)
+
+
+def second_product(place, row_pts, col_pts, raw, rhs, noise):
+    outs, ins = row_pts.shape[0] * 64, col_pts.shape[0] * 64
     return pl.pallas_call(
         second_product_kernel,
         in_specs=[SMEM] + [VMEM] * 5,
         out_specs=[VMEM] * 2,
         out_shape=[
-            jax.ShapeDtypeStruct((units.shape[0], 40, LANES), F32),
+            jax.ShapeDtypeStruct((row_pts.shape[0], 40, LANES), F32),
             jax.ShapeDtypeStruct((ins // 2, LANES), F32),
         ],
-        scratch_shapes=product_scratch(outs, ins)
-        + [pltpu.VMEM((outs // 2, LANES), F32), pltpu.VMEM((96, LANES), F32)],
+        scratch_shapes=product_scratch(outs, ins) + [pltpu.VMEM((96, LANES), F32)],
         cost_estimate=product_cost(outs, ins),
         name="second_product",
-    )(place, units, col_pts, raw, rhs, noise)
+    )(place, row_pts, col_pts, raw, rhs, noise)
 
 
 def transposed_dot(first, second):
@@ -260,13 +251,37 @@
     )
 
 
-def folded(gram):
-    total = gram[:HALF, :HALF] + gram[HALF:, HALF:]
-    return jnp.concatenate([total[:32], total[32:]], axis=1)
+def summed_halves(gram):
+    return gram[:HALF, :HALF] + gram[HALF:, HALF:]
+
+
+def folded(square):
+    return jnp.concatenate([square[:32], square[32:]], axis=1)
 
 
 def unfolded(lines):
     return jnp.concatenate([lines[:, :HALF], lines[:, HALF:]], axis=0)
+
+
+def row_and_column():
+    shape = (HALF, HALF)
+    return lax.broadcasted_iota(jnp.int32, shape, 0), lax.broadcasted_iota(jnp.int32, shape, 1)
+
+
+def squares_of(first, second, third):
+    row, column = row_and_column()
+    diagonal = jnp.sum(jnp.where(row == column, second, 0.0), axis=0, keepdims=True)
+    under = jnp.where(row == HALF - 1, diagonal, jnp.where(row == HALF - 2, diagonal[:, HALF - 1 :], 0.0))
+    return jnp.where(column >= row, first, second), jnp.where(column >= row, third, under)
+
+
+def matrices_of(upper, lower):
+    row, column = row_and_column()
+    turned, beneath = upper.T, lower.T
+    diagonal = jnp.where(column == HALF - 1, lower[HALF - 2 : HALF - 1, :1], lower[HALF - 1 :])
+    first = jnp.where(column >= row, upper, turned)
+    second = jnp.where(column == row, diagonal, jnp.where(column < row, upper, turned))
+    return first, second, jnp.where(column >= row, lower, beneath)
 
 
 def small_dot(first, second):
@@ -340,11 +355,16 @@
         jnp.concatenate([twice(eye - scaled + dcoef), twice(scaled)], axis=0),
     )
     crossed = transposed_dot(jnp.concatenate([direction, image1], axis=1), image1)
-    lines[0:32] = folded(crossed[:LANES])
-    lines[32:64] = folded(crossed[LANES:])
-    lines[64:96] = folded(transposed_dot(residual, residual))
+    curv1 = summed_halves(crossed[:LANES])
+    upper, lower = squares_of(
+        0.5 * (curv1 + curv1.T),
+        summed_halves(transposed_dot(residual, residual)),
+        summed_halves(crossed[LANES:]),
+    )
+    lines[0:32] = folded(upper)
+    lines[32:64] = folded(lower)
     start = pl.multiple_of(core_ref[0] * 16, 16)
-    part = jnp.concatenate([lines[pl.ds(32 * m + start, 16)] for m in range(3)], axis=0)
+    part = jnp.concatenate([lines[pl.ds(32 * m + start, 16)] for m in range(2)], axis=0)
     for place in range(share_ref.shape[0]):
         share_ref[place] = part
     coef_ref[0:64] = jnp.concatenate([coef0, dcoef], axis=1)
@@ -357,7 +377,7 @@
         in_specs=[SMEM] + [VMEM] * 4,
         out_specs=[VMEM] * 3,
         out_shape=[
-            jax.ShapeDtypeStruct((rows, 48, LANES), F32),
+            jax.ShapeDtypeStruct((rows, 32, LANES), F32),
             jax.ShapeDtypeStruct(rhs.shape, F32),
             jax.ShapeDtypeStruct((128, LANES), F32),
         ],
@@ -368,10 +388,11 @@
 
 def final_kernel(lines_ref, coef_ref, rhs_ref, packed_ref, image_ref, second_ref, sol_ref, res_ref, norm_ref):
     low = lane_of((32, LANES)) < HALF
-    curv1, square, gram1 = (
+    upper, lower = (
         unfolded(jnp.concatenate([lines_ref[half, 16 * m : 16 * m + 16] for half in range(2)], axis=0))
-        for m in range(3)
-    )
+        for m in range(2)
+    )
+    curv1, gram1, square = matrices_of(upper, lower)
     coef0, dcoef = coef_ref[0:64, :HALF], coef_ref[0:64, HALF:]
     gram, eye = coef_ref[64:128, :HALF], coef_ref[64:128, HALF:]
     coef1 = solve_sym(curv1, gram1)
@@ -433,15 +454,15 @@
 def on_device(points, noise_level, right_sides):
     rows, cols = lax.axis_size("row"), lax.axis_size(COL)
     col_index = lax.axis_index(COL)[None].astype(jnp.int32)
-    row_units, col_units = own_units(col_index, right_sides, points, rows, cols)
-    units = exchanged(row_units, "row")
+    row_units, col_units = own_units(points, rows, cols)
+    row_pts = exchanged(row_units, "row")
     col_pts = exchanged(col_units, COL)
     rhs, noise = packed_rows(right_sides, noise_level)
 
-    part = first_product(units, col_pts).reshape(cols, 32, LANES)
-    own = jnp.sum(exchanged(part, COL), axis=0)
+    part = first_product(row_pts, col_pts, rhs)
+    own = jnp.sum(exchanged(part, "row"), axis=0)
     raw = shared(own, COL).reshape(-1, LANES)
-    part, image = second_product(col_index, units, col_pts, raw, rhs, noise)
+    part, image = second_product(col_index, row_pts, col_pts, raw, rhs, noise)
     own = jnp.sum(exchanged(part, "row"), axis=0)
     core = lax.axis_index(COL[-1])[None].astype(jnp.int32)
     share, second, coefs = middle(core, shared(own, COL), rhs, image, noise, rows)

time: 207 us -> 198 us (0.957)
  blocking collectives: 145 us -> 105 us
  starting transfers between devices: 3.68 us -> 22.9 us
  waiting for transfers between devices: 8.72 us -> 20.4 us
    all_to_all x6 -> x5, blocking collectives: 138 us -> 98.4 us  [exchanged(): return lax.all_to_all(parts, axis, 0, 0, tiled=True)]
    all_to_all x1 -> x2, starting transfers between devices: 3.68 us -> 22.9 us  [exchanged(): return lax.all_to_all(parts, axis, 0, 0, tiled=True)]
    all_to_all x1 -> x2, waiting for transfers between devices: 8.72 us -> 20.4 us  [exchanged(): return lax.all_to_all(parts, axis, 0, 0, tiled=True)]
  transfers between devices with their start and end apart: 1 -> 2, of which waited for: 1 -> 2; matrix products, arithmetic and copies ran while one was open for 0% -> 0% of each run, Pallas kernels for 1% -> 1%
where the time goes in v3:
time: 198 us; the launch traced here: 197 us
  blocking collectives  105 us (53%)
  Pallas kernels  46.1 us (23%)
  starting transfers between devices  22.9 us (12%)
  waiting for transfers between devices  20.4 us (10%)
  local copies, waits for them, and re-layouts  2.3 us (1%)
    all_to_all x5, blocking collectives, exchanged(): return lax.all_to_all(parts, axis, 0, 0, tiled=True)  98.4 us
    all_to_all x2, starting transfers between devices, exchanged(): return lax.all_to_all(parts, axis, 0, 0, tiled=True)  22.9 us
    all_to_all x2, waiting for transfers between devices, exchanged(): return lax.all_to_all(parts, axis, 0, 0, tiled=True)  20.4 us
    pallas_call x1, Pallas kernels, middle(): pl.pallas_call(middle_kernel, in_specs=[SMEM] + [VMEM] * 4, out_specs=[VM...  11.7 us
    pallas_call x1, Pallas kernels, second_product(): pl.pallas_call(second_product_kernel, in_specs=[SMEM] + [VMEM] * 5, out_s...  11.1 us
    pallas_call x1, Pallas kernels, final_outputs(): pl.pallas_call(final_kernel, in_specs=[VMEM] * 6, out_specs=[VMEM] * 3, o...  9.73 us
    pallas_call x1, Pallas kernels, first_product(): pl.pallas_call(first_product_kernel, in_specs=[VMEM] * 3, out_specs=VMEM,...  9.37 us
    all_gather x1, blocking collectives, on_device(): lines = lax.all_gather(jnp.sum(exchanged(share, 'row'), axis=0), COL[-1])  6.4 us
  transfers between devices with their start and end apart: 2, of which 2 were waited for; matrix products, arithmetic and copies ran while one was open for 0% of the time, Pallas kernels for 1%

profile of v3, /device:TPU:1, one launch (start us, length us, event | category | flops | bytes accessed | tf_op | source)
XLA Modules:
  0.0 197.2 jit_solution(11149088977652138819)
XLA Ops:
  0.6 1.4 own_units.1
  2.0 18.5 %all_to_all.35.col_ref = f32[32,4,128]{2,1,0:T(4,128)} all-to-all(f32[32,4,128]{2,1,0:T(4,128)} %get-tuple-element.16), channel_id=1, replica_groups=mesh['row'=16,'col_0'=4,'col_1'=4,'col_2'=2] {'col_0','col_1','col_2'}, dimensions={0} | all-to-all | bytes 131072 | tf_op jit(solution)/shard_map/all_to_all | solution.py:447
  20.5 12.5 %all-to-all-start = ((f32[16,4,128]{2,1,0:T(4,128)}), f32[16,4,128]{2,1,0:T(4,128)S(1)}, u32[]{:S(2)}, u32[]{:S(2)}) async-start(f32[16,4,128]{2,1,0:T(4,128)} %get-tuple-element.15), calls=%async_computation | async-start | bytes 65536 | tf_op jit(solution)/shard_map/all_to_all | solution.py:447
  33.0 2.8 %packed_rows.1 = (f32[1024,128]{1,0:T(8,128)}, f32[1024,128]{1,0:T(8,128)}) custom-call(f32[64,2048]{1,0:T(8,128)} %rhs_ref.3, f32[1,2048]{1,0:T(1,128)} %bitcast.8), custom_call_target="tpu_custom_call" | custom-call | flops 4000000000 | bytes 1572864 | tf_op jit(solution)/shard_map/packed_rows/pallas_call | solution.py:66
  35.8 8.7 %all-to-all-done.row_ref = f32[16,4,128]{2,1,0:T(4,128)S(1)} async-done(((f32[16,4,128]{2,1,0:T(4,128)}), f32[16,4,128]{2,1,0:T(4,128)S(1)}, u32[]{:S(2)}, u32[]{:S(2)}) %all-to-all-start) | async-done | bytes 32800 | tf_op jit(solution)/shard_map/all_to_all | solution.py:447
  44.5 0.0 copy-start.1
  44.5 0.6 copy-done.1
  45.1 9.4 %first_product.1 = f32[16,32,128]{2,1,0:T(8,128)} custom-call(f32[16,4,128]{2,1,0:T(4,128)} %copy-done.1, f32[32,4,128]{2,1,0:T(4,128)} %all_to_all.35.col_ref, f32[1024,128]{1,0:T(8,128)} %get-tuple-element.17.rhs_ref.packed_ref), custom_call_target="tpu_custom_call" | custom-call | flops 2147483648 | bytes 1572864 | tf_op jit(solution)/shard_map/first_product/pallas_call | solution.py:221
  54.5 16.2 %all_to_all.36 = f32[16,32,128]{2,1,0:T(8,128)S(1)} all-to-all(f32[16,32,128]{2,1,0:T(8,128)} %first_product.1), channel_id=1, replica_groups=mesh['row'=16,'col_0'=4,'col_1'=4,'col_2'=2] {'row'}, dimensions={0} | all-to-all | bytes 524288 | tf_op jit(solution)/shard_map/all_to_all | solution.py:447
  70.7 0.9 broadcast_in_dim.24
  71.6 10.4 %all-to-all-start.3 = ((f32[32,32,128]{2,1,0:T(8,128)}), f32[32,32,128]{2,1,0:T(8,128)S(1)}, u32[]{:S(2)}, u32[]{:S(2)}) async-start(f32[32,32,128]{2,1,0:T(8,128)} %broadcast_in_dim.24), calls=%async_computation.3 | async-start | bytes 1048576 | tf_op jit(solution)/shard_map/all_to_all | solution.py:447
  82.0 11.7 %all-to-all-done.3 = f32[32,32,128]{2,1,0:T(8,128)S(1)} async-done(((f32[32,32,128]{2,1,0:T(8,128)}), f32[32,32,128]{2,1,0:T(8,128)S(1)}, u32[]{:S(2)}, u32[]{:S(2)}) %all-to-all-start.3) | async-done | bytes 524320 | tf_op jit(solution)/shard_map/all_to_all | solution.py:447
  93.7 0.0 copy-start
  93.7 0.8 copy-done
  94.5 11.1 %second_product.1 = (f32[16,40,128]{2,1,0:T(8,128)}, f32[1024,128]{1,0:T(8,128)}) custom-call(s32[1]{0:T(128)} %bitcast.1.place_ref, f32[16,4,128]{2,1,0:T(4,128)} %copy-done.1, f32[32,4,128]{2,1,0:T(4,128)} %all_to_all.35.col_ref, f32[1024,128]{1,0:T(8,128)} %bitcast.6, f32[1024,128]{1,0:T(8,128)} %get-tuple-element.17.rhs_ref.packed_ref, ...), custom_call_target="tpu_custom_call" | custom-call | flops 2147483648 | bytes 1572864 | tf_op jit(solution)/shard_map/second_product/pallas_call | solution.py:234
  105.6 23.3 %all_to_all.37 = f32[16,40,128]{2,1,0:T(8,128)S(1)} all-to-all(f32[16,40,128]{2,1,0:T(8,128)} %get-tuple-element.19), channel_id=1, replica_groups=mesh['row'=16,'col_0'=4,'col_1'=4,'col_2'=2] {'row'}, dimensions={0} | all-to-all | bytes 655360 | tf_op jit(solution)/shard_map/all_to_all | solution.py:447
  128.9 20.5 %all_to_all.38.unit_ref = f32[32,40,128]{2,1,0:T(8,128)} all-to-all(f32[32,40,128]{2,1,0:T(8,128)S(1)} %broadcast_in_dim.25), channel_id=1, replica_groups=mesh['row'=16,'col_0'=4,'col_1'=4,'col_2'=2] {'col_0','col_1','col_2'}, dimensions={0} | all-to-all | bytes 1310720 | tf_op jit(solution)/shard_map/all_to_all | solution.py:447
  149.4 11.7 %middle.1 = (f32[16,32,128]{2,1,0:T(8,128)}, f32[1024,128]{1,0:T(8,128)}, f32[128,128]{1,0:T(8,128)}) custom-call(s32[1]{0:T(128)} %bitcast.core_ref, f32[32,40,128]{2,1,0:T(8,128)} %all_to_all.38.unit_ref, f32[1024,128]{1,0:T(8,128)} %get-tuple-element.17.rhs_ref.packed_ref, f32[1024,128]{1,0:T(8,128)} %get-tuple-element.20.image_ref, ...), custom_call_target="tpu_custom_call" | custom-call | tf_op jit(solution)/shard_map/middle/pallas_call | solution.py:375
  161.1 19.9 %all_to_all.39 = f32[16,32,128]{2,1,0:T(8,128)S(1)} all-to-all(f32[16,32,128]{2,1,0:T(8,128)} %get-tuple-element.21), channel_id=1, replica_groups=mesh['row'=16,'col_0'=4,'col_1'=4,'col_2'=2] {'row'}, dimensions={0} | all-to-all | bytes 524288 | tf_op jit(solution)/shard_map/all_to_all | solution.py:447
  181.0 6.4 %all-gather = f32[64,128]{1,0:T(8,128)} all-gather(f32[32,128]{1,0:T(8,128)S(1)} %reduce_sum.29), channel_id=2, replica_groups=mesh['row'=16,'col_0'=4,'col_1'=4,'col_2'=2] {'col_2'}, dimensions={0}, use_global_device_ids=true | all-gather | bytes 49152 | tf_op jit(solution)/shard_map/all_gather | solution.py:469
  187.4 9.7 %final_outputs.1 = (f32[64,2048]{1,0:T(8,128)}, f32[64,2048]{1,0:T(8,128)}, f32[1,64]{1,0:T(1,128)}) custom-call(f32[2,32,128]{2,1,0:T(8,128)} %bitcast.7, f32[128,128]{1,0:T(8,128)} %get-tuple-element.22.coef_ref, f32[64,2048]{1,0:T(8,128)} %rhs_ref.3, f32[1024,128]{1,0:T(8,128)} %get-tuple-element.17.rhs_ref.packed_ref, ...), custom_call_target="tpu_custom_call" | custom-call | tf_op jit(solution)/shard_map/final_outputs/pallas_call | solution.py:436
  (4 shorter events, 0.1 us)
Async XLA Ops:
  20.5 24.0 %all-to-all-start = ((f32[16,4,128]{2,1,0:T(4,128)}), f32[16,4,128]{2,1,0:T(4,128)S(1)}, u32[]{:S(2)}, u32[]{:S(2)}) async-start(f32[16,4,128]{2,1,0:T(4,128)} %get-tuple-element.15), calls=%async_computation | async-start | bytes 65536 | tf_op jit(solution)/shard_map/all_to_all | solution.py:447
  44.5 0.6 copy-start.1
  71.6 22.1 %all-to-all-start.3 = ((f32[32,32,128]{2,1,0:T(8,128)}), f32[32,32,128]{2,1,0:T(8,128)S(1)}, u32[]{:S(2)}, u32[]{:S(2)}) async-start(f32[32,32,128]{2,1,0:T(8,128)} %broadcast_in_dim.24), calls=%async_computation.3 | async-start | bytes 1048576 | tf_op jit(solution)/shard_map/all_to_all | solution.py:447
  93.7 0.8 copy-start

commit v4 on v3

--- a/solution.py
+++ b/solution.py
@@ -16,6 +16,7 @@
 HALF = 64
 VMEM = pl.BlockSpec(memory_space=pltpu.VMEM)
 SMEM = pl.BlockSpec(memory_space=pltpu.SMEM)
+PARAMS = pltpu.CompilerParams(vmem_limit_bytes=16 * 1024 * 1024)
 
 
 def lane_of(shape):
@@ -43,6 +44,7 @@
             jax.ShapeDtypeStruct((rows, 4, LANES), F32),
             jax.ShapeDtypeStruct((cols, 4, LANES), F32),
         ],
+        compiler_params=PARAMS,
         name="own_units",
     )(points)
 
@@ -71,6 +73,7 @@
         cost_estimate=pl.CostEstimate(
             flops=4 * 10**9, bytes_accessed=3 * 4 * rows * LANES, transcendentals=0
         ),
+        compiler_params=PARAMS,
         name="packed_rows",
     )(right_sides, noise_level[None, :])
 
@@ -127,7 +130,7 @@
 def apply_kernel_matrix(out_pts, in_pts, values, result, left, right, stack):
     outs = left.shape[0]
     ins = right.shape[1]
-    tile = min(256, outs // 2)
+    tile = min(512, outs // 2)
     for start in range(0, outs, LANES):
         piece = augmented(out_pts[:, start : start + LANES], True)
         left[start : start + LANES] = piece.T.astype(BF16)
@@ -189,8 +192,7 @@
     image_ref[...] = image
     values = rhs - THETA * image
     apply_kernel_matrix(ordered(row_ref), ordered(col_ref), values, result, left, right, stack)
-    both = jnp.concatenate([rhs, image], axis=1)
-    gram = transposed_dot(both, both)
+    gram = gram_of(joined(two_parts(rhs), two_parts(image)))
     grams[0:32] = folded(summed_halves(gram[:LANES, :LANES]))
     grams[32:64] = folded(summed_halves(gram[:LANES, LANES:]))
     grams[64:96] = folded(summed_halves(gram[LANES:, LANES:]))
@@ -225,6 +227,7 @@
         out_shape=jax.ShapeDtypeStruct((row_pts.shape[0], 32, LANES), F32),
         scratch_shapes=product_scratch(outs, ins),
         cost_estimate=product_cost(outs, ins),
+        compiler_params=PARAMS,
         name="first_product",
     )(row_pts, col_pts, rhs)
 
@@ -241,14 +244,35 @@
         ],
         scratch_shapes=product_scratch(outs, ins) + [pltpu.VMEM((96, LANES), F32)],
         cost_estimate=product_cost(outs, ins),
+        compiler_params=PARAMS,
         name="second_product",
     )(place, row_pts, col_pts, raw, rhs, noise)
 
 
-def transposed_dot(first, second):
-    return lax.dot_general(
-        first, second, (((0,), (0,)), ((), ())), precision=HIGH, preferred_element_type=F32
-    )
+def two_parts(value):
+    high = value.astype(BF16)
+    return high, (value - high.astype(F32)).astype(BF16)
+
+
+def bf16_dot(first, second, first_dim, second_dim):
+    dims = (((first_dim,), (second_dim,)), ((), ()))
+    return lax.dot_general(first, second, dims, preferred_element_type=F32)
+
+
+def parts_dot(first, second, first_dim=1, second_dim=0):
+    high = bf16_dot(first[0], second[0], first_dim, second_dim)
+    cross = bf16_dot(first[0], second[1], first_dim, second_dim)
+    return high + cross + bf16_dot(first[1], second[0], first_dim, second_dim)
+
+
+def gram_of(parts):
+    high = bf16_dot(parts[0], parts[0], 0, 0)
+    cross = bf16_dot(parts[0], parts[1], 0, 0)
+    return high + cross + cross.T
+
+
+def joined(*pairs):
+    return tuple(jnp.concatenate([pair[i] for pair in pairs], axis=1) for i in range(2))
 
 
 def summed_halves(gram):
@@ -299,35 +323,38 @@
     return jnp.broadcast_to(tile[index : index + 1], tile.shape)
 
 
-def solve_sym(matrix, target):
-    joined = jnp.concatenate([0.5 * (matrix + matrix.T), target], axis=1)
-    tiles = tuple(joined[8 * t : 8 * t + 8] for t in range(8))
+def solve_sym(*systems):
     sub = lax.broadcasted_iota(jnp.int32, (8, LANES), 0)
-
-    def step(group, tiles):
-        tiles = list(tiles)
+    state = []
+    for matrix, target in systems:
+        both = jnp.concatenate([0.5 * (matrix + matrix.T), target], axis=1)
+        state.append(tuple(both[8 * t : 8 * t + 8] for t in range(8)))
+
+    def step(group, state):
+        state = [list(tiles) for tiles in state]
         for quad in range(2):
-            columns = []
-            for j in range(4):
-                lane = jnp.full((8, LANES), group * 8 + quad * 4 + j, jnp.int32)
-                columns.append([jnp.take_along_axis(tile, lane, axis=1) for tile in tiles])
+            lanes = [jnp.full((8, LANES), group * 8 + quad * 4 + j, jnp.int32) for j in range(4)]
+            spread = [
+                [[jnp.take_along_axis(tile, lane, axis=1) for tile in tiles] for lane in lanes] for tiles in state
+            ]
             for j in range(4):
                 at = quad * 4 + j
                 here = sub == at
-                inverse = 1.0 / line(columns[j][0], at)
-                row = line(tiles[0], at) * inverse
-                for t in range(8):
-                    new = tiles[t] - columns[j][t] * row
-                    tiles[t] = jnp.where(here, row, new) if t == 0 else new
-                for later in range(j + 1, 4):
-                    ratio = line(columns[later][0], at) * inverse
+                for tiles, columns in zip(state, spread):
+                    inverse = 1.0 / line(columns[j][0], at)
+                    row = line(tiles[0], at) * inverse
                     for t in range(8):
-                        new = columns[later][t] - columns[j][t] * ratio
-                        columns[later][t] = jnp.where(here, ratio, new) if t == 0 else new
-        return tuple(tiles[1:] + tiles[:1])
-
-    tiles = lax.fori_loop(0, 8, step, tiles)
-    return jnp.concatenate(tiles, axis=0)[:, HALF:]
+                        new = tiles[t] - columns[j][t] * row
+                        tiles[t] = jnp.where(here, row, new) if t == 0 else new
+                    for later in range(j + 1, 4):
+                        ratio = line(columns[later][0], at) * inverse
+                        for t in range(8):
+                            new = columns[later][t] - columns[j][t] * ratio
+                            columns[later][t] = jnp.where(here, ratio, new) if t == 0 else new
+        return tuple(tuple(tiles[1:] + tiles[:1]) for tiles in state)
+
+    state = lax.fori_loop(0, 8, step, tuple(state))
+    return [jnp.concatenate(tiles, axis=0)[:, HALF:] for tiles in state]
 
 
 def middle_kernel(core_ref, unit_ref, rhs_ref, image_ref, noise_ref, share_ref, second_ref, coef_ref, lines):
@@ -336,29 +363,36 @@
         for m in range(3):
             lines[32 * m + place : 32 * m + place + 1] = tail[m : m + 1]
     gram, curv, square = (unfolded(lines[32 * m : 32 * m + 32]) for m in range(3))
-    coef0 = solve_sym(curv, gram)
+    row, column = row_and_column()
+    eye = jnp.where(row == column, 1.0, 0.0)
+    coef0, inverse = solve_sym((curv, gram), (gram, eye))
     cross = small_dot(curv, coef0)
     gram1 = gram - cross - cross.T + small_dot(coef0.T, small_dot(square, coef0))
-    dcoef = solve_sym(gram, gram1)
+    dcoef = small_dot(inverse, gram1)
     rhs, image = rhs_ref[...], image_ref[...]
     raw = jnp.concatenate([unit_ref[i, :32] for i in range(unit_ref.shape[0])], axis=0)
     second = raw + noise_ref[...] * (rhs - THETA * image)
     second_ref[...] = second
-    residual = rhs - small_dot(image, twice(coef0))
-    direction = residual + small_dot(rhs, twice(dcoef))
     scaled = coef0 * (1.0 / THETA)
-    eye = (
-        lax.broadcasted_iota(jnp.int32, (HALF, HALF), 0) == lax.broadcasted_iota(jnp.int32, (HALF, HALF), 1)
-    ).astype(F32)
-    image1 = small_dot(
-        jnp.concatenate([image, second], axis=1),
-        jnp.concatenate([twice(eye - scaled + dcoef), twice(scaled)], axis=0),
-    )
-    crossed = transposed_dot(jnp.concatenate([direction, image1], axis=1), image1)
+    down = -twice(coef0)
+    turn = twice(dcoef)
+    mix = jnp.concatenate(
+        [
+            jnp.concatenate([turn, jnp.zeros_like(turn)], axis=1),
+            jnp.concatenate([down, down], axis=1),
+        ],
+        axis=0,
+    )
+    mix1 = jnp.concatenate([twice(eye - scaled + dcoef), twice(scaled)], axis=0)
+    rhs_parts, image_parts = two_parts(rhs), two_parts(image)
+    change = parts_dot(joined(rhs_parts, image_parts), two_parts(mix))
+    direction, residual = rhs + change[:, :LANES], rhs + change[:, LANES:]
+    image1 = two_parts(parts_dot(joined(image_parts, two_parts(second)), two_parts(mix1)))
+    crossed = parts_dot(joined(two_parts(direction), image1), image1, 0, 0)
     curv1 = summed_halves(crossed[:LANES])
     upper, lower = squares_of(
         0.5 * (curv1 + curv1.T),
-        summed_halves(transposed_dot(residual, residual)),
+        summed_halves(gram_of(two_parts(residual))),
         summed_halves(crossed[LANES:]),
     )
     lines[0:32] = folded(upper)
@@ -382,6 +416,7 @@
             jax.ShapeDtypeStruct((128, LANES), F32),
         ],
         scratch_shapes=[pltpu.VMEM((96, LANES), F32)],
+        compiler_params=PARAMS,
         name="middle",
     )(core, units, rhs, image, noise)
 
@@ -395,7 +430,7 @@
     curv1, gram1, square = matrices_of(upper, lower)
     coef0, dcoef = coef_ref[0:64, :HALF], coef_ref[0:64, HALF:]
     gram, eye = coef_ref[64:128, :HALF], coef_ref[64:128, HALF:]
-    coef1 = solve_sym(curv1, gram1)
+    (coef1,) = solve_sym((curv1, gram1))
     cross = small_dot(curv1, coef1)
     gram2 = gram1 - cross - cross.T + small_dot(coef1.T, small_dot(square, coef1))
     norms = jnp.sum(eye * gram2, axis=0, keepdims=True) / jnp.sum(eye * gram, axis=0, keepdims=True)
@@ -406,30 +441,28 @@
 
     def doubled(first, second):
         first, second = first.T, second.T
-        return jnp.concatenate([first, first, second, second], axis=1)
+        high, rest = two_parts(jnp.concatenate([first, first, second, second], axis=1))
+        return jnp.concatenate([high, rest], axis=0)
 
     sol_c = doubled(linear, -quadratic)
     res_c = doubled(linear - scaled, scaled)
 
-    def spread(ref, tile):
+    def spread(ref, start):
         pieces = []
-        for part in range(2):
-            rows = ref[tile * 64 + part * 32 : tile * 64 + part * 32 + 32]
+        for part in range(4):
+            rows = ref[start // 2 + part * 32 : start // 2 + part * 32 + 32]
             pieces += [jnp.where(low, rows, 0.0), jnp.where(low, 0.0, rows)]
-        return jnp.concatenate(pieces, axis=0)
-
-    def mixed(coefs, spreads):
-        return lax.dot_general(
-            coefs, spreads, (((1,), (1,)), ((), ())), precision=HIGH, preferred_element_type=F32
-        )
-
-    for tile in range(rhs_ref.shape[1] // LANES):
-        cut = slice(tile * LANES, (tile + 1) * LANES)
-        image = spread(image_ref, tile)
-        sol_ref[:, cut] = mixed(sol_c, jnp.concatenate([spread(packed_ref, tile), image], axis=1))
-        res_ref[:, cut] = rhs_ref[:, cut] - mixed(
-            res_c, jnp.concatenate([image, spread(second_ref, tile)], axis=1)
-        )
+        return two_parts(jnp.concatenate(pieces, axis=0))
+
+    def mixed(coefs, pair):
+        both = bf16_dot(coefs, pair[0], 1, 1)
+        return both[:HALF] + both[HALF:] + bf16_dot(coefs[:HALF], pair[1], 1, 1)
+
+    for start in range(0, rhs_ref.shape[1], 256):
+        cut = slice(start, start + 256)
+        image = spread(image_ref, start)
+        sol_ref[:, cut] = mixed(sol_c, joined(spread(packed_ref, start), image))
+        res_ref[:, cut] = rhs_ref[:, cut] - mixed(res_c, joined(image, spread(second_ref, start)))
 
 
 def final_outputs(lines, coefs, right_sides, rhs, image, second):
@@ -439,6 +472,7 @@
         out_specs=[VMEM] * 3,
         out_shape=[jax.ShapeDtypeStruct(right_sides.shape, F32)] * 2
         + [jax.ShapeDtypeStruct((1, HALF), F32)],
+        compiler_params=PARAMS,
         name="final_outputs",
     )(lines, coefs, right_sides, rhs, image, second)
 

time: 198 us -> 174 us (0.88)
  Pallas kernels: 46.1 us -> 23.3 us
  blocking collectives: 105 us -> 101 us
    pallas_call x1, Pallas kernels: 11.7 us -> 5.41 us  [middle(): pl.pallas_call(middle_kernel, in_specs=[SMEM] + [VMEM] * 4, out_specs=[VM...]
    pallas_call x1, Pallas kernels: 11.1 us -> 6.02 us  [second_product(): pl.pallas_call(second_product_kernel, in_specs=[SMEM] + [VMEM] * 5, out_s...]
    pallas_call x1, Pallas kernels: 9.73 us -> 5.13 us  [final_outputs(): pl.pallas_call(final_kernel, in_specs=[VMEM] * 6, out_specs=[VMEM] * 3, o...]
    pallas_call x1, Pallas kernels: 9.37 us -> 5.28 us  [first_product(): pl.pallas_call(first_product_kernel, in_specs=[VMEM] * 3, out_specs=VMEM,...]
    all_to_all x5, blocking collectives: 98.4 us -> 95.3 us  [exchanged(): return lax.all_to_all(parts, axis, 0, 0, tiled=True)]
    pallas_call x1, Pallas kernels: 2.78 us -> 0.77 us  [packed_rows(): pl.pallas_call(packed_kernel, in_specs=[VMEM] * 2, out_specs=[VMEM] * 2,...]
  transfers between devices with their start and end apart: 2 -> 2, of which waited for: 2 -> 2; matrix products, arithmetic and copies ran while one was open for 0% -> 0% of each run, Pallas kernels for 1% -> 0%
where the time goes in v4:
time: 174 us
  blocking collectives  101 us (58%)
  starting transfers between devices  24.3 us (14%)
  Pallas kernels  23.3 us (13%)
  waiting for transfers between devices  21.3 us (12%)
  local copies, waits for them, and re-layouts  2.62 us (2%)
    all_to_all x5, blocking collectives, exchanged(): return lax.all_to_all(parts, axis, 0, 0, tiled=True)  95.3 us
    all_to_all x2, starting transfers between devices, exchanged(): return lax.all_to_all(parts, axis, 0, 0, tiled=True)  24.3 us
    all_to_all x2, waiting for transfers between devices, exchanged(): return lax.all_to_all(parts, axis, 0, 0, tiled=True)  21.3 us
    all_gather x1, blocking collectives, on_device(): lines = lax.all_gather(jnp.sum(exchanged(share, 'row'), axis=0), COL[-1])  6.13 us
    pallas_call x1, Pallas kernels, second_product(): pl.pallas_call(second_product_kernel, in_specs=[SMEM] + [VMEM] * 5, out_s...  6.02 us
    pallas_call x1, Pallas kernels, middle(): pl.pallas_call(middle_kernel, in_specs=[SMEM] + [VMEM] * 4, out_specs=[VM...  5.41 us
    pallas_call x1, Pallas kernels, first_product(): pl.pallas_call(first_product_kernel, in_specs=[VMEM] * 3, out_specs=VMEM,...  5.28 us
    pallas_call x1, Pallas kernels, final_outputs(): pl.pallas_call(final_kernel, in_specs=[VMEM] * 6, out_specs=[VMEM] * 3, o...  5.13 us
  transfers between devices with their start and end apart: 2, of which 2 were waited for; matrix products, arithmetic and copies ran while one was open for 0% of the time, Pallas kernels for 0%

profile of v4, /device:TPU:1, one launch (start us, length us, event | category | flops | bytes accessed | tf_op | source)
XLA Modules:
  0.0 173.8 jit_solution(6045989381985700692)
XLA Ops:
  0.6 0.0 copy-start.2
  0.6 0.7 copy-done.2
  1.3 0.7 own_units.1
  2.0 16.9 %all_to_all.35.col_ref = f32[32,4,128]{2,1,0:T(4,128)S(1)} all-to-all(f32[32,4,128]{2,1,0:T(4,128)S(1)} %get-tuple-element.16), channel_id=1, replica_groups=mesh['row'=16,'col_0'=4,'col_1'=4,'col_2'=2] {'col_0','col_1','col_2'}, dimensions={0} | all-to-all | bytes 131072 | tf_op jit(solution)/shard_map/all_to_all | solution.py:481
  18.9 0.0 copy-start.3
  18.9 13.9 %all-to-all-start = ((f32[16,4,128]{2,1,0:T(4,128)}), f32[16,4,128]{2,1,0:T(4,128)S(1)}, u32[]{:S(2)}, u32[]{:S(2)}) async-start(f32[16,4,128]{2,1,0:T(4,128)} %get-tuple-element.15), calls=%async_computation | async-start | bytes 65536 | tf_op jit(solution)/shard_map/all_to_all | solution.py:481
  32.8 0.0 copy-done.3
  32.8 0.0 copy-start
  32.8 1.0 copy-done
  33.9 0.8 packed_rows.1
  34.6 9.6 %all-to-all-done.row_ref = f32[16,4,128]{2,1,0:T(4,128)S(1)} async-done(((f32[16,4,128]{2,1,0:T(4,128)}), f32[16,4,128]{2,1,0:T(4,128)S(1)}, u32[]{:S(2)}, u32[]{:S(2)}) %all-to-all-start) | async-done | bytes 32800 | tf_op jit(solution)/shard_map/all_to_all | solution.py:481
  44.3 5.3 %first_product.1 = f32[16,32,128]{2,1,0:T(8,128)S(1)} custom-call(f32[16,4,128]{2,1,0:T(4,128)S(1)} %all-to-all-done.row_ref, f32[32,4,128]{2,1,0:T(4,128)S(1)} %all_to_all.35.col_ref, f32[1024,128]{1,0:T(8,128)S(1)} %get-tuple-element.17.rhs_ref.packed_ref), custom_call_target="tpu_custom_call" | custom-call | flops 2147483648 | bytes 1572864 | tf_op jit(solution)/shard_map/first_product/pallas_call | solution.py:223
  49.6 15.3 %all_to_all.36 = f32[16,32,128]{2,1,0:T(8,128)S(1)} all-to-all(f32[16,32,128]{2,1,0:T(8,128)S(1)} %first_product.1), channel_id=1, replica_groups=mesh['row'=16,'col_0'=4,'col_1'=4,'col_2'=2] {'row'}, dimensions={0} | all-to-all | bytes 524288 | tf_op jit(solution)/shard_map/all_to_all | solution.py:481
  64.9 0.9 broadcast_in_dim.24
  65.8 10.4 %all-to-all-start.3 = ((f32[32,32,128]{2,1,0:T(8,128)}), f32[32,32,128]{2,1,0:T(8,128)S(1)}, u32[]{:S(2)}, u32[]{:S(2)}) async-start(f32[32,32,128]{2,1,0:T(8,128)} %broadcast_in_dim.24), calls=%async_computation.3 | async-start | bytes 1048576 | tf_op jit(solution)/shard_map/all_to_all | solution.py:481
  76.2 11.7 %all-to-all-done.3 = f32[32,32,128]{2,1,0:T(8,128)S(1)} async-done(((f32[32,32,128]{2,1,0:T(8,128)}), f32[32,32,128]{2,1,0:T(8,128)S(1)}, u32[]{:S(2)}, u32[]{:S(2)}) %all-to-all-start.3) | async-done | bytes 524320 | tf_op jit(solution)/shard_map/all_to_all | solution.py:481
  87.9 6.0 %second_product.1 = (f32[16,40,128]{2,1,0:T(8,128)S(1)}, f32[1024,128]{1,0:T(8,128)S(1)}) custom-call(s32[1]{0:T(128)} %bitcast.1.place_ref, f32[16,4,128]{2,1,0:T(4,128)S(1)} %all-to-all-done.row_ref, f32[32,4,128]{2,1,0:T(4,128)S(1)} %all_to_all.35.col_ref, f32[1024,128]{1,0:T(8,128)S(1)} %bitcast.6, f32[1024,128]{1,0:T(8,128)S(1)} %get-tuple-element.17.rhs_ref.packed_ref, ...), custom_call_target="tpu_custom_call" | custom-call | flops 2147483648 | bytes 1572864 | tf_op jit(solution)/shard_map/second_product/pallas_call | solution.py:237
  93.9 23.1 %all_to_all.37 = f32[16,40,128]{2,1,0:T(8,128)S(1)} all-to-all(f32[16,40,128]{2,1,0:T(8,128)S(1)} %get-tuple-element.19), channel_id=1, replica_groups=mesh['row'=16,'col_0'=4,'col_1'=4,'col_2'=2] {'row'}, dimensions={0} | all-to-all | bytes 655360 | tf_op jit(solution)/shard_map/all_to_all | solution.py:481
  117.1 20.3 %all_to_all.38.unit_ref = f32[32,40,128]{2,1,0:T(8,128)S(1)} all-to-all(f32[32,40,128]{2,1,0:T(8,128)S(1)} %broadcast_in_dim.25), channel_id=1, replica_groups=mesh['row'=16,'col_0'=4,'col_1'=4,'col_2'=2] {'col_0','col_1','col_2'}, dimensions={0} | all-to-all | bytes 1310720 | tf_op jit(solution)/shard_map/all_to_all | solution.py:481
  137.4 5.4 %middle.1 = (f32[16,32,128]{2,1,0:T(8,128)S(1)}, f32[1024,128]{1,0:T(8,128)S(1)}, f32[128,128]{1,0:T(8,128)S(1)}) custom-call(s32[1]{0:T(128)} %bitcast.core_ref, f32[32,40,128]{2,1,0:T(8,128)S(1)} %all_to_all.38.unit_ref, f32[1024,128]{1,0:T(8,128)S(1)} %get-tuple-element.17.rhs_ref.packed_ref, f32[1024,128]{1,0:T(8,128)S(1)} %get-tuple-element.20.image_ref, ...), custom_call_target="tpu_custom_call" | custom-call | tf_op jit(solution)/shard_map/middle/pallas_call | solution.py:409
  142.8 0.0 copy-start.1
  142.8 19.7 %all_to_all.39 = f32[16,32,128]{2,1,0:T(8,128)S(1)} all-to-all(f32[16,32,128]{2,1,0:T(8,128)S(1)} %get-tuple-element.21), channel_id=1, replica_groups=mesh['row'=16,'col_0'=4,'col_1'=4,'col_2'=2] {'row'}, dimensions={0} | all-to-all | bytes 524288 | tf_op jit(solution)/shard_map/all_to_all | solution.py:481
  162.5 6.1 %all-gather = f32[64,128]{1,0:T(8,128)S(1)} all-gather(f32[32,128]{1,0:T(8,128)S(1)} %reduce_sum.29), channel_id=2, replica_groups=mesh['row'=16,'col_0'=4,'col_1'=4,'col_2'=2] {'col_2'}, dimensions={0}, use_global_device_ids=true | all-gather | bytes 49152 | tf_op jit(solution)/shard_map/all_gather | solution.py:503
  168.6 0.0 copy-done.1
  168.6 5.1 %final_outputs.1 = (f32[64,2048]{1,0:T(8,128)}, f32[64,2048]{1,0:T(8,128)}, f32[1,64]{1,0:T(1,128)}) custom-call(f32[2,32,128]{2,1,0:T(8,128)S(1)} %bitcast.7, f32[128,128]{1,0:T(8,128)S(1)} %get-tuple-element.22.coef_ref, f32[64,2048]{1,0:T(8,128)S(1)} %copy-done.1, f32[1024,128]{1,0:T(8,128)S(1)} %get-tuple-element.17.rhs_ref.packed_ref, ...), custom_call_target="tpu_custom_call" | custom-call | tf_op jit(solution)/shard_map/final_outputs/pallas_call | solution.py:469
  (4 shorter events, 0.1 us)
Async XLA Ops:
  0.6 0.7 copy-start.2
  18.9 13.9 %copy-start.3 = (f32[2048]{0:T(1024)S(1)}, f32[2048]{0:T(1024)}, u32[]{:S(2)}) copy-start(f32[2048]{0:T(1024)} %param.4) | copy-start | bytes 24580
  18.9 25.3 %all-to-all-start = ((f32[16,4,128]{2,1,0:T(4,128)}), f32[16,4,128]{2,1,0:T(4,128)S(1)}, u32[]{:S(2)}, u32[]{:S(2)}) async-start(f32[16,4,128]{2,1,0:T(4,128)} %get-tuple-element.15), calls=%async_computation | async-start | bytes 65536 | tf_op jit(solution)/shard_map/all_to_all | solution.py:481
  32.8 1.0 copy-start
  65.8 22.1 %all-to-all-start.3 = ((f32[32,32,128]{2,1,0:T(8,128)}), f32[32,32,128]{2,1,0:T(8,128)S(1)}, u32[]{:S(2)}, u32[]{:S(2)}) async-start(f32[32,32,128]{2,1,0:T(8,128)} %broadcast_in_dim.24), calls=%async_computation.3 | async-start | bytes 1048576 | tf_op jit(solution)/shard_map/all_to_all | solution.py:481
  142.8 25.8 %copy-start.1 = (f32[64,2048]{1,0:T(8,128)S(1)}, f32[64,2048]{1,0:T(8,128)}, u32[]{:S(2)}) copy-start(f32[64,2048]{1,0:T(8,128)} %rhs_ref.3) | copy-start | bytes 1572868

commit v5 on v4

--- a/solution.py
+++ b/solution.py
@@ -15,7 +15,6 @@
 LANES = 128
 HALF = 64
 VMEM = pl.BlockSpec(memory_space=pltpu.VMEM)
-SMEM = pl.BlockSpec(memory_space=pltpu.SMEM)
 PARAMS = pltpu.CompilerParams(vmem_limit_bytes=16 * 1024 * 1024)
 
 
@@ -27,55 +26,61 @@
     return jnp.concatenate([turned[:32], turned[32:64]], axis=1)
 
 
-def own_kernel(pts_ref, row_out, col_out):
+def prepare_kernel(
+    pts_hbm, rhs_hbm, noise_hbm, row_out, col_out, packed_out, noise_out, pts_ref, rhs_ref, noise_ref, sems
+):
+    copies = [
+        pltpu.make_async_copy(source, target, sems.at[i])
+        for i, (source, target) in enumerate(((pts_hbm, pts_ref), (noise_hbm, noise_ref), (rhs_hbm, rhs_ref)))
+    ]
+    for copy in copies:
+        copy.start()
+    copies[0].wait()
     unit = jnp.concatenate([pts_ref[:4], pts_ref[4:]], axis=1)
     for place in range(row_out.shape[0]):
         row_out[place] = unit
     for place in range(col_out.shape[0]):
         col_out[place] = unit
-
-
-def own_units(points, rows, cols):
-    return pl.pallas_call(
-        own_kernel,
-        in_specs=[VMEM],
-        out_specs=[VMEM] * 2,
-        out_shape=[
-            jax.ShapeDtypeStruct((rows, 4, LANES), F32),
-            jax.ShapeDtypeStruct((cols, 4, LANES), F32),
-        ],
-        compiler_params=PARAMS,
-        name="own_units",
-    )(points)
-
-
-def packed_kernel(rhs_ref, noise_ref, packed_out, noise_out):
+    copies[1].wait()
     low = lane_of((32, LANES)) < HALF
     for tile in range(rhs_ref.shape[1] // LANES):
-        turned = rhs_ref[:, tile * LANES : (tile + 1) * LANES].T
         noise = noise_ref[:, tile * LANES : (tile + 1) * LANES]
         noise = jnp.broadcast_to(noise, (LANES, LANES)).T
         for part in range(2):
             rows = slice(tile * 64 + part * 32, tile * 64 + part * 32 + 32)
-            packed_out[rows] = packed(turned[part * 64 : part * 64 + 64])
             noise_out[rows] = jnp.where(
                 low, noise[part * 64 : part * 64 + 32], noise[part * 64 + 32 : part * 64 + 64]
             )
-
-
-def packed_rows(right_sides, noise_level):
-    rows = right_sides.shape[1] // 2
+    copies[2].wait()
+    for tile in range(rhs_ref.shape[1] // LANES):
+        turned = rhs_ref[:, tile * LANES : (tile + 1) * LANES].T
+        for part in range(2):
+            rows = slice(tile * 64 + part * 32, tile * 64 + part * 32 + 32)
+            packed_out[rows] = packed(turned[part * 64 : part * 64 + 64])
+
+
+def prepare(points, right_sides, noise_level, rows, cols):
+    lines = right_sides.shape[1] // 2
+    noise_row = noise_level[None, :]
     return pl.pallas_call(
-        packed_kernel,
-        in_specs=[VMEM] * 2,
-        out_specs=[VMEM] * 2,
-        out_shape=[jax.ShapeDtypeStruct((rows, LANES), F32)] * 2,
-        cost_estimate=pl.CostEstimate(
-            flops=4 * 10**9, bytes_accessed=3 * 4 * rows * LANES, transcendentals=0
-        ),
+        prepare_kernel,
+        in_specs=[pl.BlockSpec(memory_space=pltpu.HBM)] * 3,
+        out_specs=[VMEM] * 4,
+        out_shape=[
+            jax.ShapeDtypeStruct((rows, 4, LANES), F32),
+            jax.ShapeDtypeStruct((cols, 4, LANES), F32),
+            jax.ShapeDtypeStruct((lines, LANES), F32),
+            jax.ShapeDtypeStruct((lines, LANES), F32),
+        ],
+        scratch_shapes=[
+            pltpu.VMEM(points.shape, F32),
+            pltpu.VMEM(right_sides.shape, F32),
+            pltpu.VMEM(noise_row.shape, F32),
+            pltpu.SemaphoreType.DMA((3,)),
+        ],
         compiler_params=PARAMS,
-        name="packed_rows",
-    )(right_sides, noise_level[None, :])
+        name="prepare",
+    )(points, right_sides, noise_row)
 
 
 def ordered(ref):
@@ -127,16 +132,8 @@
     return jnp.concatenate(blocks + [zeros] * 6, axis=0)
 
 
-def apply_kernel_matrix(out_pts, in_pts, values, result, left, right, stack):
-    outs = left.shape[0]
-    ins = right.shape[1]
-    tile = min(512, outs // 2)
-    for start in range(0, outs, LANES):
-        piece = augmented(out_pts[:, start : start + LANES], True)
-        left[start : start + LANES] = piece.T.astype(BF16)
-    for start in range(0, ins, 256):
-        right[:, start : start + 256] = augmented(in_pts[:, start : start + 256], False).astype(BF16)
-    groups = ins // 256
+def stack_values(values, stack):
+    groups = values.shape[0] // LANES
     low = lane_of((LANES, LANES)) < HALF
     for group in range(groups):
         rows = values[group * LANES : (group + 1) * LANES]
@@ -144,34 +141,41 @@
         for h in range(2):
             top = jnp.where(low, turned if h else rows, 0.0)
             bottom = jnp.where(low, 0.0, rows if h else turned)
-            both = jnp.concatenate([top, bottom], axis=0)
-            high = both.astype(BF16)
-            rest = (both - high.astype(F32)).astype(BF16)
+            high, rest = two_parts(jnp.concatenate([top, bottom], axis=0))
             stack[h * groups + group, :, :LANES] = high
             stack[h * groups + group, :, LANES:] = rest
+
+
+def apply_kernel_matrix(out_pts, in_pts, values, result, left, right, stack):
+    outs, ins = left.shape[0], right.shape[1]
+    for start in range(0, outs, LANES):
+        piece = augmented(out_pts[:, start : start + LANES], True)
+        left[start : start + LANES] = piece.T.astype(BF16)
+    for start in range(0, ins, 256):
+        right[:, start : start + 256] = augmented(in_pts[:, start : start + 256], False).astype(BF16)
+    stack_values(values, stack)
     result[...] = jnp.zeros_like(result)
+    tile = min(512, outs // 2)
     pairs = ins // 256
 
     def step(index, carry):
         at = pl.multiple_of(lax.div(index, pairs) * tile, tile)
         pair = lax.rem(index, pairs)
         columns = right[:, pl.ds(pl.multiple_of(pair * 256, 256), 256)]
-        highs, lows = [], []
+        halves = []
         for h in range(2):
             lines = left[pl.ds(h * (outs // 2) + at, tile)]
-            kernel = jnp.exp(jnp.dot(lines, columns, preferred_element_type=F32))
-            high = kernel.astype(BF16)
-            highs.append(high)
-            lows.append((kernel - high.astype(F32)).astype(BF16))
+            halves.append(two_parts(jnp.exp(bf16_dot(lines, columns, 1, 0))))
         total = result[pl.ds(at, tile)]
         for a in range(2):
+            cut = slice(a * LANES, (a + 1) * LANES)
+            high, low = (
+                jnp.concatenate([halves[0][part][:, cut], halves[1][part][:, cut]], axis=1) for part in range(2)
+            )
             weights = stack[pair * 2 + a]
-            cut = slice(a * LANES, (a + 1) * LANES)
-            high = jnp.concatenate([highs[0][:, cut], highs[1][:, cut]], axis=1)
-            rest = jnp.concatenate([lows[0][:, cut], lows[1][:, cut]], axis=1)
-            both = jnp.dot(high, weights, preferred_element_type=F32)
+            both = bf16_dot(high, weights, 1, 0)
             total = total + both[:, :LANES] + both[:, LANES:]
-            total = total + jnp.dot(rest, weights[:, :LANES], preferred_element_type=F32)
+            total = total + bf16_dot(low, weights[:, :LANES], 1, 0)
         result[pl.ds(at, tile)] = total
         return carry
 
@@ -185,7 +189,7 @@
 
 
 def second_product_kernel(
-    place_ref, row_ref, col_ref, raw_ref, rhs_ref, noise_ref, out_ref, image_ref, left, right, stack, result, grams
+    row_ref, col_ref, raw_ref, rhs_ref, noise_ref, out_ref, image_ref, left, right, stack, result, grams
 ):
     rhs = rhs_ref[...]
     image = raw_ref[...] + noise_ref[...] * rhs
@@ -196,11 +200,14 @@
     grams[0:32] = folded(summed_halves(gram[:LANES, :LANES]))
     grams[32:64] = folded(summed_halves(gram[:LANES, LANES:]))
     grams[64:96] = folded(summed_halves(gram[LANES:, LANES:]))
-    lines = [grams[pl.ds(32 * m + place_ref[0], 1)] for m in range(3)]
-    tail = jnp.concatenate(lines + [jnp.zeros((5, LANES), F32)], axis=0)
+    own = lax.axis_index(COL)
+    lines = [grams[pl.ds(32 * m + own, 1)] for m in range(3)]
+    tail = jnp.concatenate(lines + [jnp.zeros((1, LANES), F32)], axis=0)
     for place in range(out_ref.shape[0]):
-        out_ref[place, :32] = result[place * 32 : place * 32 + 32]
-        out_ref[place, 32:] = tail
+        for quad in range(8):
+            start = place * 32 + quad * 4
+            out_ref[place, quad] = result[start : start + 4]
+        out_ref[place, 8] = tail
 
 
 def product_scratch(outs, ins):
@@ -232,21 +239,21 @@
     )(row_pts, col_pts, rhs)
 
 
-def second_product(place, row_pts, col_pts, raw, rhs, noise):
+def second_product(row_pts, col_pts, raw, rhs, noise):
     outs, ins = row_pts.shape[0] * 64, col_pts.shape[0] * 64
     return pl.pallas_call(
         second_product_kernel,
-        in_specs=[SMEM] + [VMEM] * 5,
+        in_specs=[VMEM] * 5,
         out_specs=[VMEM] * 2,
         out_shape=[
-            jax.ShapeDtypeStruct((row_pts.shape[0], 40, LANES), F32),
+            jax.ShapeDtypeStruct((row_pts.shape[0], 9, 4, LANES), F32),
             jax.ShapeDtypeStruct((ins // 2, LANES), F32),
         ],
         scratch_shapes=product_scratch(outs, ins) + [pltpu.VMEM((96, LANES), F32)],
         cost_estimate=product_cost(outs, ins),
         compiler_params=PARAMS,
         name="second_product",
-    )(place, row_pts, col_pts, raw, rhs, noise)
+    )(row_pts, col_pts, raw, rhs, noise)
 
 
 def two_parts(value):
@@ -357,9 +364,9 @@
     return [jnp.concatenate(tiles, axis=0)[:, HALF:] for tiles in state]
 
 
-def middle_kernel(core_ref, unit_ref, rhs_ref, image_ref, noise_ref, share_ref, second_ref, coef_ref, lines):
+def middle_kernel(unit_ref, rhs_ref, image_ref, noise_ref, share_ref, second_ref, coef_ref, lines):
     for place in range(unit_ref.shape[0]):
-        tail = unit_ref[place, 32:]
+        tail = unit_ref[place, 8]
         for m in range(3):
             lines[32 * m + place : 32 * m + place + 1] = tail[m : m + 1]
     gram, curv, square = (unfolded(lines[32 * m : 32 * m + 32]) for m in range(3))
@@ -370,7 +377,7 @@
     gram1 = gram - cross - cross.T + small_dot(coef0.T, small_dot(square, coef0))
     dcoef = small_dot(inverse, gram1)
     rhs, image = rhs_ref[...], image_ref[...]
-    raw = jnp.concatenate([unit_ref[i, :32] for i in range(unit_ref.shape[0])], axis=0)
+    raw = jnp.concatenate([unit_ref[i, quad] for i in range(unit_ref.shape[0]) for quad in range(8)], axis=0)
     second = raw + noise_ref[...] * (rhs - THETA * image)
     second_ref[...] = second
     scaled = coef0 * (1.0 / THETA)
@@ -397,7 +404,7 @@
     )
     lines[0:32] = folded(upper)
     lines[32:64] = folded(lower)
-    start = pl.multiple_of(core_ref[0] * 16, 16)
+    start = pl.multiple_of(lax.axis_index(COL[-1]) * 16, 16)
     part = jnp.concatenate([lines[pl.ds(32 * m + start, 16)] for m in range(2)], axis=0)
     for place in range(share_ref.shape[0]):
         share_ref[place] = part
@@ -405,10 +412,10 @@
     coef_ref[64:128] = jnp.concatenate([gram, eye], axis=1)
 
 
-def middle(core, units, rhs, image, noise, rows):
+def middle(units, rhs, image, noise, rows):
     return pl.pallas_call(
         middle_kernel,
-        in_specs=[SMEM] + [VMEM] * 4,
+        in_specs=[VMEM] * 4,
         out_specs=[VMEM] * 3,
         out_shape=[
             jax.ShapeDtypeStruct((rows, 32, LANES), F32),
@@ -418,7 +425,7 @@
         scratch_shapes=[pltpu.VMEM((96, LANES), F32)],
         compiler_params=PARAMS,
         name="middle",
-    )(core, units, rhs, image, noise)
+    )(units, rhs, image, noise)
 
 
 def final_kernel(lines_ref, coef_ref, rhs_ref, packed_ref, image_ref, second_ref, sol_ref, res_ref, norm_ref):
@@ -487,19 +494,16 @@
 
 def on_device(points, noise_level, right_sides):
     rows, cols = lax.axis_size("row"), lax.axis_size(COL)
-    col_index = lax.axis_index(COL)[None].astype(jnp.int32)
-    row_units, col_units = own_units(points, rows, cols)
+    row_units, col_units, rhs, noise = prepare(points, right_sides, noise_level, rows, cols)
+    col_pts = exchanged(col_units, COL)
     row_pts = exchanged(row_units, "row")
-    col_pts = exchanged(col_units, COL)
-    rhs, noise = packed_rows(right_sides, noise_level)
 
     part = first_product(row_pts, col_pts, rhs)
     own = jnp.sum(exchanged(part, "row"), axis=0)
     raw = shared(own, COL).reshape(-1, LANES)
-    part, image = second_product(col_index, row_pts, col_pts, raw, rhs, noise)
+    part, image = second_product(row_pts, col_pts, raw, rhs, noise)
     own = jnp.sum(exchanged(part, "row"), axis=0)
-    core = lax.axis_index(COL[-1])[None].astype(jnp.int32)
-    share, second, coefs = middle(core, shared(own, COL), rhs, image, noise, rows)
+    share, second, coefs = middle(shared(own, COL), rhs, image, noise, rows)
     lines = lax.all_gather(jnp.sum(exchanged(share, "row"), axis=0), COL[-1])
     sol, res, norms = final_outputs(lines, coefs, right_sides, rhs, image, second)
     return sol, res, norms[0]

time: 174 us -> 173 us (level)
  blocking collectives: 101 us -> 146 us
  starting transfers between devices: 24.3 us -> 0 us
  waiting for transfers between devices: 21.3 us -> 0 us
    all_to_all x5 -> x7, blocking collectives: 95.3 us -> 141 us  [exchanged(): return lax.all_to_all(parts, axis, 0, 0, tiled=True)]
    all_to_all x2 -> x0, starting transfers between devices: 24.3 us -> none  [exchanged(): return lax.all_to_all(parts, axis, 0, 0, tiled=True)]
    all_to_all x2 -> x0, waiting for transfers between devices: 21.3 us -> none  [exchanged(): return lax.all_to_all(parts, axis, 0, 0, tiled=True)]
    pallas_call x4 -> x3, Pallas kernels: 12.9 us -> 12.4 us  [the longest x1 6.01 us: second_product(): pl.pallas_call(second_product_kernel, in_specs=[VMEM] * 5, out_specs=[VME...]
  transfers between devices with their start and end apart: 2 -> 0, of which waited for: 2 -> 0; matrix products, arithmetic and copies ran while one was open for 0% -> 0% of each run, Pallas kernels for 0% -> 0%
where the time goes in v5:
time: 173 us; the launch traced here: 172 us
  blocking collectives  146 us (84%)
  Pallas kernels  22.8 us (13%)
  local copies, waits for them, and re-layouts  2.55 us (1%)
    all_to_all x7, blocking collectives, exchanged(): return lax.all_to_all(parts, axis, 0, 0, tiled=True)  141 us
    pallas_call x1, Pallas kernels, second_product(): pl.pallas_call(second_product_kernel, in_specs=[VMEM] * 5, out_specs=[VME...  6.01 us
    pallas_call x1, Pallas kernels, middle(): pl.pallas_call(middle_kernel, in_specs=[VMEM] * 4, out_specs=[VMEM] * 3,...  5.42 us
    all_gather x1, blocking collectives, on_device(): lines = lax.all_gather(jnp.sum(exchanged(share, 'row'), axis=0), COL[-1])  5.42 us
    pallas_call x1, Pallas kernels, first_product(): pl.pallas_call(first_product_kernel, in_specs=[VMEM] * 3, out_specs=VMEM,...  5.28 us
    pallas_call x1, Pallas kernels, final_outputs(): pl.pallas_call(final_kernel, in_specs=[VMEM] * 6, out_specs=[VMEM] * 3, o...  5.13 us

profile of v5, /device:TPU:1, one launch (start us, length us, event | category | flops | bytes accessed | tf_op | source)
XLA Modules:
  0.0 172.2 jit_solution(18201667901498112046)
XLA Ops:
  0.6 0.0 copy-start
  0.6 1.0 copy-done
  1.7 0.0 copy-start.2
  1.7 0.7 copy-done.2
  2.4 0.0 copy-start.3
  2.4 0.7 copy-done.3
  3.1 1.0 prepare.1
  4.1 16.9 %all_to_all.35.col_ref = f32[32,4,128]{2,1,0:T(4,128)S(1)} all-to-all(f32[32,4,128]{2,1,0:T(4,128)S(1)} %get-tuple-element.16), channel_id=1, replica_groups=mesh['row'=16,'col_0'=4,'col_1'=4,'col_2'=2] {'col_0','col_1','col_2'}, dimensions={0} | all-to-all | bytes 131072 | tf_op jit(solution)/shard_map/all_to_all | solution.py:488
  21.0 25.0 %all_to_all.36.row_ref = f32[16,4,128]{2,1,0:T(4,128)S(1)} all-to-all(f32[16,4,128]{2,1,0:T(4,128)S(1)} %get-tuple-element.15), channel_id=1, replica_groups=mesh['row'=16,'col_0'=4,'col_1'=4,'col_2'=2] {'row'}, dimensions={0} | all-to-all | bytes 65536 | tf_op jit(solution)/shard_map/all_to_all | solution.py:488
  46.0 5.3 %first_product.1 = f32[16,32,128]{2,1,0:T(8,128)S(1)} custom-call(f32[16,4,128]{2,1,0:T(4,128)S(1)} %all_to_all.36.row_ref, f32[32,4,128]{2,1,0:T(4,128)S(1)} %all_to_all.35.col_ref, f32[1024,128]{1,0:T(8,128)S(1)} %get-tuple-element.17.rhs_ref.packed_ref), custom_call_target="tpu_custom_call" | custom-call | flops 2147483648 | bytes 1572864 | tf_op jit(solution)/shard_map/first_product/pallas_call | solution.py:230
  51.3 15.3 %all_to_all.37 = f32[16,32,128]{2,1,0:T(8,128)S(1)} all-to-all(f32[16,32,128]{2,1,0:T(8,128)S(1)} %first_product.1), channel_id=1, replica_groups=mesh['row'=16,'col_0'=4,'col_1'=4,'col_2'=2] {'row'}, dimensions={0} | all-to-all | bytes 524288 | tf_op jit(solution)/shard_map/all_to_all | solution.py:488
  66.6 0.1 broadcast_in_dim.7
  66.7 21.5 %all_to_all.38 = f32[32,32,128]{2,1,0:T(8,128)S(1)} all-to-all(f32[32,32,128]{2,1,0:T(8,128)S(1)} %broadcast_in_dim.7), channel_id=1, replica_groups=mesh['row'=16,'col_0'=4,'col_1'=4,'col_2'=2] {'col_0','col_1','col_2'}, dimensions={0} | all-to-all | bytes 1048576 | tf_op jit(solution)/shard_map/all_to_all | solution.py:488
  88.2 6.0 %second_product.1 = (f32[16,9,4,128]{3,2,1,0:T(4,128)S(1)}, f32[1024,128]{1,0:T(8,128)S(1)}) custom-call(f32[16,4,128]{2,1,0:T(4,128)S(1)} %all_to_all.36.row_ref, f32[32,4,128]{2,1,0:T(4,128)S(1)} %all_to_all.35.col_ref, f32[1024,128]{1,0:T(8,128)S(1)} %bitcast.4, f32[1024,128]{1,0:T(8,128)S(1)} %get-tuple-element.17.rhs_ref.packed_ref, ...), custom_call_target="tpu_custom_call" | custom-call | flops 2147483648 | bytes 1572864 | tf_op jit(solution)/shard_map/second_product/pallas_call | solution.py:244
  94.2 21.2 %all_to_all.39 = f32[16,9,4,128]{3,2,1,0:T(4,128)S(1)} all-to-all(f32[16,9,4,128]{3,2,1,0:T(4,128)S(1)} %get-tuple-element.19), channel_id=1, replica_groups=mesh['row'=16,'col_0'=4,'col_1'=4,'col_2'=2] {'row'}, dimensions={0} | all-to-all | bytes 589824 | tf_op jit(solution)/shard_map/all_to_all | solution.py:488
  115.4 0.1 reduce_sum.28
  115.4 0.1 broadcast_in_dim.8
  115.5 19.9 %all_to_all.40.unit_ref = f32[32,9,4,128]{3,2,1,0:T(4,128)S(1)} all-to-all(f32[32,9,4,128]{3,2,1,0:T(4,128)S(1)} %broadcast_in_dim.8), channel_id=1, replica_groups=mesh['row'=16,'col_0'=4,'col_1'=4,'col_2'=2] {'col_0','col_1','col_2'}, dimensions={0} | all-to-all | bytes 1179648 | tf_op jit(solution)/shard_map/all_to_all | solution.py:488
  135.4 5.4 %middle.1 = (f32[16,32,128]{2,1,0:T(8,128)S(1)}, f32[1024,128]{1,0:T(8,128)S(1)}, f32[128,128]{1,0:T(8,128)S(1)}) custom-call(f32[32,9,4,128]{3,2,1,0:T(4,128)S(1)} %all_to_all.40.unit_ref, f32[1024,128]{1,0:T(8,128)S(1)} %get-tuple-element.17.rhs_ref.packed_ref, f32[1024,128]{1,0:T(8,128)S(1)} %get-tuple-element.20.image_ref, ...), custom_call_target="tpu_custom_call" | custom-call | tf_op jit(solution)/shard_map/middle/pallas_call | solution.py:416
  140.8 0.0 copy-start.1
  140.9 20.7 %all_to_all.41 = f32[16,32,128]{2,1,0:T(8,128)S(1)} all-to-all(f32[16,32,128]{2,1,0:T(8,128)S(1)} %get-tuple-element.21), channel_id=1, replica_groups=mesh['row'=16,'col_0'=4,'col_1'=4,'col_2'=2] {'row'}, dimensions={0} | all-to-all | bytes 524288 | tf_op jit(solution)/shard_map/all_to_all | solution.py:488
  161.6 5.4 %all-gather = f32[64,128]{1,0:T(8,128)S(1)} all-gather(f32[32,128]{1,0:T(8,128)S(1)} %reduce_sum.29), channel_id=2, replica_groups=mesh['row'=16,'col_0'=4,'col_1'=4,'col_2'=2] {'col_2'}, dimensions={0}, use_global_device_ids=true | all-gather | bytes 49152 | tf_op jit(solution)/shard_map/all_gather | solution.py:507
  167.0 0.0 copy-done.1
  167.0 5.1 %final_outputs.1 = (f32[64,2048]{1,0:T(8,128)}, f32[64,2048]{1,0:T(8,128)}, f32[1,64]{1,0:T(1,128)}) custom-call(f32[2,32,128]{2,1,0:T(8,128)S(1)} %bitcast.5, f32[128,128]{1,0:T(8,128)S(1)} %get-tuple-element.22.coef_ref, f32[64,2048]{1,0:T(8,128)S(1)} %copy-done.1, f32[1024,128]{1,0:T(8,128)S(1)} %get-tuple-element.17.rhs_ref.packed_ref, ...), custom_call_target="tpu_custom_call" | custom-call | tf_op jit(solution)/shard_map/final_outputs/pallas_call | solution.py:476
  (2 shorter events, 0.0 us)
Async XLA Ops:
  0.6 1.0 copy-start
  1.7 0.7 copy-start.2
  2.4 0.7 copy-start.3
  140.8 26.2 %copy-start.1 = (f32[64,2048]{1,0:T(8,128)S(1)}, f32[64,2048]{1,0:T(8,128)}, u32[]{:S(2)}) copy-start(f32[64,2048]{1,0:T(8,128)} %rhs_ref.1) | copy-start | bytes 1572868

commit v6 on v5

--- a/solution.py
+++ b/solution.py
@@ -26,61 +26,53 @@
     return jnp.concatenate([turned[:32], turned[32:64]], axis=1)
 
 
-def prepare_kernel(
-    pts_hbm, rhs_hbm, noise_hbm, row_out, col_out, packed_out, noise_out, pts_ref, rhs_ref, noise_ref, sems
-):
-    copies = [
-        pltpu.make_async_copy(source, target, sems.at[i])
-        for i, (source, target) in enumerate(((pts_hbm, pts_ref), (noise_hbm, noise_ref), (rhs_hbm, rhs_ref)))
-    ]
-    for copy in copies:
-        copy.start()
-    copies[0].wait()
+def own_kernel(pts_ref, row_out, col_out):
     unit = jnp.concatenate([pts_ref[:4], pts_ref[4:]], axis=1)
     for place in range(row_out.shape[0]):
         row_out[place] = unit
     for place in range(col_out.shape[0]):
         col_out[place] = unit
-    copies[1].wait()
+
+
+def own_units(points, rows, cols):
+    return pl.pallas_call(
+        own_kernel,
+        in_specs=[VMEM],
+        out_specs=[VMEM] * 2,
+        out_shape=[
+            jax.ShapeDtypeStruct((rows, 4, LANES), F32),
+            jax.ShapeDtypeStruct((cols, 4, LANES), F32),
+        ],
+        compiler_params=PARAMS,
+        name="own_units",
+    )(points)
+
+
+def prepare_kernel(rhs_ref, noise_ref, packed_out, noise_out):
     low = lane_of((32, LANES)) < HALF
     for tile in range(rhs_ref.shape[1] // LANES):
+        turned = rhs_ref[:, tile * LANES : (tile + 1) * LANES].T
         noise = noise_ref[:, tile * LANES : (tile + 1) * LANES]
         noise = jnp.broadcast_to(noise, (LANES, LANES)).T
         for part in range(2):
             rows = slice(tile * 64 + part * 32, tile * 64 + part * 32 + 32)
+            packed_out[rows] = packed(turned[part * 64 : part * 64 + 64])
             noise_out[rows] = jnp.where(
                 low, noise[part * 64 : part * 64 + 32], noise[part * 64 + 32 : part * 64 + 64]
             )
-    copies[2].wait()
-    for tile in range(rhs_ref.shape[1] // LANES):
-        turned = rhs_ref[:, tile * LANES : (tile + 1) * LANES].T
-        for part in range(2):
-            rows = slice(tile * 64 + part * 32, tile * 64 + part * 32 + 32)
-            packed_out[rows] = packed(turned[part * 64 : part * 64 + 64])
-
-
-def prepare(points, right_sides, noise_level, rows, cols):
-    lines = right_sides.shape[1] // 2
-    noise_row = noise_level[None, :]
+
+
+def prepare(right_sides, noise_level):
+    ins = right_sides.shape[1]
     return pl.pallas_call(
         prepare_kernel,
-        in_specs=[pl.BlockSpec(memory_space=pltpu.HBM)] * 3,
-        out_specs=[VMEM] * 4,
-        out_shape=[
-            jax.ShapeDtypeStruct((rows, 4, LANES), F32),
-            jax.ShapeDtypeStruct((cols, 4, LANES), F32),
-            jax.ShapeDtypeStruct((lines, LANES), F32),
-            jax.ShapeDtypeStruct((lines, LANES), F32),
-        ],
-        scratch_shapes=[
-            pltpu.VMEM(points.shape, F32),
-            pltpu.VMEM(right_sides.shape, F32),
-            pltpu.VMEM(noise_row.shape, F32),
-            pltpu.SemaphoreType.DMA((3,)),
-        ],
+        in_specs=[VMEM] * 2,
+        out_specs=[VMEM] * 2,
+        out_shape=[jax.ShapeDtypeStruct((ins // 2, LANES), F32)] * 2,
+        cost_estimate=pl.CostEstimate(flops=4 * 10**9, bytes_accessed=6 * 10**6, transcendentals=0),
         compiler_params=PARAMS,
         name="prepare",
-    )(points, right_sides, noise_row)
+    )(right_sides, noise_level[None, :])
 
 
 def ordered(ref):
@@ -146,14 +138,19 @@
             stack[h * groups + group, :, LANES:] = rest
 
 
-def apply_kernel_matrix(out_pts, in_pts, values, result, left, right, stack):
-    outs, ins = left.shape[0], right.shape[1]
-    for start in range(0, outs, LANES):
+def fill_left(out_pts, left):
+    for start in range(0, left.shape[0], LANES):
         piece = augmented(out_pts[:, start : start + LANES], True)
         left[start : start + LANES] = piece.T.astype(BF16)
-    for start in range(0, ins, 256):
+
+
+def fill_right(in_pts, right):
+    for start in range(0, right.shape[1], 256):
         right[:, start : start + 256] = augmented(in_pts[:, start : start + 256], False).astype(BF16)
-    stack_values(values, stack)
+
+
+def apply_kernel_matrix(left, right, stack, result):
+    outs, ins = left.shape[0], right.shape[1]
     result[...] = jnp.zeros_like(result)
     tile = min(512, outs // 2)
     pairs = ins // 256
@@ -183,7 +180,10 @@
 
 
 def first_product_kernel(row_ref, col_ref, rhs_ref, out_ref, left, right, stack, result):
-    apply_kernel_matrix(ordered(row_ref), ordered(col_ref), rhs_ref[...], result, left, right, stack)
+    fill_left(ordered(row_ref), left)
+    fill_right(ordered(col_ref), right)
+    stack_values(rhs_ref[...], stack)
+    apply_kernel_matrix(left, right, stack, result)
     for place in range(out_ref.shape[0]):
         out_ref[place] = result[place * 32 : place * 32 + 32]
 
@@ -194,8 +194,10 @@
     rhs = rhs_ref[...]
     image = raw_ref[...] + noise_ref[...] * rhs
     image_ref[...] = image
-    values = rhs - THETA * image
-    apply_kernel_matrix(ordered(row_ref), ordered(col_ref), values, result, left, right, stack)
+    fill_left(ordered(row_ref), left)
+    fill_right(ordered(col_ref), right)
+    stack_values(rhs - THETA * image, stack)
+    apply_kernel_matrix(left, right, stack, result)
     gram = gram_of(joined(two_parts(rhs), two_parts(image)))
     grams[0:32] = folded(summed_halves(gram[:LANES, :LANES]))
     grams[32:64] = folded(summed_halves(gram[:LANES, LANES:]))
@@ -210,6 +212,12 @@
         out_ref[place, 8] = tail
 
 
+def product_cost(outs, ins):
+    return pl.CostEstimate(
+        flops=2 * outs * ins * 512, bytes_accessed=8 * (outs + ins) * HALF, transcendentals=outs * ins
+    )
+
+
 def product_scratch(outs, ins):
     return [
         pltpu.VMEM((outs, LANES), BF16),
@@ -217,12 +225,6 @@
         pltpu.VMEM((ins // LANES, 256, 256), BF16),
         pltpu.VMEM((outs // 2, LANES), F32),
     ]
-
-
-def product_cost(outs, ins):
-    return pl.CostEstimate(
-        flops=2 * outs * ins * 512, bytes_accessed=8 * (outs + ins) * HALF, transcendentals=outs * ins
-    )
 
 
 def first_product(row_pts, col_pts, rhs):
@@ -494,9 +496,10 @@
 
 def on_device(points, noise_level, right_sides):
     rows, cols = lax.axis_size("row"), lax.axis_size(COL)
-    row_units, col_units, rhs, noise = prepare(points, right_sides, noise_level, rows, cols)
+    row_units, col_units = own_units(points, rows, cols)
     col_pts = exchanged(col_units, COL)
     row_pts = exchanged(row_units, "row")
+    rhs, noise = prepare(right_sides, noise_level)
 
     part = first_product(row_pts, col_pts, rhs)
     own = jnp.sum(exchanged(part, "row"), axis=0)

time: 173 us -> 171 us (0.988)
  blocking collectives: 146 us -> 121 us
  starting transfers between devices: 0 us -> 13.9 us
  waiting for transfers between devices: 0 us -> 9.64 us
    all_to_all x7 -> x6, blocking collectives: 141 us -> 115 us  [exchanged(): return lax.all_to_all(parts, axis, 0, 0, tiled=True)]
    all_to_all x0 -> x1, starting transfers between devices: none -> 13.9 us  [exchanged(): return lax.all_to_all(parts, axis, 0, 0, tiled=True)]
    all_to_all x0 -> x1, waiting for transfers between devices: none -> 9.64 us  [exchanged(): return lax.all_to_all(parts, axis, 0, 0, tiled=True)]
  transfers between devices with their start and end apart: 0 -> 1, of which waited for: 0 -> 1; matrix products, arithmetic and copies ran while one was open for 0% -> 0% of each run, Pallas kernels for 0% -> 0%
where the time goes in v6:
time: 171 us
  blocking collectives  121 us (71%)
  Pallas kernels  23.4 us (14%)
  starting transfers between devices  13.9 us (8%)
  waiting for transfers between devices  9.64 us (6%)
  local copies, waits for them, and re-layouts  1.85 us (1%)
    all_to_all x6, blocking collectives, exchanged(): return lax.all_to_all(parts, axis, 0, 0, tiled=True)  115 us
    all_to_all x1, starting transfers between devices, exchanged(): return lax.all_to_all(parts, axis, 0, 0, tiled=True)  13.9 us
    all_to_all x1, waiting for transfers between devices, exchanged(): return lax.all_to_all(parts, axis, 0, 0, tiled=True)  9.64 us
    pallas_call x1, Pallas kernels, second_product(): pl.pallas_call(second_product_kernel, in_specs=[VMEM] * 5, out_specs=[VME...  6.08 us
    all_gather x1, blocking collectives, on_device(): lines = lax.all_gather(jnp.sum(exchanged(share, 'row'), axis=0), COL[-1])  5.74 us
    pallas_call x1, Pallas kernels, middle(): pl.pallas_call(middle_kernel, in_specs=[VMEM] * 4, out_specs=[VMEM] * 3,...  5.41 us
    pallas_call x1, Pallas kernels, first_product(): pl.pallas_call(first_product_kernel, in_specs=[VMEM] * 3, out_specs=VMEM,...  5.35 us
    pallas_call x1, Pallas kernels, final_outputs(): pl.pallas_call(final_kernel, in_specs=[VMEM] * 6, out_specs=[VMEM] * 3, o...  5.13 us
  transfers between devices with their start and end apart: 1, of which 1 were waited for; matrix products, arithmetic and copies ran while one was open for 0% of the time, Pallas kernels for 0%

profile of v6, /device:TPU:1, one launch (start us, length us, event | category | flops | bytes accessed | tf_op | source)
XLA Modules:
  0.0 170.6 jit_solution(13742171707435994459)
XLA Ops:
  0.6 0.0 copy-start.2
  0.6 0.7 copy-done.2
  1.3 0.7 own_units.1
  2.0 16.9 %all_to_all.35.col_ref = f32[32,4,128]{2,1,0:T(4,128)S(1)} all-to-all(f32[32,4,128]{2,1,0:T(4,128)S(1)} %get-tuple-element.16), channel_id=1, replica_groups=mesh['row'=16,'col_0'=4,'col_1'=4,'col_2'=2] {'col_0','col_1','col_2'}, dimensions={0} | all-to-all | bytes 131072 | tf_op jit(solution)/shard_map/all_to_all | solution.py:490
  18.9 0.0 copy-start.3
  18.9 13.9 %all-to-all-start = ((f32[16,4,128]{2,1,0:T(4,128)}), f32[16,4,128]{2,1,0:T(4,128)S(1)}, u32[]{:S(2)}, u32[]{:S(2)}) async-start(f32[16,4,128]{2,1,0:T(4,128)} %get-tuple-element.15), calls=%async_computation | async-start | bytes 65536 | tf_op jit(solution)/shard_map/all_to_all | solution.py:490
  32.8 0.0 copy-done.3
  32.8 0.0 copy-start
  32.8 1.0 copy-done
  33.9 0.8 prepare.1
  34.6 9.6 %all-to-all-done.row_ref = f32[16,4,128]{2,1,0:T(4,128)S(1)} async-done(((f32[16,4,128]{2,1,0:T(4,128)}), f32[16,4,128]{2,1,0:T(4,128)S(1)}, u32[]{:S(2)}, u32[]{:S(2)}) %all-to-all-start) | async-done | bytes 32800 | tf_op jit(solution)/shard_map/all_to_all | solution.py:490
  44.3 5.3 %first_product.1 = f32[16,32,128]{2,1,0:T(8,128)S(1)} custom-call(f32[16,4,128]{2,1,0:T(4,128)S(1)} %all-to-all-done.row_ref, f32[32,4,128]{2,1,0:T(4,128)S(1)} %all_to_all.35.col_ref, f32[1024,128]{1,0:T(8,128)S(1)} %get-tuple-element.17.rhs_ref.packed_ref), custom_call_target="tpu_custom_call" | custom-call | flops 2147483648 | bytes 1572864 | tf_op jit(solution)/shard_map/first_product/pallas_call | solution.py:232
  49.6 15.3 %all_to_all.36 = f32[16,32,128]{2,1,0:T(8,128)S(1)} all-to-all(f32[16,32,128]{2,1,0:T(8,128)S(1)} %first_product.1), channel_id=1, replica_groups=mesh['row'=16,'col_0'=4,'col_1'=4,'col_2'=2] {'row'}, dimensions={0} | all-to-all | bytes 524288 | tf_op jit(solution)/shard_map/all_to_all | solution.py:490
  65.0 0.1 broadcast_in_dim.7
  65.1 21.5 %all_to_all.37 = f32[32,32,128]{2,1,0:T(8,128)S(1)} all-to-all(f32[32,32,128]{2,1,0:T(8,128)S(1)} %broadcast_in_dim.7), channel_id=1, replica_groups=mesh['row'=16,'col_0'=4,'col_1'=4,'col_2'=2] {'col_0','col_1','col_2'}, dimensions={0} | all-to-all | bytes 1048576 | tf_op jit(solution)/shard_map/all_to_all | solution.py:490
  86.5 6.1 %second_product.1 = (f32[16,9,4,128]{3,2,1,0:T(4,128)S(1)}, f32[1024,128]{1,0:T(8,128)S(1)}) custom-call(f32[16,4,128]{2,1,0:T(4,128)S(1)} %all-to-all-done.row_ref, f32[32,4,128]{2,1,0:T(4,128)S(1)} %all_to_all.35.col_ref, f32[1024,128]{1,0:T(8,128)S(1)} %bitcast.4, f32[1024,128]{1,0:T(8,128)S(1)} %get-tuple-element.17.rhs_ref.packed_ref, ...), custom_call_target="tpu_custom_call" | custom-call | flops 2147483648 | bytes 1572864 | tf_op jit(solution)/shard_map/second_product/pallas_call | solution.py:246
  92.6 21.2 %all_to_all.38 = f32[16,9,4,128]{3,2,1,0:T(4,128)S(1)} all-to-all(f32[16,9,4,128]{3,2,1,0:T(4,128)S(1)} %get-tuple-element.19), channel_id=1, replica_groups=mesh['row'=16,'col_0'=4,'col_1'=4,'col_2'=2] {'row'}, dimensions={0} | all-to-all | bytes 589824 | tf_op jit(solution)/shard_map/all_to_all | solution.py:490
  113.8 0.1 reduce_sum.28
  113.9 0.1 broadcast_in_dim.8
  114.0 19.9 %all_to_all.39.unit_ref = f32[32,9,4,128]{3,2,1,0:T(4,128)S(1)} all-to-all(f32[32,9,4,128]{3,2,1,0:T(4,128)S(1)} %broadcast_in_dim.8), channel_id=1, replica_groups=mesh['row'=16,'col_0'=4,'col_1'=4,'col_2'=2] {'col_0','col_1','col_2'}, dimensions={0} | all-to-all | bytes 1179648 | tf_op jit(solution)/shard_map/all_to_all | solution.py:490
  133.9 5.4 %middle.1 = (f32[16,32,128]{2,1,0:T(8,128)S(1)}, f32[1024,128]{1,0:T(8,128)S(1)}, f32[128,128]{1,0:T(8,128)S(1)}) custom-call(f32[32,9,4,128]{3,2,1,0:T(4,128)S(1)} %all_to_all.39.unit_ref, f32[1024,128]{1,0:T(8,128)S(1)} %get-tuple-element.17.rhs_ref.packed_ref, f32[1024,128]{1,0:T(8,128)S(1)} %get-tuple-element.20.image_ref, ...), custom_call_target="tpu_custom_call" | custom-call | tf_op jit(solution)/shard_map/middle/pallas_call | solution.py:418
  139.3 0.0 copy-start.1
  139.3 20.4 %all_to_all.40 = f32[16,32,128]{2,1,0:T(8,128)S(1)} all-to-all(f32[16,32,128]{2,1,0:T(8,128)S(1)} %get-tuple-element.21), channel_id=1, replica_groups=mesh['row'=16,'col_0'=4,'col_1'=4,'col_2'=2] {'row'}, dimensions={0} | all-to-all | bytes 524288 | tf_op jit(solution)/shard_map/all_to_all | solution.py:490
  159.7 5.7 %all-gather = f32[64,128]{1,0:T(8,128)S(1)} all-gather(f32[32,128]{1,0:T(8,128)S(1)} %reduce_sum.29), channel_id=2, replica_groups=mesh['row'=16,'col_0'=4,'col_1'=4,'col_2'=2] {'col_2'}, dimensions={0}, use_global_device_ids=true | all-gather | bytes 49152 | tf_op jit(solution)/shard_map/all_gather | solution.py:510
  165.4 0.0 copy-done.1
  165.4 5.1 %final_outputs.1 = (f32[64,2048]{1,0:T(8,128)}, f32[64,2048]{1,0:T(8,128)}, f32[1,64]{1,0:T(1,128)}) custom-call(f32[2,32,128]{2,1,0:T(8,128)S(1)} %bitcast.5, f32[128,128]{1,0:T(8,128)S(1)} %get-tuple-element.22.coef_ref, f32[64,2048]{1,0:T(8,128)S(1)} %copy-done.1, f32[1024,128]{1,0:T(8,128)S(1)} %get-tuple-element.17.rhs_ref.packed_ref, ...), custom_call_target="tpu_custom_call" | custom-call | tf_op jit(solution)/shard_map/final_outputs/pallas_call | solution.py:478
  (2 shorter events, 0.0 us)
Async XLA Ops:
  0.6 0.7 copy-start.2
  18.9 13.9 %copy-start.3 = (f32[2048]{0:T(1024)S(1)}, f32[2048]{0:T(1024)}, u32[]{:S(2)}) copy-start(f32[2048]{0:T(1024)} %param.4) | copy-start | bytes 24580
  18.9 25.3 %all-to-all-start = ((f32[16,4,128]{2,1,0:T(4,128)}), f32[16,4,128]{2,1,0:T(4,128)S(1)}, u32[]{:S(2)}, u32[]{:S(2)}) async-start(f32[16,4,128]{2,1,0:T(4,128)} %get-tuple-element.15), calls=%async_computation | async-start | bytes 65536 | tf_op jit(solution)/shard_map/all_to_all | solution.py:490
  32.8 1.0 copy-start
  139.3 26.2 %copy-start.1 = (f32[64,2048]{1,0:T(8,128)S(1)}, f32[64,2048]{1,0:T(8,128)}, u32[]{:S(2)}) copy-start(f32[64,2048]{1,0:T(8,128)} %rhs_ref.3) | copy-start | bytes 1572868

commit v7 on v6

--- a/solution.py
+++ b/solution.py
@@ -26,26 +26,9 @@
     return jnp.concatenate([turned[:32], turned[32:64]], axis=1)
 
 
-def own_kernel(pts_ref, row_out, col_out):
-    unit = jnp.concatenate([pts_ref[:4], pts_ref[4:]], axis=1)
-    for place in range(row_out.shape[0]):
-        row_out[place] = unit
-    for place in range(col_out.shape[0]):
-        col_out[place] = unit
-
-
 def own_units(points, rows, cols):
-    return pl.pallas_call(
-        own_kernel,
-        in_specs=[VMEM],
-        out_specs=[VMEM] * 2,
-        out_shape=[
-            jax.ShapeDtypeStruct((rows, 4, LANES), F32),
-            jax.ShapeDtypeStruct((cols, 4, LANES), F32),
-        ],
-        compiler_params=PARAMS,
-        name="own_units",
-    )(points)
+    unit = jnp.concatenate([points[:4], points[4:]], axis=1)
+    return (jnp.broadcast_to(unit[None], (count, 4, LANES)) for count in (rows, cols))
 
 
 def prepare_kernel(rhs_ref, noise_ref, packed_out, noise_out):
@@ -176,7 +159,7 @@
         result[pl.ds(at, tile)] = total
         return carry
 
-    lax.fori_loop(0, (outs // 2 // tile) * pairs, step, 0)
+    lax.fori_loop(0, (outs // 2 // tile) * pairs, step, 0, unroll=8)
 
 
 def first_product_kernel(row_ref, col_ref, rhs_ref, out_ref, left, right, stack, result):
@@ -341,13 +324,13 @@
 
     def step(group, state):
         state = [list(tiles) for tiles in state]
-        for quad in range(2):
-            lanes = [jnp.full((8, LANES), group * 8 + quad * 4 + j, jnp.int32) for j in range(4)]
+        for quad in range(1):
+            lanes = [jnp.full((8, LANES), group * 8 + j, jnp.int32) for j in range(8)]
             spread = [
                 [[jnp.take_along_axis(tile, lane, axis=1) for tile in tiles] for lane in lanes] for tiles in state
             ]
-            for j in range(4):
-                at = quad * 4 + j
+            for j in range(8):
+                at = j
                 here = sub == at
                 for tiles, columns in zip(state, spread):
                     inverse = 1.0 / line(columns[j][0], at)
@@ -355,7 +338,7 @@
                     for t in range(8):
                         new = tiles[t] - columns[j][t] * row
                         tiles[t] = jnp.where(here, row, new) if t == 0 else new
-                    for later in range(j + 1, 4):
+                    for later in range(j + 1, 8):
                         ratio = line(columns[later][0], at) * inverse
                         for t in range(8):
                             new = columns[later][t] - columns[j][t] * ratio

time: 171 us -> 168 us (0.982)
  Pallas kernels: 23.4 us -> 19.3 us
where the time goes in v7:
time: 168 us; the launch traced here: 167 us
  blocking collectives  121 us (72%)
  Pallas kernels  19.3 us (11%)
  starting transfers between devices  13.9 us (8%)
  waiting for transfers between devices  9.64 us (6%)
  local copies, waits for them, and re-layouts  2.57 us (2%)
    all_to_all x6, blocking collectives, exchanged(): return lax.all_to_all(parts, axis, 0, 0, tiled=True)  116 us
    all_to_all x1, starting transfers between devices, exchanged(): return lax.all_to_all(parts, axis, 0, 0, tiled=True)  13.9 us
    all_to_all x1, waiting for transfers between devices, exchanged(): return lax.all_to_all(parts, axis, 0, 0, tiled=True)  9.64 us
    all_gather x1, blocking collectives, on_device(): lines = lax.all_gather(jnp.sum(exchanged(share, 'row'), axis=0), COL[-1])  5.44 us
    pallas_call x1, Pallas kernels, middle(): pl.pallas_call(middle_kernel, in_specs=[VMEM] * 4, out_specs=[VMEM] * 3,...  5.22 us
    pallas_call x1, Pallas kernels, final_outputs(): pl.pallas_call(final_kernel, in_specs=[VMEM] * 6, out_specs=[VMEM] * 3, o...  4.77 us
    pallas_call x1, Pallas kernels, second_product(): pl.pallas_call(second_product_kernel, in_specs=[VMEM] * 5, out_specs=[VME...  4.58 us
    pallas_call x1, Pallas kernels, first_product(): pl.pallas_call(first_product_kernel, in_specs=[VMEM] * 3, out_specs=VMEM,...  3.99 us
  transfers between devices with their start and end apart: 1, of which 1 were waited for; matrix products, arithmetic and copies ran while one was open for 0% of the time, Pallas kernels for 0%

profile of v7, /device:TPU:1, one launch (start us, length us, event | category | flops | bytes accessed | tf_op | source)
XLA Modules:
  0.0 167.3 jit_solution(16794034572786165551)
XLA Ops:
  0.6 0.8 fusion
  1.4 0.1 pad_maximum_fusion
  1.5 16.9 %all_to_all.35.col_ref = f32[32,4,128]{2,1,0:T(4,128)S(1)} all-to-all(f32[32,4,128]{2,1,0:T(4,128)S(1)} %broadcast_in_dim.11), channel_id=1, replica_groups=mesh['row'=16,'col_0'=4,'col_1'=4,'col_2'=2] {'col_0','col_1','col_2'}, dimensions={0} | all-to-all | bytes 131072 | tf_op jit(solution)/shard_map/all_to_all | solution.py:473
  18.4 0.6 broadcast_in_dim.10
  19.0 0.0 copy-start.2
  19.0 13.9 %all-to-all-start = ((f32[16,4,128]{2,1,0:T(4,128)}), f32[16,4,128]{2,1,0:T(4,128)S(1)}, u32[]{:S(2)}, u32[]{:S(2)}) async-start(f32[16,4,128]{2,1,0:T(4,128)} %broadcast_in_dim.10), calls=%async_computation | async-start | bytes 65536 | tf_op jit(solution)/shard_map/all_to_all | solution.py:473
  32.9 0.0 copy-done.2
  32.9 0.0 copy-start
  32.9 1.0 copy-done
  34.0 0.8 prepare.1
  34.7 9.6 %all-to-all-done.row_ref = f32[16,4,128]{2,1,0:T(4,128)S(1)} async-done(((f32[16,4,128]{2,1,0:T(4,128)}), f32[16,4,128]{2,1,0:T(4,128)S(1)}, u32[]{:S(2)}, u32[]{:S(2)}) %all-to-all-start) | async-done | bytes 32800 | tf_op jit(solution)/shard_map/all_to_all | solution.py:473
  44.4 4.0 %first_product.1 = f32[16,32,128]{2,1,0:T(8,128)S(1)} custom-call(f32[16,4,128]{2,1,0:T(4,128)S(1)} %all-to-all-done.row_ref, f32[32,4,128]{2,1,0:T(4,128)S(1)} %all_to_all.35.col_ref, f32[1024,128]{1,0:T(8,128)S(1)} %get-tuple-element.13.rhs_ref.packed_ref), custom_call_target="tpu_custom_call" | custom-call | flops 2147483648 | bytes 1572864 | tf_op jit(solution)/shard_map/first_product/pallas_call | solution.py:215
  48.4 15.3 %all_to_all.36 = f32[16,32,128]{2,1,0:T(8,128)S(1)} all-to-all(f32[16,32,128]{2,1,0:T(8,128)S(1)} %first_product.1), channel_id=1, replica_groups=mesh['row'=16,'col_0'=4,'col_1'=4,'col_2'=2] {'row'}, dimensions={0} | all-to-all | bytes 524288 | tf_op jit(solution)/shard_map/all_to_all | solution.py:473
  63.7 0.1 broadcast_in_dim.13
  63.8 21.5 %all_to_all.37 = f32[32,32,128]{2,1,0:T(8,128)S(1)} all-to-all(f32[32,32,128]{2,1,0:T(8,128)S(1)} %broadcast_in_dim.13), channel_id=1, replica_groups=mesh['row'=16,'col_0'=4,'col_1'=4,'col_2'=2] {'col_0','col_1','col_2'}, dimensions={0} | all-to-all | bytes 1048576 | tf_op jit(solution)/shard_map/all_to_all | solution.py:473
  85.3 4.6 %second_product.1 = (f32[16,9,4,128]{3,2,1,0:T(4,128)S(1)}, f32[1024,128]{1,0:T(8,128)S(1)}) custom-call(f32[16,4,128]{2,1,0:T(4,128)S(1)} %all-to-all-done.row_ref, f32[32,4,128]{2,1,0:T(4,128)S(1)} %all_to_all.35.col_ref, f32[1024,128]{1,0:T(8,128)S(1)} %bitcast.4, f32[1024,128]{1,0:T(8,128)S(1)} %get-tuple-element.13.rhs_ref.packed_ref, ...), custom_call_target="tpu_custom_call" | custom-call | flops 2147483648 | bytes 1572864 | tf_op jit(solution)/shard_map/second_product/pallas_call | solution.py:229
  89.9 21.2 %all_to_all.38 = f32[16,9,4,128]{3,2,1,0:T(4,128)S(1)} all-to-all(f32[16,9,4,128]{3,2,1,0:T(4,128)S(1)} %get-tuple-element.15), channel_id=1, replica_groups=mesh['row'=16,'col_0'=4,'col_1'=4,'col_2'=2] {'row'}, dimensions={0} | all-to-all | bytes 589824 | tf_op jit(solution)/shard_map/all_to_all | solution.py:473
  111.1 0.1 reduce_sum.28
  111.1 0.1 broadcast_in_dim.14
  111.2 19.9 %all_to_all.39.unit_ref = f32[32,9,4,128]{3,2,1,0:T(4,128)S(1)} all-to-all(f32[32,9,4,128]{3,2,1,0:T(4,128)S(1)} %broadcast_in_dim.14), channel_id=1, replica_groups=mesh['row'=16,'col_0'=4,'col_1'=4,'col_2'=2] {'col_0','col_1','col_2'}, dimensions={0} | all-to-all | bytes 1179648 | tf_op jit(solution)/shard_map/all_to_all | solution.py:473
  131.1 5.2 %middle.1 = (f32[16,32,128]{2,1,0:T(8,128)S(1)}, f32[1024,128]{1,0:T(8,128)S(1)}, f32[128,128]{1,0:T(8,128)S(1)}) custom-call(f32[32,9,4,128]{3,2,1,0:T(4,128)S(1)} %all_to_all.39.unit_ref, f32[1024,128]{1,0:T(8,128)S(1)} %get-tuple-element.13.rhs_ref.packed_ref, f32[1024,128]{1,0:T(8,128)S(1)} %get-tuple-element.16.image_ref, ...), custom_call_target="tpu_custom_call" | custom-call | tf_op jit(solution)/shard_map/middle/pallas_call | solution.py:401
  136.3 0.0 copy-start.1
  136.3 20.7 %all_to_all.40 = f32[16,32,128]{2,1,0:T(8,128)S(1)} all-to-all(f32[16,32,128]{2,1,0:T(8,128)S(1)} %get-tuple-element.17), channel_id=1, replica_groups=mesh['row'=16,'col_0'=4,'col_1'=4,'col_2'=2] {'row'}, dimensions={0} | all-to-all | bytes 524288 | tf_op jit(solution)/shard_map/all_to_all | solution.py:473
  157.1 5.4 %all-gather = f32[64,128]{1,0:T(8,128)S(1)} all-gather(f32[32,128]{1,0:T(8,128)S(1)} %reduce_sum.29), channel_id=2, replica_groups=mesh['row'=16,'col_0'=4,'col_1'=4,'col_2'=2] {'col_2'}, dimensions={0}, use_global_device_ids=true | all-gather | bytes 49152 | tf_op jit(solution)/shard_map/all_gather | solution.py:493
  162.5 0.0 copy-done.1
  162.5 4.8 %final_outputs.1 = (f32[64,2048]{1,0:T(8,128)}, f32[64,2048]{1,0:T(8,128)}, f32[1,64]{1,0:T(1,128)}) custom-call(f32[2,32,128]{2,1,0:T(8,128)S(1)} %bitcast.5, f32[128,128]{1,0:T(8,128)S(1)} %get-tuple-element.18.coef_ref, f32[64,2048]{1,0:T(8,128)S(1)} %copy-done.1, f32[1024,128]{1,0:T(8,128)S(1)} %get-tuple-element.13.rhs_ref.packed_ref, ...), custom_call_target="tpu_custom_call" | custom-call | tf_op jit(solution)/shard_map/final_outputs/pallas_call | solution.py:461
  (3 shorter events, 0.1 us)
Async XLA Ops:
  19.0 13.9 %copy-start.2 = (f32[2048]{0:T(1024)S(1)}, f32[2048]{0:T(1024)}, u32[]{:S(2)}) copy-start(f32[2048]{0:T(1024)} %param.4) | copy-start | bytes 24580
  19.0 25.3 %all-to-all-start = ((f32[16,4,128]{2,1,0:T(4,128)}), f32[16,4,128]{2,1,0:T(4,128)S(1)}, u32[]{:S(2)}, u32[]{:S(2)}) async-start(f32[16,4,128]{2,1,0:T(4,128)} %broadcast_in_dim.10), calls=%async_computation | async-start | bytes 65536 | tf_op jit(solution)/shard_map/all_to_all | solution.py:473
  32.9 1.0 copy-start
  136.3 26.2 %copy-start.1 = (f32[64,2048]{1,0:T(8,128)S(1)}, f32[64,2048]{1,0:T(8,128)}, u32[]{:S(2)}) copy-start(f32[64,2048]{1,0:T(8,128)} %rhs_ref.3) | copy-start | bytes 1572868

commit v8 on v7

--- a/solution.py
+++ b/solution.py
@@ -380,12 +380,12 @@
     change = parts_dot(joined(rhs_parts, image_parts), two_parts(mix))
     direction, residual = rhs + change[:, :LANES], rhs + change[:, LANES:]
     image1 = two_parts(parts_dot(joined(image_parts, two_parts(second)), two_parts(mix1)))
-    crossed = parts_dot(joined(two_parts(direction), image1), image1, 0, 0)
-    curv1 = summed_halves(crossed[:LANES])
+    crossed = parts_dot(image1, joined(two_parts(direction), image1), 0, 0)
+    curv1 = summed_halves(crossed[:, :LANES])
     upper, lower = squares_of(
         0.5 * (curv1 + curv1.T),
         summed_halves(gram_of(two_parts(residual))),
-        summed_halves(crossed[LANES:]),
+        summed_halves(crossed[:, LANES:]),
     )
     lines[0:32] = folded(upper)
     lines[32:64] = folded(lower)

time: 168 us -> 168 us (level)
  no operation moved by 1% of the time
where the time goes in v8:
time: 168 us; the launch traced here: 167 us
  blocking collectives  121 us (72%)
  Pallas kernels  19.2 us (11%)
  starting transfers between devices  13.9 us (8%)
  waiting for transfers between devices  9.64 us (6%)
  local copies, waits for them, and re-layouts  2.57 us (2%)
    all_to_all x6, blocking collectives, exchanged(): return lax.all_to_all(parts, axis, 0, 0, tiled=True)  116 us
    all_to_all x1, starting transfers between devices, exchanged(): return lax.all_to_all(parts, axis, 0, 0, tiled=True)  13.9 us
    all_to_all x1, waiting for transfers between devices, exchanged(): return lax.all_to_all(parts, axis, 0, 0, tiled=True)  9.64 us
    all_gather x1, blocking collectives, on_device(): lines = lax.all_gather(jnp.sum(exchanged(share, 'row'), axis=0), COL[-1])  5.42 us
    pallas_call x1, Pallas kernels, middle(): pl.pallas_call(middle_kernel, in_specs=[VMEM] * 4, out_specs=[VMEM] * 3,...  5.1 us
    pallas_call x1, Pallas kernels, final_outputs(): pl.pallas_call(final_kernel, in_specs=[VMEM] * 6, out_specs=[VMEM] * 3, o...  4.77 us
    pallas_call x1, Pallas kernels, second_product(): pl.pallas_call(second_product_kernel, in_specs=[VMEM] * 5, out_specs=[VME...  4.58 us
    pallas_call x1, Pallas kernels, first_product(): pl.pallas_call(first_product_kernel, in_specs=[VMEM] * 3, out_specs=VMEM,...  3.99 us
  transfers between devices with their start and end apart: 1, of which 1 were waited for; matrix products, arithmetic and copies ran while one was open for 0% of the time, Pallas kernels for 0%

profile of v8, /device:TPU:1, one launch (start us, length us, event | category | flops | bytes accessed | tf_op | source)
XLA Modules:
  0.0 167.2 jit_solution(9798018529470305795)
XLA Ops:
  0.6 0.8 fusion
  1.4 0.1 pad_maximum_fusion
  1.5 16.9 %all_to_all.35.col_ref = f32[32,4,128]{2,1,0:T(4,128)S(1)} all-to-all(f32[32,4,128]{2,1,0:T(4,128)S(1)} %broadcast_in_dim.11), channel_id=1, replica_groups=mesh['row'=16,'col_0'=4,'col_1'=4,'col_2'=2] {'col_0','col_1','col_2'}, dimensions={0} | all-to-all | bytes 131072 | tf_op jit(solution)/shard_map/all_to_all | solution.py:473
  18.4 0.6 broadcast_in_dim.10
  19.0 0.0 copy-start.2
  19.0 13.9 %all-to-all-start = ((f32[16,4,128]{2,1,0:T(4,128)}), f32[16,4,128]{2,1,0:T(4,128)S(1)}, u32[]{:S(2)}, u32[]{:S(2)}) async-start(f32[16,4,128]{2,1,0:T(4,128)} %broadcast_in_dim.10), calls=%async_computation | async-start | bytes 65536 | tf_op jit(solution)/shard_map/all_to_all | solution.py:473
  32.9 0.0 copy-done.2
  32.9 0.0 copy-start
  32.9 1.0 copy-done
  34.0 0.8 prepare.1
  34.7 9.6 %all-to-all-done.row_ref = f32[16,4,128]{2,1,0:T(4,128)S(1)} async-done(((f32[16,4,128]{2,1,0:T(4,128)}), f32[16,4,128]{2,1,0:T(4,128)S(1)}, u32[]{:S(2)}, u32[]{:S(2)}) %all-to-all-start) | async-done | bytes 32800 | tf_op jit(solution)/shard_map/all_to_all | solution.py:473
  44.4 4.0 %first_product.1 = f32[16,32,128]{2,1,0:T(8,128)S(1)} custom-call(f32[16,4,128]{2,1,0:T(4,128)S(1)} %all-to-all-done.row_ref, f32[32,4,128]{2,1,0:T(4,128)S(1)} %all_to_all.35.col_ref, f32[1024,128]{1,0:T(8,128)S(1)} %get-tuple-element.13.rhs_ref.packed_ref), custom_call_target="tpu_custom_call" | custom-call | flops 2147483648 | bytes 1572864 | tf_op jit(solution)/shard_map/first_product/pallas_call | solution.py:215
  48.4 15.3 %all_to_all.36 = f32[16,32,128]{2,1,0:T(8,128)S(1)} all-to-all(f32[16,32,128]{2,1,0:T(8,128)S(1)} %first_product.1), channel_id=1, replica_groups=mesh['row'=16,'col_0'=4,'col_1'=4,'col_2'=2] {'row'}, dimensions={0} | all-to-all | bytes 524288 | tf_op jit(solution)/shard_map/all_to_all | solution.py:473
  63.7 0.1 broadcast_in_dim.13
  63.8 21.5 %all_to_all.37 = f32[32,32,128]{2,1,0:T(8,128)S(1)} all-to-all(f32[32,32,128]{2,1,0:T(8,128)S(1)} %broadcast_in_dim.13), channel_id=1, replica_groups=mesh['row'=16,'col_0'=4,'col_1'=4,'col_2'=2] {'col_0','col_1','col_2'}, dimensions={0} | all-to-all | bytes 1048576 | tf_op jit(solution)/shard_map/all_to_all | solution.py:473
  85.3 4.6 %second_product.1 = (f32[16,9,4,128]{3,2,1,0:T(4,128)S(1)}, f32[1024,128]{1,0:T(8,128)S(1)}) custom-call(f32[16,4,128]{2,1,0:T(4,128)S(1)} %all-to-all-done.row_ref, f32[32,4,128]{2,1,0:T(4,128)S(1)} %all_to_all.35.col_ref, f32[1024,128]{1,0:T(8,128)S(1)} %bitcast.4, f32[1024,128]{1,0:T(8,128)S(1)} %get-tuple-element.13.rhs_ref.packed_ref, ...), custom_call_target="tpu_custom_call" | custom-call | flops 2147483648 | bytes 1572864 | tf_op jit(solution)/shard_map/second_product/pallas_call | solution.py:229
  89.9 21.2 %all_to_all.38 = f32[16,9,4,128]{3,2,1,0:T(4,128)S(1)} all-to-all(f32[16,9,4,128]{3,2,1,0:T(4,128)S(1)} %get-tuple-element.15), channel_id=1, replica_groups=mesh['row'=16,'col_0'=4,'col_1'=4,'col_2'=2] {'row'}, dimensions={0} | all-to-all | bytes 589824 | tf_op jit(solution)/shard_map/all_to_all | solution.py:473
  111.1 0.1 reduce_sum.28
  111.1 0.1 broadcast_in_dim.14
  111.2 19.9 %all_to_all.39.unit_ref = f32[32,9,4,128]{3,2,1,0:T(4,128)S(1)} all-to-all(f32[32,9,4,128]{3,2,1,0:T(4,128)S(1)} %broadcast_in_dim.14), channel_id=1, replica_groups=mesh['row'=16,'col_0'=4,'col_1'=4,'col_2'=2] {'col_0','col_1','col_2'}, dimensions={0} | all-to-all | bytes 1179648 | tf_op jit(solution)/shard_map/all_to_all | solution.py:473
  131.1 5.1 %middle.1 = (f32[16,32,128]{2,1,0:T(8,128)S(1)}, f32[1024,128]{1,0:T(8,128)S(1)}, f32[128,128]{1,0:T(8,128)S(1)}) custom-call(f32[32,9,4,128]{3,2,1,0:T(4,128)S(1)} %all_to_all.39.unit_ref, f32[1024,128]{1,0:T(8,128)S(1)} %get-tuple-element.13.rhs_ref.packed_ref, f32[1024,128]{1,0:T(8,128)S(1)} %get-tuple-element.16.image_ref, ...), custom_call_target="tpu_custom_call" | custom-call | tf_op jit(solution)/shard_map/middle/pallas_call | solution.py:401
  136.2 0.0 copy-start.1
  136.2 20.7 %all_to_all.40 = f32[16,32,128]{2,1,0:T(8,128)S(1)} all-to-all(f32[16,32,128]{2,1,0:T(8,128)S(1)} %get-tuple-element.17), channel_id=1, replica_groups=mesh['row'=16,'col_0'=4,'col_1'=4,'col_2'=2] {'row'}, dimensions={0} | all-to-all | bytes 524288 | tf_op jit(solution)/shard_map/all_to_all | solution.py:473
  157.0 5.4 %all-gather = f32[64,128]{1,0:T(8,128)S(1)} all-gather(f32[32,128]{1,0:T(8,128)S(1)} %reduce_sum.29), channel_id=2, replica_groups=mesh['row'=16,'col_0'=4,'col_1'=4,'col_2'=2] {'col_2'}, dimensions={0}, use_global_device_ids=true | all-gather | bytes 49152 | tf_op jit(solution)/shard_map/all_gather | solution.py:493
  162.4 0.0 copy-done.1
  162.4 4.8 %final_outputs.1 = (f32[64,2048]{1,0:T(8,128)}, f32[64,2048]{1,0:T(8,128)}, f32[1,64]{1,0:T(1,128)}) custom-call(f32[2,32,128]{2,1,0:T(8,128)S(1)} %bitcast.5, f32[128,128]{1,0:T(8,128)S(1)} %get-tuple-element.18.coef_ref, f32[64,2048]{1,0:T(8,128)S(1)} %copy-done.1, f32[1024,128]{1,0:T(8,128)S(1)} %get-tuple-element.13.rhs_ref.packed_ref, ...), custom_call_target="tpu_custom_call" | custom-call | tf_op jit(solution)/shard_map/final_outputs/pallas_call | solution.py:461
  (3 shorter events, 0.1 us)
Async XLA Ops:
  19.0 13.9 %copy-start.2 = (f32[2048]{0:T(1024)S(1)}, f32[2048]{0:T(1024)}, u32[]{:S(2)}) copy-start(f32[2048]{0:T(1024)} %param.4) | copy-start | bytes 24580
  19.0 25.3 %all-to-all-start = ((f32[16,4,128]{2,1,0:T(4,128)}), f32[16,4,128]{2,1,0:T(4,128)S(1)}, u32[]{:S(2)}, u32[]{:S(2)}) async-start(f32[16,4,128]{2,1,0:T(4,128)} %broadcast_in_dim.10), calls=%async_computation | async-start | bytes 65536 | tf_op jit(solution)/shard_map/all_to_all | solution.py:473
  32.9 1.0 copy-start
  136.2 26.2 %copy-start.1 = (f32[64,2048]{1,0:T(8,128)S(1)}, f32[64,2048]{1,0:T(8,128)}, u32[]{:S(2)}) copy-start(f32[64,2048]{1,0:T(8,128)} %rhs_ref.3) | copy-start | bytes 1572868

commit v9 on v8

--- a/solution.py
+++ b/solution.py
@@ -168,14 +168,20 @@
     stack_values(rhs_ref[...], stack)
     apply_kernel_matrix(left, right, stack, result)
     for place in range(out_ref.shape[0]):
-        out_ref[place] = result[place * 32 : place * 32 + 32]
+        for quad in range(8):
+            start = place * 32 + quad * 4
+            out_ref[place, quad] = result[start : start + 4]
+
+
+def lines_of(ref):
+    return jnp.concatenate([ref[i, quad] for i in range(ref.shape[0]) for quad in range(8)], axis=0)
 
 
 def second_product_kernel(
     row_ref, col_ref, raw_ref, rhs_ref, noise_ref, out_ref, image_ref, left, right, stack, result, grams
 ):
     rhs = rhs_ref[...]
-    image = raw_ref[...] + noise_ref[...] * rhs
+    image = lines_of(raw_ref) + noise_ref[...] * rhs
     image_ref[...] = image
     fill_left(ordered(row_ref), left)
     fill_right(ordered(col_ref), right)
@@ -216,7 +222,7 @@
         first_product_kernel,
         in_specs=[VMEM] * 3,
         out_specs=VMEM,
-        out_shape=jax.ShapeDtypeStruct((row_pts.shape[0], 32, LANES), F32),
+        out_shape=jax.ShapeDtypeStruct((row_pts.shape[0], 8, 4, LANES), F32),
         scratch_shapes=product_scratch(outs, ins),
         cost_estimate=product_cost(outs, ins),
         compiler_params=PARAMS,
@@ -362,7 +368,7 @@
     gram1 = gram - cross - cross.T + small_dot(coef0.T, small_dot(square, coef0))
     dcoef = small_dot(inverse, gram1)
     rhs, image = rhs_ref[...], image_ref[...]
-    raw = jnp.concatenate([unit_ref[i, quad] for i in range(unit_ref.shape[0]) for quad in range(8)], axis=0)
+    raw = lines_of(unit_ref)
     second = raw + noise_ref[...] * (rhs - THETA * image)
     second_ref[...] = second
     scaled = coef0 * (1.0 / THETA)
@@ -392,7 +398,8 @@
     start = pl.multiple_of(lax.axis_index(COL[-1]) * 16, 16)
     part = jnp.concatenate([lines[pl.ds(32 * m + start, 16)] for m in range(2)], axis=0)
     for place in range(share_ref.shape[0]):
-        share_ref[place] = part
+        for quad in range(8):
+            share_ref[place, quad] = part[4 * quad : 4 * quad + 4]
     coef_ref[0:64] = jnp.concatenate([coef0, dcoef], axis=1)
     coef_ref[64:128] = jnp.concatenate([gram, eye], axis=1)
 
@@ -403,7 +410,7 @@
         in_specs=[VMEM] * 4,
         out_specs=[VMEM] * 3,
         out_shape=[
-            jax.ShapeDtypeStruct((rows, 32, LANES), F32),
+            jax.ShapeDtypeStruct((rows, 8, 4, LANES), F32),
             jax.ShapeDtypeStruct(rhs.shape, F32),
             jax.ShapeDtypeStruct((128, LANES), F32),
         ],
@@ -416,7 +423,11 @@
 def final_kernel(lines_ref, coef_ref, rhs_ref, packed_ref, image_ref, second_ref, sol_ref, res_ref, norm_ref):
     low = lane_of((32, LANES)) < HALF
     upper, lower = (
-        unfolded(jnp.concatenate([lines_ref[half, 16 * m : 16 * m + 16] for half in range(2)], axis=0))
+        unfolded(
+            jnp.concatenate(
+                [lines_ref[half, 4 * m + quad] for half in range(2) for quad in range(4)], axis=0
+            )
+        )
         for m in range(2)
     )
     curv1, gram1, square = matrices_of(upper, lower)
@@ -486,7 +497,7 @@
 
     part = first_product(row_pts, col_pts, rhs)
     own = jnp.sum(exchanged(part, "row"), axis=0)
-    raw = shared(own, COL).reshape(-1, LANES)
+    raw = shared(own, COL)
     part, image = second_product(row_pts, col_pts, raw, rhs, noise)
     own = jnp.sum(exchanged(part, "row"), axis=0)
     share, second, coefs = middle(shared(own, COL), rhs, image, noise, rows)

time: 168 us -> 168 us (level)
  no operation moved by 1% of the time
where the time goes in v9:
time: 168 us; the launch traced here: 167 us
  blocking collectives  121 us (72%)
  Pallas kernels  19.3 us (11%)
  starting transfers between devices  13.9 us (8%)
  waiting for transfers between devices  9.64 us (6%)
  local copies, waits for them, and re-layouts  2.63 us (2%)
    all_to_all x6, blocking collectives, exchanged(): return lax.all_to_all(parts, axis, 0, 0, tiled=True)  116 us
    all_to_all x1, starting transfers between devices, exchanged(): return lax.all_to_all(parts, axis, 0, 0, tiled=True)  13.9 us
    all_to_all x1, waiting for transfers between devices, exchanged(): return lax.all_to_all(parts, axis, 0, 0, tiled=True)  9.64 us
    all_gather x1, blocking collectives, on_device(): lines = lax.all_gather(jnp.sum(exchanged(share, 'row'), axis=0), COL[-1])  5.41 us
    pallas_call x1, Pallas kernels, middle(): pl.pallas_call(middle_kernel, in_specs=[VMEM] * 4, out_specs=[VMEM] * 3,...  5.11 us
    pallas_call x1, Pallas kernels, final_outputs(): pl.pallas_call(final_kernel, in_specs=[VMEM] * 6, out_specs=[VMEM] * 3, o...  4.76 us
    pallas_call x1, Pallas kernels, second_product(): pl.pallas_call(second_product_kernel, in_specs=[VMEM] * 5, out_specs=[VME...  4.6 us
    pallas_call x1, Pallas kernels, first_product(): pl.pallas_call(first_product_kernel, in_specs=[VMEM] * 3, out_specs=VMEM,...  4.02 us
  transfers between devices with their start and end apart: 1, of which 1 were waited for; matrix products, arithmetic and copies ran while one was open for 0% of the time, Pallas kernels for 0%

profile of v9, /device:TPU:1, one launch (start us, length us, event | category | flops | bytes accessed | tf_op | source)
XLA Modules:
  0.0 167.3 jit_solution(4500787425343037588)
XLA Ops:
  0.6 0.8 fusion
  1.4 0.1 pad_maximum_fusion
  1.5 16.9 %all_to_all.35.col_ref = f32[32,4,128]{2,1,0:T(4,128)S(1)} all-to-all(f32[32,4,128]{2,1,0:T(4,128)S(1)} %broadcast_in_dim.11), channel_id=1, replica_groups=mesh['row'=16,'col_0'=4,'col_1'=4,'col_2'=2] {'col_0','col_1','col_2'}, dimensions={0} | all-to-all | bytes 131072 | tf_op jit(solution)/shard_map/all_to_all | solution.py:484
  18.4 0.6 broadcast_in_dim.10
  19.0 0.0 copy-start.2
  19.0 13.9 %all-to-all-start = ((f32[16,4,128]{2,1,0:T(4,128)}), f32[16,4,128]{2,1,0:T(4,128)S(1)}, u32[]{:S(2)}, u32[]{:S(2)}) async-start(f32[16,4,128]{2,1,0:T(4,128)} %broadcast_in_dim.10), calls=%async_computation | async-start | bytes 65536 | tf_op jit(solution)/shard_map/all_to_all | solution.py:484
  32.9 0.0 copy-done.2
  32.9 0.0 copy-start
  32.9 1.0 copy-done
  34.0 0.8 prepare.1
  34.7 9.6 %all-to-all-done.row_ref = f32[16,4,128]{2,1,0:T(4,128)S(1)} async-done(((f32[16,4,128]{2,1,0:T(4,128)}), f32[16,4,128]{2,1,0:T(4,128)S(1)}, u32[]{:S(2)}, u32[]{:S(2)}) %all-to-all-start) | async-done | bytes 32800 | tf_op jit(solution)/shard_map/all_to_all | solution.py:484
  44.4 4.0 %first_product.1 = f32[16,8,4,128]{3,2,1,0:T(4,128)S(1)} custom-call(f32[16,4,128]{2,1,0:T(4,128)S(1)} %all-to-all-done.row_ref, f32[32,4,128]{2,1,0:T(4,128)S(1)} %all_to_all.35.col_ref, f32[1024,128]{1,0:T(8,128)S(1)} %get-tuple-element.13.rhs_ref.packed_ref), custom_call_target="tpu_custom_call" | custom-call | flops 2147483648 | bytes 1572864 | tf_op jit(solution)/shard_map/first_product/pallas_call | solution.py:221
  48.4 15.3 %all_to_all.36 = f32[16,8,4,128]{3,2,1,0:T(4,128)S(1)} all-to-all(f32[16,8,4,128]{3,2,1,0:T(4,128)S(1)} %first_product.1), channel_id=1, replica_groups=mesh['row'=16,'col_0'=4,'col_1'=4,'col_2'=2] {'row'}, dimensions={0} | all-to-all | bytes 524288 | tf_op jit(solution)/shard_map/all_to_all | solution.py:484
  63.7 0.1 reduce_sum.27
  63.8 0.1 broadcast_in_dim.13
  63.9 21.5 %all_to_all.37.raw_ref = f32[32,8,4,128]{3,2,1,0:T(4,128)S(1)} all-to-all(f32[32,8,4,128]{3,2,1,0:T(4,128)S(1)} %broadcast_in_dim.13), channel_id=1, replica_groups=mesh['row'=16,'col_0'=4,'col_1'=4,'col_2'=2] {'col_0','col_1','col_2'}, dimensions={0} | all-to-all | bytes 1048576 | tf_op jit(solution)/shard_map/all_to_all | solution.py:484
  85.4 4.6 %second_product.1 = (f32[16,9,4,128]{3,2,1,0:T(4,128)S(1)}, f32[1024,128]{1,0:T(8,128)S(1)}) custom-call(f32[16,4,128]{2,1,0:T(4,128)S(1)} %all-to-all-done.row_ref, f32[32,4,128]{2,1,0:T(4,128)S(1)} %all_to_all.35.col_ref, f32[32,8,4,128]{3,2,1,0:T(4,128)S(1)} %all_to_all.37.raw_ref, f32[1024,128]{1,0:T(8,128)S(1)} %get-tuple-element.13.rhs_ref.packed_ref, ...), custom_call_target="tpu_custom_call" | custom-call | flops 2147483648 | bytes 1572864 | tf_op jit(solution)/shard_map/second_product/pallas_call | solution.py:235
  90.0 21.2 %all_to_all.38 = f32[16,9,4,128]{3,2,1,0:T(4,128)S(1)} all-to-all(f32[16,9,4,128]{3,2,1,0:T(4,128)S(1)} %get-tuple-element.15), channel_id=1, replica_groups=mesh['row'=16,'col_0'=4,'col_1'=4,'col_2'=2] {'row'}, dimensions={0} | all-to-all | bytes 589824 | tf_op jit(solution)/shard_map/all_to_all | solution.py:484
  111.2 0.1 reduce_sum.28
  111.3 0.1 broadcast_in_dim.14
  111.3 19.9 %all_to_all.39.unit_ref = f32[32,9,4,128]{3,2,1,0:T(4,128)S(1)} all-to-all(f32[32,9,4,128]{3,2,1,0:T(4,128)S(1)} %broadcast_in_dim.14), channel_id=1, replica_groups=mesh['row'=16,'col_0'=4,'col_1'=4,'col_2'=2] {'col_0','col_1','col_2'}, dimensions={0} | all-to-all | bytes 1179648 | tf_op jit(solution)/shard_map/all_to_all | solution.py:484
  131.2 5.1 %middle.1 = (f32[16,8,4,128]{3,2,1,0:T(4,128)S(1)}, f32[1024,128]{1,0:T(8,128)S(1)}, f32[128,128]{1,0:T(8,128)S(1)}) custom-call(f32[32,9,4,128]{3,2,1,0:T(4,128)S(1)} %all_to_all.39.unit_ref, f32[1024,128]{1,0:T(8,128)S(1)} %get-tuple-element.13.rhs_ref.packed_ref, f32[1024,128]{1,0:T(8,128)S(1)} %get-tuple-element.16.image_ref, ...), custom_call_target="tpu_custom_call" | custom-call | tf_op jit(solution)/shard_map/middle/pallas_call | solution.py:408
  136.4 0.0 copy-start.1
  136.4 20.7 %all_to_all.40 = f32[16,8,4,128]{3,2,1,0:T(4,128)S(1)} all-to-all(f32[16,8,4,128]{3,2,1,0:T(4,128)S(1)} %get-tuple-element.17), channel_id=1, replica_groups=mesh['row'=16,'col_0'=4,'col_1'=4,'col_2'=2] {'row'}, dimensions={0} | all-to-all | bytes 524288 | tf_op jit(solution)/shard_map/all_to_all | solution.py:484
  157.1 0.1 reduce_sum.29
  157.1 5.4 %all-gather = f32[16,4,128]{2,1,0:T(4,128)S(1)} all-gather(f32[8,4,128]{2,1,0:T(4,128)S(1)} %reduce_sum.29), channel_id=2, replica_groups=mesh['row'=16,'col_0'=4,'col_1'=4,'col_2'=2] {'col_2'}, dimensions={0}, use_global_device_ids=true | all-gather | bytes 49152 | tf_op jit(solution)/shard_map/all_gather | solution.py:504
  162.6 0.0 copy-done.1
  162.6 4.8 %final_outputs.1 = (f32[64,2048]{1,0:T(8,128)}, f32[64,2048]{1,0:T(8,128)}, f32[1,64]{1,0:T(1,128)}) custom-call(f32[2,8,4,128]{3,2,1,0:T(4,128)S(1)} %bitcast.3, f32[128,128]{1,0:T(8,128)S(1)} %get-tuple-element.18.coef_ref, f32[64,2048]{1,0:T(8,128)S(1)} %copy-done.1, f32[1024,128]{1,0:T(8,128)S(1)} %get-tuple-element.13.rhs_ref.packed_ref, ...), custom_call_target="tpu_custom_call" | custom-call | tf_op jit(solution)/shard_map/final_outputs/pallas_call | solution.py:472
  (1 shorter events, 0.0 us)
Async XLA Ops:
  19.0 13.9 %copy-start.2 = (f32[2048]{0:T(1024)S(1)}, f32[2048]{0:T(1024)}, u32[]{:S(2)}) copy-start(f32[2048]{0:T(1024)} %param.4) | copy-start | bytes 24580
  19.0 25.3 %all-to-all-start = ((f32[16,4,128]{2,1,0:T(4,128)}), f32[16,4,128]{2,1,0:T(4,128)S(1)}, u32[]{:S(2)}, u32[]{:S(2)}) async-start(f32[16,4,128]{2,1,0:T(4,128)} %broadcast_in_dim.10), calls=%async_computation | async-start | bytes 65536 | tf_op jit(solution)/shard_map/all_to_all | solution.py:484
  32.9 1.0 copy-start
  136.4 26.2 %copy-start.1 = (f32[64,2048]{1,0:T(8,128)S(1)}, f32[64,2048]{1,0:T(8,128)}, u32[]{:S(2)}) copy-start(f32[64,2048]{1,0:T(8,128)} %rhs_ref.3) | copy-start | bytes 1572868
